TPU v7x, 16 devices: a whole 2x2x2 slice. The times are simulated.
16 devices in a mesh: tp: 4 (over z, y), dp: 4 (over x, core).
Axes of the slice: x: 2, y: 2, z: 2, core: 2. Of those that a mesh axis runs over, the one named last changes fastest.
Arguments:
- x: bfloat16 [4096, 5120], P(('dp', 'tp'))
- w_gate: bfloat16 [5120, 13824], P('dp', 'tp')
- w_up: bfloat16 [5120, 13824], P('dp', 'tp')
- w_down: bfloat16 [13824, 5120], P('tp', 'dp')
- dy: bfloat16 [4096, 5120], P(('dp', 'tp'))
Outputs:
- output 1: bfloat16 [4096, 5120], P(('dp', 'tp'))
- output 2: bfloat16 [4096, 5120], P(('dp', 'tp'))
- output 3: float32 [5120, 13824], P('dp', 'tp')
- output 4: float32 [5120, 13824], P('dp', 'tp')
- output 5: float32 [13824, 5120], P('tp', 'dp')
All inputs are finite; a program needn't handle non-finite values.
Results may differ from a plain program's by a relative error of at most 0.0012.
Values are sent between devices in bfloat16 or wider.
A program may use at most 1 GiB of HBM per device.

v0:
```python
import jax
import jax.numpy as jnp
from jax import lax
from jax.sharding import PartitionSpec as P


def solution(mesh):
    nx = mesh.shape["dp"]
    ny = mesh.shape["tp"]
    rows = P(("dp", "tp"), None)
    wsp = P("dp", "tp")
    dsp = P("tp", "dp")
    f32 = jnp.float32
    bf = jnp.bfloat16

    def to_columns(v):
        tl = v.shape[0]
        dl = v.shape[1] // nx
        vr = v.reshape(tl, nx, dl).transpose(1, 0, 2)
        return lax.all_to_all(vr, "dp", 0, 0, tiled=True)

    def from_columns(v):
        tl = v.shape[1]
        dl = v.shape[2]
        vr = lax.all_to_all(v, "dp", 0, 0, tiled=True)
        return vr.transpose(1, 0, 2).reshape(tl, nx * dl)

    def all_tokens(va):
        vg = lax.all_gather(va, "tp", axis=0, tiled=False)
        tl = vg.shape[2]
        dl = vg.shape[3]
        return vg.transpose(1, 0, 2, 3).reshape(nx * ny * tl, dl)

    def combine_tp(q, res):
        dl = q.shape[1]
        tl = q.shape[0] // (nx * ny)
        qs = lax.psum_scatter(q.reshape(nx, ny, tl, dl), "tp", scatter_dimension=1, tiled=True)
        out = res.astype(f32) + qs.reshape(nx, tl, dl)
        return from_columns(out.astype(bf))

    def local(x, w_gate, w_up, w_down, dy):
        fl = w_gate.shape[1]
        w = jnp.concatenate([w_gate, w_up], axis=1)
        xa = to_columns(x)
        xt = all_tokens(xa)
        p = lax.psum_scatter(jnp.dot(xt, w, preferred_element_type=f32), "dp", scatter_dimension=0, tiled=True)
        a = p[:, :fl]
        b = p[:, fl:]
        sig = jax.nn.sigmoid(a)
        sa = a * sig
        h = (sa * b).astype(bf)
        hg = lax.all_gather(h, "dp", axis=0, tiled=True)
        y = combine_tp(jnp.dot(hg, w_down, preferred_element_type=f32), xa)
        dya = to_columns(dy)
        dyt = all_tokens(dya)
        g = lax.psum_scatter(jnp.dot(dyt, w_down.T, preferred_element_type=f32), "dp", scatter_dimension=0, tiled=True)
        da = (g * b * sig * (1.0 + a * (1.0 - sig))).astype(bf)
        db = (g * sa).astype(bf)
        dab = lax.all_gather(jnp.concatenate([da, db], axis=1), "dp", axis=0, tiled=True)
        dx = combine_tp(jnp.dot(dab, w.T, preferred_element_type=f32), dya)
        dw = jnp.dot(xt.T, dab, preferred_element_type=f32)
        dw_down = jnp.dot(hg.T, dyt, preferred_element_type=f32)
        return y, dx, dw[:, :fl], dw[:, fl:], dw_down

    return jax.shard_map(local, mesh=mesh, in_specs=(rows, wsp, wsp, dsp, rows), out_specs=(rows, rows, wsp, wsp, dsp), check_vma=False)
```

profile of v0, /device:TPU:0, one launch (start us, length us, event | category | flops | bytes accessed | tf_op | source)
XLA Modules:
  0.0 2329.9 jit_solution(3411449403456889146)
XLA Ops:
  7.2 0.0 all-gather.13.cloned.1.call-start
  7.2 4.4 copy.48
  11.6 35.6 %all_to_all.20 = bf16[4,256,1280]{1,2,0:T(8,128)(2,1)S(1)} all-to-all(bf16[4,256,1280]{1,2,0:T(8,128)(2,1)} %bitcast.56), channel_id=1, replica_groups=mesh['tp'=4,'dp'=4] {'dp'}, dimensions={0} | all-to-all | bytes 5242880 | tf_op jit(solution)/shard_map/all_to_all | solution.py:20
  47.2 0.0 copy-start
  47.2 3.0 copy.49
  50.2 0.0 all-gather.13.cloned.1.call-update
  50.2 0.0 all-gather.11.cloned.1.call-start
  50.3 4.4 copy.44
  54.7 35.5 %all_to_all.21 = bf16[4,256,1280]{1,2,0:T(8,128)(2,1)} all-to-all(bf16[4,256,1280]{1,2,0:T(8,128)(2,1)} %bitcast.57), channel_id=1, replica_groups=mesh['tp'=4,'dp'=4] {'dp'}, dimensions={0} | all-to-all | bytes 5242880 | tf_op jit(solution)/shard_map/all_to_all | solution.py:20
  90.1 4.4 copy.45
  94.5 0.0 all-gather.11.cloned.1.call-update
  94.5 0.0 reduce-scatter.11.cloned.1.call-start
  94.6 57.9 %all-gather.13.cloned.1.call-done = bf16[16,256,1280]{2,1,0:T(8,128)(2,1)} async-done(((bf16[4,256,1280]{2,1,0:T(8,128)(2,1)}), bf16[16,256,1280]{2,1,0:T(8,128)(2,1)}) %all-gather.13.cloned.1.call-update) | async-done | bytes 10485776 | tf_op jit(solution)/shard_map/all_gather | solution.py:29
  152.5 9.0 copy.50
  161.5 0.0 copy-done
  161.5 45.3 %fusion.5 = f32[4096,3456]{0,1:T(8,128)} fusion(bf16[4096,1280]{1,0:T(8,128)(2,1)} %bitcast.49, bf16[3456,1280]{1,0:T(8,128)(2,1)} %param.8), kind=kOutput, calls=%fused_computation.16 | convolution fusion | flops 36238786560 | bytes 75956224 | tf_op jit(solution)/shard_map/dot_general | solution.py:56
  206.8 0.0 reduce-scatter.11.cloned.1.call-update
  206.8 0.2 reduce-scatter.9.cloned.1.call-start
  207.0 7.7 constant_dynamic-update-slice_fusion.1
  214.7 7.7 constant_dynamic-update-slice_fusion
  222.3 33.7 %all-gather.11.cloned.1.call-done = bf16[16,256,1280]{2,1,0:T(8,128)(2,1)} async-done(((bf16[4,256,1280]{2,1,0:T(8,128)(2,1)}), bf16[16,256,1280]{2,1,0:T(8,128)(2,1)}) %all-gather.11.cloned.1.call-update) | async-done | bytes 10485776 | tf_op jit(solution)/shard_map/all_gather | solution.py:29
  256.0 8.8 copy.46
  264.8 84.2 %convolution_bitcast_fusion = f32[4096,6912]{0,1:T(8,128)} fusion(bf16[1280,6912]{1,0:T(8,128)(2,1)} %constant_dynamic-update-slice_fusion, bf16[4096,1280]{1,0:T(8,128)(2,1)} %bitcast.51), kind=kOutput, calls=%fused_computation | convolution fusion | flops 72477573120 | bytes 141426688 | tf_op jit(solution)/shard_map/dot_general | solution.py:46
  349.0 0.0 reduce-scatter.9.cloned.1.call-update
  349.1 0.0 all-gather.7.cloned.1.call-start
  349.1 274.9 %reduce-scatter.11.cloned.1.call-done = f32[1024,3456]{0,1:T(8,128)} async-done(((f32[4096,3456]{0,1:T(8,128)}), f32[1024,3456]{0,1:T(8,128)}) %reduce-scatter.11.cloned.1.call-update) | async-done | bytes 14155792 | tf_op jit(solution)/shard_map/reduce_scatter | solution.py:56
  624.0 719.1 %reduce-scatter.9.cloned.1.call-done = f32[1024,6912]{0,1:T(8,128)} async-done(((f32[4096,6912]{0,1:T(8,128)}), f32[1024,6912]{0,1:T(8,128)}) %reduce-scatter.9.cloned.1.call-update) | async-done | bytes 28311568 | tf_op jit(solution)/shard_map/reduce_scatter | solution.py:46
  1343.1 23.0 multiply_convert_fusion.1
  1366.1 0.0 all-gather.7.cloned.1.call-update
  1366.2 0.0 all-gather.9.cloned.1.call-start
  1366.2 12.2 pad_maximum_fusion
  1378.4 0.0 all-gather.9.cloned.1.call-update
  1378.4 0.4 reduce-scatter.13.cloned.1.call-start
  1378.9 158.6 %all-gather.7.cloned.1.call-done = bf16[4096,3456]{0,1:T(8,128)(2,1)} async-done(((bf16[1024,3456]{0,1:T(8,128)(2,1)}), bf16[4096,3456]{0,1:T(8,128)(2,1)}) %all-gather.7.cloned.1.call-update) | async-done | bytes 28311568 | tf_op jit(solution)/shard_map/all_gather | solution.py:52
  1537.5 47.8 %fusion.4 = f32[4096,1280]{1,0:T(8,128)} fusion(bf16[4096,3456]{0,1:T(8,128)(2,1)} %all-gather.7.cloned.1.call-done, bf16[3456,1280]{1,0:T(8,128)(2,1)} %param.8), kind=kOutput, calls=%fused_computation.15 | convolution fusion | flops 36238786560 | bytes 58130432 | tf_op jit(solution)/shard_map/dot_general | solution.py:53
  1585.3 21.9 copy.47
  1607.2 0.0 reduce-scatter.13.cloned.1.call-update
  1607.2 0.2 reduce-scatter.15.cloned.1.call-start
  1607.4 264.6 %all-gather.9.cloned.1.call-done = bf16[4096,6912]{0,1:T(8,128)(2,1)} async-done(((bf16[1024,6912]{0,1:T(8,128)(2,1)}), bf16[4096,6912]{0,1:T(8,128)(2,1)}) %all-gather.9.cloned.1.call-update) | async-done | bytes 56623120 | tf_op jit(solution)/shard_map/all_gather | solution.py:59
  1872.0 82.9 %fusion.6 = f32[4096,1280]{1,0:T(8,128)} fusion(bf16[4096,6912]{0,1:T(8,128)(2,1)} %all-gather.9.cloned.1.call-done, bf16[1280,6912]{1,0:T(8,128)(2,1)} %constant_dynamic-update-slice_fusion), kind=kOutput, calls=%fused_computation.17 | convolution fusion | flops 72477573120 | bytes 95289344 | tf_op jit(solution)/shard_map/dot_general | solution.py:60
  1954.9 21.9 copy.52
  1976.8 0.0 reduce-scatter.15.cloned.1.call-update
  1976.8 0.0 copy-start.2
  1976.9 45.4 %fusion.7 = f32[3456,1280]{1,0:T(8,128)} fusion(bf16[4096,3456]{0,1:T(8,128)(2,1)} %all-gather.7.cloned.1.call-done, bf16[4096,1280]{1,0:T(8,128)(2,1)} %bitcast.50), kind=kOutput, calls=%fused_computation.18 | convolution fusion | flops 36238786560 | bytes 56492032 | tf_op jit(solution)/shard_map/dot_general | solution.py:62
  2022.2 36.6 %reduce-scatter.13.cloned.1.call-done = f32[4,1,256,1280]{2,3,0,1:T(8,128)} async-done(((f32[4,4,256,1280]{2,3,0,1:T(8,128)}), f32[4,1,256,1280]{2,3,0,1:T(8,128)}) %reduce-scatter.13.cloned.1.call-update) | async-done | bytes 5242896
  2058.8 0.0 copy-done.2
  2058.8 4.6 fusion.2
  2063.4 4.8 all-to-all-start.1
  2068.2 0.0 copy-start.1
  2068.2 83.8 %convolution_bitcast_fusion.1 = f32[1280,6912]{0,1:T(8,128)} fusion(bf16[4096,6912]{0,1:T(8,128)(2,1)} %all-gather.9.cloned.1.call-done, bf16[4096,1280]{1,0:T(8,128)(2,1)} %bitcast.52), kind=kOutput, calls=%fused_computation.1 | convolution fusion | flops 72477573120 | bytes 102498304 | tf_op jit(solution)/shard_map/dot_general | solution.py:61
  2152.1 93.7 %reduce-scatter.15.cloned.1.call-done = f32[4,1,256,1280]{2,3,0,1:T(8,128)} async-done(((f32[4,4,256,1280]{2,3,0,1:T(8,128)}), f32[4,1,256,1280]{2,3,0,1:T(8,128)}) %reduce-scatter.15.cloned.1.call-update) | async-done | bytes 5242896
  2245.7 0.0 copy-done.1
  2245.7 4.6 fusion.1
  2250.3 0.0 all-to-all-done.1
  2250.3 3.7 all-to-all-start.3
  2254.0 25.0 %fusion.3 = (f32[1280,3456]{0,1:T(8,128)}, f32[1280,3456]{0,1:T(8,128)}) fusion(f32[1280,6912]{0,1:T(8,128)} %convolution_bitcast_fusion.1), kind=kLoop, calls=%fused_computation.14 | loop fusion | bytes 70778880 | tf_op jit(solution)/shard_map/slice | solution.py:63
  2279.0 18.3 copy.55
  2297.3 18.3 copy.56
  2315.7 4.4 copy.53
  2320.0 0.0 all-to-all-done.3
  2320.0 2.8 copy.54
Async XLA Ops:
  7.2 145.3 %all-gather.13.cloned.1.call-start = ((), (), s32[]{:S(2)}) async-start(), calls=%async_computation.13 | async-start | bytes 13107200 | tf_op jit(solution)/shard_map/all_gather | solution.py:29
  47.2 114.3 %copy-start = (bf16[4,256,1280]{1,2,0:T(8,128)(2,1)}, bf16[4,256,1280]{1,2,0:T(8,128)(2,1)S(1)}, u32[]{:S(2)}) copy-start(bf16[4,256,1280]{1,2,0:T(8,128)(2,1)S(1)} %all_to_all.20) | copy-start | bytes 7864324
  50.2 205.8 %all-gather.11.cloned.1.call-start = ((), (), s32[]{:S(2)}) async-start(), calls=%async_computation.12 | async-start | bytes 13107200 | tf_op jit(solution)/shard_map/all_gather | solution.py:29
  94.5 529.5 %reduce-scatter.11.cloned.1.call-start = ((), (), s32[]{:S(2)}) async-start(), calls=%async_computation.10 | async-start | bytes 70778880 | tf_op jit(solution)/shard_map/reduce_scatter | solution.py:56
  206.8 1136.3 %reduce-scatter.9.cloned.1.call-start = ((), (), s32[]{:S(2)}) async-start(), calls=%async_computation.8 | async-start | bytes 141557760 | tf_op jit(solution)/shard_map/reduce_scatter | solution.py:46
  349.1 1188.4 %all-gather.7.cloned.1.call-start = ((), (), s32[]{:S(2)}) async-start(), calls=%async_computation.9 | async-start | bytes 35389440 | tf_op jit(solution)/shard_map/all_gather | solution.py:52
  1366.2 505.8 %all-gather.9.cloned.1.call-start = ((), (), s32[]{:S(2)}) async-start(), calls=%async_computation.11 | async-start | bytes 70778880 | tf_op jit(solution)/shard_map/all_gather | solution.py:59
  1378.4 680.4 %reduce-scatter.13.cloned.1.call-start = ((), (), s32[]{:S(2)}) async-start(), calls=%async_computation.14 | async-start | bytes 26214400
  1607.2 638.5 %reduce-scatter.15.cloned.1.call-start = ((), (), s32[]{:S(2)}) async-start(), calls=%async_computation.15 | async-start | bytes 26214400
  1976.8 82.0 %copy-start.2 = (bf16[4,256,1280]{1,2,0:T(8,128)(2,1)S(1)}, bf16[4,256,1280]{1,2,0:T(8,128)(2,1)}, u32[]{:S(2)}) copy-start(bf16[4,256,1280]{1,2,0:T(8,128)(2,1)} %all_to_all.21) | copy-start | bytes 7864324
  2063.4 186.9 %all-to-all-start.1 = ((bf16[4,256,1280]{1,2,0:T(8,128)(2,1)}), bf16[4,256,1280]{1,2,0:T(8,128)(2,1)}, u32[]{:S(2)}, u32[]{:S(2)}) async-start(bf16[4,256,1280]{1,2,0:T(8,128)(2,1)} %fusion.2), calls=%async_computation.2 | async-start | bytes 5242880 | tf_op jit(solution)/shard_map/all_to_all | solution.py:25
  2068.2 177.5 %copy-start.1 = (bf16[4,256,1280]{1,2,0:T(8,128)(2,1)S(1)}, bf16[4,256,1280]{1,2,0:T(8,128)(2,1)}, u32[]{:S(2)}) copy-start(bf16[4,256,1280]{1,2,0:T(8,128)(2,1)} %copy-done) | copy-start | bytes 7864324
  2250.3 69.7 %all-to-all-start.3 = ((bf16[4,256,1280]{1,2,0:T(8,128)(2,1)}), bf16[4,256,1280]{1,2,0:T(8,128)(2,1)S(1)}, u32[]{:S(2)}, u32[]{:S(2)}) async-start(bf16[4,256,1280]{1,2,0:T(8,128)(2,1)} %fusion.1), calls=%async_computation.5 | async-start | bytes 5242880 | tf_op jit(solution)/shard_map/all_to_all | solution.py:25
Sparse Core Ops, SparseCore 0:
  50.4 102.0 all-gather.12
  154.9 101.1 all-gather.10
  258.6 365.3 reduce-scatter.10
  626.4 716.6 reduce-scatter.8
  1366.3 171.1 all-gather.6
  1539.4 332.4 all-gather.8
  1875.0 183.7 reduce-scatter.12
  2061.9 183.7 reduce-scatter.14
where the time goes:
time: 2340 us; the launch traced here: 2330 us
  waiting for transfers between devices  1640 us (70%)
  matrix products  389 us (17%)
  local copies, waits for them, and re-layouts  162 us (7%)
  blocking collectives  71.1 us (3%)
  other arithmetic  44.4 us (2%)
    reduce_scatter x1, waiting for transfers between devices, local(): lax.psum_scatter(jnp.dot(xt, w, preferred_element_type=f32), 'dp', scatte...  719 us
    reduce_scatter x1, waiting for transfers between devices, local(): lax.psum_scatter(jnp.dot(dyt, w_down.T, preferred_element_type=f32), 'dp'...  275 us
    all_gather x1, waiting for transfers between devices, local(): lax.all_gather(jnp.concatenate([da, db], axis=1), 'dp', axis=0, tiled=True)  265 us
    all_gather x1, waiting for transfers between devices, local(): hg = lax.all_gather(h, 'dp', axis=0, tiled=True)  159 us
    unnamed x10, waiting for transfers between devices  130 us
    all_gather x2, waiting for transfers between devices, all_tokens(): vg = lax.all_gather(va, 'tp', axis=0, tiled=False)  91.6 us
    dot_general x1, matrix products, local(): jnp.dot(xt, w, preferred_element_type=f32)  84.2 us
    dot_general x1, matrix products, local(): dw = jnp.dot(xt.T, dab, preferred_element_type=f32)  83.8 us
  transfers between devices with their start and end apart: 10, of which 8 were waited for; matrix products, arithmetic and copies ran while one was open for 24% of the time, Pallas kernels for 0%

commit v1 on v0

v1 whole, which is shorter than its diff:
```python
import functools

import jax
import jax.numpy as jnp
from jax import lax
from jax.experimental import pallas as pl
from jax.experimental.pallas import tpu as pltpu
from jax.sharding import PartitionSpec as P


f32 = jnp.float32
bf = jnp.bfloat16
TILE = 256
CHUNK = 1280


def dot(u, v):
    return jnp.dot(u, v, preferred_element_type=f32)


def params():
    return pltpu.CompilerParams(vmem_limit_bytes=60 * 2**20)


def cost(flops, nbytes):
    return pl.CostEstimate(flops=int(flops), bytes_accessed=int(nbytes), transcendentals=0)


def quarters(buf, m, ws):
    dq = ws[0].shape[0]
    acc = dot(buf[m, :, :dq], ws[0][...])
    for k in range(1, 4):
        acc += dot(buf[m, :, k * dq : (k + 1) * dq], ws[k][...])
    return acc


def load(pieces, buf, sems):
    m, n = pl.program_id(0), pl.program_id(1)
    r, w = pieces[0].shape
    copies = []
    for k, p in enumerate(pieces):
        g, row, col = k // 8, k % 8 // 2, k % 2
        dst = buf.at[g, pl.ds(row * r, r), pl.ds(col * w, w)]
        copies.append(pltpu.make_async_copy(p, dst, sems.at[k]))

    @pl.when((m == 0) & (n == 0))
    def _():
        for c in copies:
            c.start()
        for c in copies[:8]:
            c.wait()

    @pl.when((m == 1) & (n == 0))
    def _():
        for c in copies[8:]:
            c.wait()

    return m


def fwd_body(*refs):
    pieces, ws, (a_ref, b_ref, ht_ref), (buf, sems) = refs[:16], refs[16:24], refs[24:27], refs[27:]
    m = load(pieces, buf, sems)
    a = quarters(buf, m, ws[:4])
    b = quarters(buf, m, ws[4:])
    a_ref[...] = a
    b_ref[...] = b
    ht_ref[...] = (a * jax.nn.sigmoid(a) * b).T.astype(bf)


def bwd_body(*refs):
    pieces, ws, (a_ref, b_ref, da_ref, db_ref, dat_ref, dbt_ref), (buf, sems) = refs[:16], refs[16:20], refs[20:26], refs[26:]
    m = load(pieces, buf, sems)
    g = quarters(buf, m, ws)
    a = a_ref[...]
    s = jax.nn.sigmoid(a)
    da = g * b_ref[...] * s * (1.0 + a * (1.0 - s))
    db = g * (a * s)
    da_ref[...] = da.astype(bf)
    db_ref[...] = db.astype(bf)

    @pl.when(m == 0)
    def _():
        dat_ref[...] = da.T.astype(bf)
        dbt_ref[...] = db.T.astype(bf)


def weight_specs(own, c):
    dq = own.shape[0]
    first = c * (CHUNK // TILE)
    whole = pl.BlockSpec((dq, TILE), lambda m, n: (0, first + n))
    piece = pl.BlockSpec((dq, TILE), lambda m, n: (0, n))
    return [whole, whole, piece, piece]


def grouped(body, pieces, ws, wspecs, extra, fc, outs, flops):
    tm = 4 * pieces[0].shape[0]
    d = 2 * pieces[0].shape[1]
    nt = pl.cdiv(fc, TILE)
    specs = {
        "mn": (pl.BlockSpec((tm, TILE), lambda m, n: (m, n)), (2 * tm, fc)),
        "nm": (pl.BlockSpec((TILE, tm), lambda m, n: (n, m)), (fc, 2 * tm)),
        "n0": (pl.BlockSpec((TILE, tm), lambda m, n: (n + m * (nt - 1 - n), 0)), (fc, tm)),
    }
    return pl.pallas_call(
        body,
        grid=(2, nt),
        in_specs=[pl.BlockSpec(memory_space=pl.ANY)] * 16 + wspecs + [specs["mn"][0]] * len(extra),
        out_specs=[specs[k][0] for k, _ in outs],
        out_shape=[jax.ShapeDtypeStruct(specs[k][1], t) for k, t in outs],
        scratch_shapes=[pltpu.VMEM((2, tm, d), bf), pltpu.SemaphoreType.DMA((16,))],
        compiler_params=params(),
        cost_estimate=cost(flops * tm * d * fc, 8e7),
    )(*pieces, *ws, *extra)


def forward(xp, wg, wu, c):
    fc = wg[2].shape[1]
    outs = [("mn", f32), ("mn", f32), ("nm", bf)]
    return grouped(fwd_body, xp, wg + wu, weight_specs(wg[0], c) * 2, [], fc, outs, 8)


def backward(dyp, wd, a, b, c):
    fc = wd[2].shape[1]
    outs = [("mn", bf), ("mn", bf), ("n0", bf), ("n0", bf)]
    return grouped(bwd_body, dyp, wd, weight_specs(wd[0], c), [a, b], fc, outs, 4)


def part_body(axis, terms, nw, nt, groups, has_acc, *refs):
    ws, ts, rest = refs[:nw], refs[nw : nw + nt], refs[nw + nt :]
    no = 2 * groups
    accs = rest[:no] if has_acc else [None] * no
    outs = rest[-no:]
    cols = ts[0].shape[1] // groups
    w = cols // 4
    stay, leave = ((0, 2), (1, 3)) if axis == "y" else ((0, 1), (2, 3))
    for g in range(groups):
        t = None
        for wi, start, ti in terms:
            fc = ts[ti].shape[0]
            u = dot(ws[wi][:, start : start + fc], ts[ti][:, g * cols : (g + 1) * cols])
            t = u if t is None else t + u
        for o, sel in ((2 * g, stay), (2 * g + 1, leave)):
            for n, k in enumerate(sel):
                v = t[:, k * w : (k + 1) * w]
                if has_acc:
                    v = v + accs[o][:, n * w : (n + 1) * w]
                outs[o][:, n * w : (n + 1) * w] = v


def partial_sums(ws, ts, terms, axis, groups, accs=None):
    dq = ws[0].shape[0]
    half = ts[0].shape[1] // groups // 2
    o = pl.BlockSpec((TILE, half), lambda m: (m, 0))
    no = 2 * groups
    n_in = len(ws) + len(ts)
    flops = sum(2 * dq * ts[t[2]].shape[0] * ts[0].shape[1] for t in terms)
    return pl.pallas_call(
        functools.partial(part_body, axis, terms, len(ws), len(ts), groups, accs is not None),
        grid=(dq // TILE,),
        in_specs=[pl.BlockSpec((TILE, w.shape[1]), lambda m: (m, 0)) for w in ws]
        + [pl.BlockSpec(t.shape, lambda m: (0, 0)) for t in ts]
        + ([o] * no if accs else []),
        out_specs=[o] * no,
        out_shape=[jax.ShapeDtypeStruct((dq, half), f32)] * no,
        input_output_aliases={n_in + k: k for k in range(no)} if accs else {},
        compiler_params=params(),
        cost_estimate=cost(flops, 3e7),
        name="partial_sums",
    )(*ws, *ts, *(accs or []))


def dw_body(counts, rows, *refs):
    n = pl.program_id(0)
    fixed, out = refs[:2], refs[-1]
    for c, (lo, hi) in enumerate(counts):
        u, v = refs[2 + 2 * c : 4 + 2 * c]

        @pl.when((n >= lo) & (n < hi))
        def _(u=u, v=v):
            if rows:
                out[...] = dot(u[...], fixed[0][...]) + dot(v[...], fixed[1][...])
            else:
                out[...] = dot(fixed[0][...], u[...]) + dot(fixed[1][...], v[...])


def weight_grad(fixed, streams, rows, full, first, prev=None):
    m = fixed[0].shape[1] if rows else fixed[0].shape[0]
    k = fixed[0].shape[0] if rows else fixed[0].shape[1]
    counts, n = [], 0
    specs = []
    for u, _ in streams:
        nt = pl.cdiv(u.shape[0] if rows else u.shape[1], TILE)

        def index(j, lo=n, nt=nt):
            t = jnp.clip(j - lo, 0, nt - 1)
            return (t, 0) if rows else (0, t)

        specs += [pl.BlockSpec((TILE, k) if rows else (k, TILE), index)] * 2
        counts.append((n, n + nt))
        n += nt
    fspec = pl.BlockSpec(fixed[0].shape, lambda j: (0, 0))
    base = first * (CHUNK // TILE)
    ospec = pl.BlockSpec((TILE, m), lambda j: (base + j, 0)) if rows else pl.BlockSpec((m, TILE), lambda j: (0, base + j))
    n_in = 2 + 2 * len(streams)
    return pl.pallas_call(
        functools.partial(dw_body, counts, rows),
        grid=(n,),
        in_specs=[fspec, fspec] + specs + ([] if prev is None else [pl.BlockSpec(memory_space=pl.ANY)]),
        out_specs=ospec,
        out_shape=jax.ShapeDtypeStruct((full, m) if rows else (m, full), f32),
        input_output_aliases={} if prev is None else {n_in: 0},
        compiler_params=params(),
        cost_estimate=cost(4 * m * k * n * TILE, 5e7),
        name="weight_grad",
    )(*fixed, *[v for p in streams for v in p], *([] if prev is None else [prev]))


def solution(mesh):
    rows = P(("dp", "tp"), None)
    wsp = P("dp", "tp")
    dsp = P("tp", "dp")

    def hop(axis, bit):
        pairs = [(k, k ^ bit) for k in range(mesh.shape[axis])]
        return lambda v: lax.ppermute(v, axis, pairs)

    px, pc = hop("dp", 2), hop("dp", 1)
    py, pz = hop("tp", 1), hop("tp", 2)

    def after(v, *deps):
        return lax.optimization_barrier((v, deps))[0]

    def cross(v):
        return px(v)

    def body(x, w_gate, w_up, w_down, dy):
        i = lax.axis_index("dp")
        dq, fl = w_gate.shape
        starts = list(range(0, fl, CHUNK))
        nc = len(starts)

        def reorder(v):
            return jnp.concatenate([lax.dynamic_slice_in_dim(v, (i ^ k) * dq, dq, 1) for k in range(4)], axis=1)

        def gather(v, dep=None):
            va, vb = v[:, : 2 * dq], v[:, 2 * dq :]
            a_y, b_z, b_y, a_z = py(va), pz(vb), py(vb), pz(va)
            a1, b1 = (a_y, b_z) if dep is None else after((a_y, b_z), *dep)
            a_yz, b_yz = pz(a1), py(b1)
            return [va, vb, a_y, b_y, a_z, b_z, a_yz, b_yz]

        def swap(v):
            return jnp.concatenate([v[:, 2 * dq :], v[:, : 2 * dq]], axis=1)

        piece = lambda w, c: w[:, starts[c] : starts[c] + CHUNK]
        wgx, wux, wdx = [None] * nc, [None] * nc, [None] * nc
        xo, dyo = reorder(x), reorder(dy)
        x_other = swap(cross(xo))
        for c in range(nc):
            if c == nc - 1:
                dy_other = cross(dyo)
            wgx[c] = cross(piece(w_gate, c))
            wux[c] = cross(piece(w_up, c))
        wd_t = w_down.T
        for c in range(nc):
            wdx[c] = cross(piece(wd_t, c))
        wg_s, wu_s, wd_s = pc(w_gate), pc(w_up), pc(wd_t)

        xp = gather(xo) + gather(x_other)
        dyp = gather(after(dyo, *xp[8:]))
        blk = xo.shape[0]
        col = lambda ps, k: jnp.concatenate([p[:, k * dq : (k + 1) * dq] for p in ps[0::2]], axis=0)
        xq, xq_s = col(xp, 0).T, pc(col(xp, 1).T)

        a, b, ht, ht_s, across = [], [], [], [], []
        done = xp
        for c in range(nc):
            gx, ux = after((wgx[c], wux[c]), *done)
            gs, us = pc(gx), pc(ux)
            across.append([(gx, ux), (gs, us)])
            ac, bc, htc = forward(xp, [w_gate, wg_s, gx, gs], [w_up, wu_s, ux, us], c)
            a.append(ac)
            b.append(bc)
            ht.append(htc)
            ht_s.append(pc(htc))
            done = [htc]
            if c == nc - 2:
                terms = [(0, starts[k], k) for k in range(nc - 1)]
                dy_other = swap(after(dy_other, htc))
                yacc = [partial_sums([w], ht, terms, "yz"[q], 2) for q, w in enumerate((wd_t, wd_s))]
                dyp += gather(dy_other, [yacc[0][0], yacc[1][0]])
                dyq, dyq_s = col(dyp, 0), pc(col(dyp, 1))
                done = [yacc[0][0], yacc[1][0]]
        yacc = [partial_sums([w], ht[-1:], [(0, starts[-1], 0)], "yz"[q], 2, yacc[q]) for q, w in enumerate((wd_t, wd_s))]
        done = [yacc[0][0], yacc[1][0]]

        def first_hop(axis, send):
            return (py if axis == "y" else pz)(send)

        def second_hop(axis, keep, r):
            s = keep[:, blk:] + r[:, blk:]
            return keep[:, :blk] + r[:, :blk], (pz if axis == "y" else py)(s)

        order = [(1, 0), (1, 1), (0, 0), (0, 1)]
        y_first = {(g, q): first_hop("yz"[q], yacc[q][2 * g + 1]) for g, q in order}

        da, db, dat, dbt = [], [], [], []
        for c in range(nc):
            dx_ = after(wdx[c], *done)
            grads = backward(dyp, [wd_t, wd_s, dx_, pc(dx_)], a[c], b[c], c)
            for lst, v in zip((da, db, dat, dbt), grads):
                lst.append(v)
            done = [da[c]]
            if c == nc - 2:
                y_first = dict(zip(order, after([y_first[k] for k in order], *done)))
                y_second = {(g, q): second_hop("yz"[q], yacc[q][2 * g], y_first[g, q]) for g, q in order}
        da_s, db_s = [pc(v) for v in da], [pc(v) for v in db]

        dx_keep, dx_first = [], []
        for q in range(4):
            if q < 2:
                ws = ((w_gate, w_up), (wg_s, wu_s))[q]
                terms = [(0, starts[c], c) for c in range(nc)] + [(1, starts[c], nc + c) for c in range(nc)]
            else:
                ws = [across[c][q - 2][0] for c in range(nc)] + [across[c][q - 2][1] for c in range(nc)]
                terms = [(k, 0, k) for k in range(2 * nc)]
            ts = dat + dbt
            if q:
                ts = after(ts, dx_keep[-1])
            keep, send = partial_sums(list(ws), ts, terms, "yzyz"[q], 1)
            dx_keep.append(keep)
            dx_first.append(first_hop("yzyz"[q], send))

        y_second = dict(zip(order, after([y_second[k] for k in order], *dx_keep)))
        part = lambda g: jnp.concatenate([(s + r).T for s, r in (y_second[g, 0], y_second[g, 1])], axis=1)
        y_out = (x_other[:, : 2 * dq].astype(f32) + part(1)).astype(bf)
        y_in = px(y_out)
        y_own = (xo[:, : 2 * dq].astype(f32) + part(0)).astype(bf)
        y = reorder(jnp.concatenate([y_own, y_in], axis=1))

        xq, dyq = after((xq, dyq), *dx_keep)
        dwd = weight_grad((dyq, dyq_s), list(zip(ht, ht_s)), True, fl, 0)
        dwg = weight_grad((xq, xq_s), list(zip(da, da_s)), False, fl, 0)
        dwu = weight_grad((xq, xq_s), list(zip(db, db_s)), False, fl, 0)

        sums = []
        for q in range(4):
            sums.append(second_hop("yzyz"[q], dx_keep[q], dx_first[q]))
        dx = jnp.concatenate([(s + r).T for s, r in sums], axis=1)
        dx = reorder((dyo.astype(f32) + dx).astype(bf))
        return y, dx, dwg, dwu, dwd

    return jax.shard_map(body, mesh=mesh, in_specs=(rows, wsp, wsp, dsp, rows), out_specs=(rows, rows, wsp, wsp, dsp), check_vma=False)
```

time: 2340 us -> 1500 us (0.64)
  waiting for transfers between devices: 1640 us -> 599 us
  Pallas kernels: 0 us -> 632 us
  matrix products: 389 us -> 0 us
  blocking collectives: 71.1 us -> 0 us
  starting transfers between devices: 9.51 us -> 63.6 us
    reduce_scatter x2 -> x0, waiting for transfers between devices: 994 us -> none  [the longest x1 719 us: local(): lax.psum_scatter(jnp.dot(xt, w, preferred_element_type=f32), 'dp', scatte...]
    pallas_call x0 -> x17, Pallas kernels: none -> 632 us  [the longest x6 308 us: grouped(): pl.pallas_call(body, grid=(2, nt), in_specs=[pl.BlockSpec(memory_space=pl...]
    ppermute x0 -> x75, waiting for transfers between devices: none -> 599 us  [hop(): return lambda v: lax.ppermute(v, axis, pairs)]
    all_gather x4 -> x0, waiting for transfers between devices: 515 us -> none  [the longest x1 265 us: local(): lax.all_gather(jnp.concatenate([da, db], axis=1), 'dp', axis=0, tiled=True)]
    dot_general x6 -> x0, matrix products: 389 us -> none  [the longest x1 84.2 us: local(): jnp.dot(xt, w, preferred_element_type=f32)]
    unnamed x10 -> x0, waiting for transfers between devices: 130 us -> none
    all_to_all x2 -> x0, blocking collectives: 71.1 us -> none  [to_columns(): return lax.all_to_all(vr, 'dp', 0, 0, tiled=True)]
    ppermute x0 -> x75, starting transfers between devices: none -> 63.6 us  [hop(): return lambda v: lax.ppermute(v, axis, pairs)]
  transfers between devices with their start and end apart: 10 -> 75, of which waited for: 8 -> 25; matrix products, arithmetic and copies ran while one was open for 24% -> 12% of each run, Pallas kernels for 0% -> 42%
where the time goes in v1:
time: 1500 us; the launch traced here: 1490 us
  Pallas kernels  632 us (42%)
  waiting for transfers between devices  599 us (40%)
  local copies, waits for them, and re-layouts  139 us (9%)
  starting transfers between devices  63.6 us (4%)
  other arithmetic  56.8 us (4%)
    ppermute x75, waiting for transfers between devices, hop(): return lambda v: lax.ppermute(v, axis, pairs)  599 us
    pallas_call x6, Pallas kernels, grouped(): pl.pallas_call(body, grid=(2, nt), in_specs=[pl.BlockSpec(memory_space=pl...  308 us
    pallas_call x8, Pallas kernels, partial_sums(): pl.pallas_call(functools.partial(part_body, axis, terms, len(ws), len(ts)...  178 us
    pallas_call x3, Pallas kernels, weight_grad(): pl.pallas_call(functools.partial(dw_body, counts, rows), grid=(n,), in_sp...  147 us
    ppermute x75, starting transfers between devices, hop(): return lambda v: lax.ppermute(v, axis, pairs)  63.6 us
    unnamed x147, local copies, waits for them, and re-layouts  49.1 us
  transfers between devices with their start and end apart: 75, of which 25 were waited for; matrix products, arithmetic and copies ran while one was open for 12% of the time, Pallas kernels for 42%

profile of v1, /device:TPU:0, one launch (start us, length us, event | category | flops | bytes accessed | tf_op | source)
XLA Modules:
  0.0 1492.3 jit_solution(3942170827897364821)
XLA Ops:
  0.7 4.2 constant_dynamic-slice_fusion.7
  6.6 3.2 collective-permute-start
  14.9 5.1 fusion.17
  20.0 19.7 %collective-permute-done = bf16[256,2560]{0,1:T(8,128)(2,1)} collective-permute-done((bf16[256,2560]{0,1:T(8,128)(2,1)}, bf16[256,2560]{0,1:T(8,128)(2,1)}, u32[]{:S(2)}, u32[]{:S(2)}) %collective-permute-start) | collective-permute-done | bytes 1310752 | tf_op jit(solution)/shard_map/ppermute | solution.py:226
  41.8 5.1 fusion.16
  46.9 19.9 %collective-permute-done.1 = bf16[256,2560]{0,1:T(8,128)(2,1)S(1)} collective-permute-done((bf16[256,2560]{0,1:T(8,128)(2,1)S(1)}, bf16[256,2560]{0,1:T(8,128)(2,1)S(1)}, u32[]{:S(2)}, u32[]{:S(2)}) %collective-permute-start.1) | collective-permute-done | bytes 1310752 | tf_op jit(solution)/shard_map/ppermute | solution.py:226
  69.7 26.7 %collective-permute-done.4 = bf16[256,2560]{0,1:T(8,128)(2,1)S(1)} collective-permute-done((bf16[256,2560]{0,1:T(8,128)(2,1)}, bf16[256,2560]{0,1:T(8,128)(2,1)S(1)}, u32[]{:S(2)}, u32[]{:S(2)}) %collective-permute-start.4) | collective-permute-done | bytes 1310752 | tf_op jit(solution)/shard_map/ppermute | solution.py:226
  97.0 30.6 %collective-permute-done.5 = bf16[256,2560]{0,1:T(8,128)(2,1)S(1)} collective-permute-done((bf16[256,2560]{0,1:T(8,128)(2,1)S(1)}, bf16[256,2560]{0,1:T(8,128)(2,1)S(1)}, u32[]{:S(2)}, u32[]{:S(2)}) %collective-permute-start.5) | collective-permute-done | bytes 1310752 | tf_op jit(solution)/shard_map/ppermute | solution.py:226
  129.1 14.0 collective-permute-done.16.refs_18_.refs_0_
  145.0 66.3 %collective-permute-done.17.refs_22_.refs_3_ = bf16[1280,1280]{1,0:T(8,128)(2,1)} collective-permute-done((bf16[1280,1280]{1,0:T(8,128)(2,1)S(1)}, bf16[1280,1280]{1,0:T(8,128)(2,1)}, u32[]{:S(2)}, u32[]{:S(2)}) %collective-permute-start.17) | collective-permute-done | bytes 3276832 | tf_op jit(solution)/shard_map/ppermute | solution.py:226
  215.1 27.9 %collective-permute-done.10 = bf16[256,2560]{0,1:T(8,128)(2,1)S(1)} collective-permute-done((bf16[256,2560]{0,1:T(8,128)(2,1)S(1)}, bf16[256,2560]{0,1:T(8,128)(2,1)S(1)}, u32[]{:S(2)}, u32[]{:S(2)}) %collective-permute-start.10) | collective-permute-done | bytes 1310752 | tf_op jit(solution)/shard_map/ppermute | solution.py:226
  244.7 26.4 %collective-permute-done.9 = bf16[256,2560]{0,1:T(8,128)(2,1)S(1)} collective-permute-done((bf16[256,2560]{0,1:T(8,128)(2,1)S(1)}, bf16[256,2560]{0,1:T(8,128)(2,1)S(1)}, u32[]{:S(2)}, u32[]{:S(2)}) %collective-permute-start.9) | collective-permute-done | bytes 1310752 | tf_op jit(solution)/shard_map/ppermute | solution.py:226
  272.1 24.3 %collective-permute-done.11 = bf16[256,2560]{0,1:T(8,128)(2,1)} collective-permute-done((bf16[256,2560]{0,1:T(8,128)(2,1)S(1)}, bf16[256,2560]{0,1:T(8,128)(2,1)}, u32[]{:S(2)}, u32[]{:S(2)}) %collective-permute-start.11) | collective-permute-done | bytes 1310752 | tf_op jit(solution)/shard_map/ppermute | solution.py:226
  321.5 2.6 copy.66.refs_11_
  332.0 66.5 %shard_map.92 = (f32[2048,1280]{1,0:T(8,128)}, f32[2048,1280]{1,0:T(8,128)}, bf16[1280,2048]{1,0:T(8,128)(2,1)}) custom-call(bf16[256,2560]{1,0:T(8,128)(2,1)} %copy.55.refs_0_, bf16[256,2560]{1,0:T(8,128)(2,1)} %copy.56.refs_1_, bf16[256,2560]{1,0:T(8,128)(2,1)} %copy.57.refs_2_, bf16[256,2560]{1,0:T(8,128)(2,1)} %copy.58.refs_3_, ...), custom_call_target="tpu_custom_call" | custom-call | flops 53687091200 | bytes 80000000 | tf_op jit(solution)/shard_map/pallas_call | solution.py:105
  398.5 41.9 %collective-permute-done.22.refs_22_.refs_4_ = bf16[1280,1280]{1,0:T(8,128)(2,1)} collective-permute-done((bf16[1280,1280]{1,0:T(8,128)(2,1)}, bf16[1280,1280]{1,0:T(8,128)(2,1)}, u32[]{:S(2)}, u32[]{:S(2)}) %collective-permute-start.22) | collective-permute-done | bytes 3276832 | tf_op jit(solution)/shard_map/ppermute | solution.py:226
  440.9 12.6 copy.20
  457.0 3.3 slice.246
  461.0 3.3 slice.247
  466.8 3.1 fusion.15
  472.0 66.6 %shard_map.93 = (f32[2048,1280]{1,0:T(8,128)}, f32[2048,1280]{1,0:T(8,128)}, bf16[1280,2048]{1,0:T(8,128)(2,1)}) custom-call(bf16[256,2560]{1,0:T(8,128)(2,1)} %copy.55.refs_0_, bf16[256,2560]{1,0:T(8,128)(2,1)} %copy.56.refs_1_, bf16[256,2560]{1,0:T(8,128)(2,1)} %copy.57.refs_2_, bf16[256,2560]{1,0:T(8,128)(2,1)} %copy.58.refs_3_, ...), custom_call_target="tpu_custom_call" | custom-call | flops 53687091200 | bytes 80000000 | tf_op jit(solution)/shard_map/pallas_call | solution.py:105
  538.6 19.9 %partial_sums.8 = (f32[1280,512]{1,0:T(8,128)}, f32[1280,512]{1,0:T(8,128)}, f32[1280,512]{1,0:T(8,128)}, f32[1280,512]{1,0:T(8,128)}) custom-call(bf16[1280,3456]{1,0:T(8,128)(2,1)} %bitcast.20, bf16[1280,2048]{1,0:T(8,128)(2,1)} %get-tuple-element.97.refs_1_.refs_2_, bf16[1280,2048]{1,0:T(8,128)(2,1)} %get-tuple-element.100.refs_2_.refs_4_), custom_call_target="tpu_custom_call" | custom-call | flops 13421772800 | bytes 30000000 | tf_op jit(solution)/shard_map/partial_sums/pallas_call | solution.py:158
  558.5 19.9 %partial_sums.9 = (f32[1280,512]{1,0:T(8,128)}, f32[1280,512]{1,0:T(8,128)}, f32[1280,512]{1,0:T(8,128)}, f32[1280,512]{1,0:T(8,128)}) custom-call(bf16[1280,3456]{1,0:T(8,128)(2,1)} %collective-permute-done.25.refs_0_.refs_17_, bf16[1280,2048]{1,0:T(8,128)(2,1)} %get-tuple-element.97.refs_1_.refs_2_, bf16[1280,2048]{1,0:T(8,128)(2,1)} %get-tuple-element.100.refs_2_.refs_4_), custom_call_target="tpu_custom_call" | custom-call | flops 13421772800 | bytes 30000000 | tf_op jit(solution)/shard_map/partial_sums/pallas_call | solution.py:158
  578.4 35.4 %collective-permute-done.15.refs_22_.refs_5_ = bf16[1280,896]{1,0:T(8,128)(2,1)} collective-permute-done((bf16[1280,896]{1,0:T(8,128)(2,1)}, bf16[1280,896]{1,0:T(8,128)(2,1)}, u32[]{:S(2)}, u32[]{:S(2)}) %collective-permute-start.15) | collective-permute-done | bytes 2293792 | tf_op jit(solution)/shard_map/ppermute | solution.py:226
  620.1 2.6 slice_dynamic-update-slice_fusion.12
  624.4 23.4 %collective-permute-done.39.refs_10_ = bf16[256,2560]{1,0:T(8,128)(2,1)S(1)} collective-permute-done((bf16[256,2560]{1,0:T(8,128)(2,1)S(1)}, bf16[256,2560]{1,0:T(8,128)(2,1)S(1)}, u32[]{:S(2)}, u32[]{:S(2)}) %collective-permute-start.39) | collective-permute-done | bytes 1310752 | tf_op jit(solution)/shard_map/ppermute | solution.py:226
  651.9 55.4 %shard_map.94 = (f32[2048,896]{1,0:T(8,128)}, f32[2048,896]{1,0:T(8,128)}, bf16[896,2048]{1,0:T(8,128)(2,1)}) custom-call(bf16[256,2560]{1,0:T(8,128)(2,1)} %copy.55.refs_0_, bf16[256,2560]{1,0:T(8,128)(2,1)} %copy.56.refs_1_, bf16[256,2560]{1,0:T(8,128)(2,1)} %copy.57.refs_2_, bf16[256,2560]{1,0:T(8,128)(2,1)} %copy.58.refs_3_, ...), custom_call_target="tpu_custom_call" | custom-call | flops 37580963840 | bytes 80000000 | tf_op jit(solution)/shard_map/pallas_call | solution.py:105
  707.2 14.7 partial_sums.10
  721.9 15.0 %partial_sums.11 = (f32[1280,512]{1,0:T(8,128)}, f32[1280,512]{1,0:T(8,128)}, f32[1280,512]{1,0:T(8,128)}, f32[1280,512]{1,0:T(8,128)}) custom-call(bf16[1280,3456]{1,0:T(8,128)(2,1)} %collective-permute-done.25.refs_0_.refs_17_, ...), custom_call_target="tpu_custom_call", output_to_operand_aliasing={{0}: (2, {}), {1}: (3, {}), {2}: (4, {}), {3}: (5, {})} | custom-call | flops 4697620480 | bytes 30000000 | tf_op jit(solution)/shard_map/partial_sums/pallas_call | solution.py:158
  737.0 2.7 slice_dynamic-update-slice_fusion.11
  747.7 23.9 %collective-permute-done.34.refs_4_ = bf16[256,2560]{1,0:T(8,128)(2,1)S(1)} collective-permute-done((bf16[256,2560]{1,0:T(8,128)(2,1)}, bf16[256,2560]{1,0:T(8,128)(2,1)S(1)}, u32[]{:S(2)}, u32[]{:S(2)}) %collective-permute-start.34) | collective-permute-done | bytes 1310752 | tf_op jit(solution)/shard_map/ppermute | solution.py:226
  772.7 27.0 %collective-permute-done.36.refs_6_ = bf16[256,2560]{1,0:T(8,128)(2,1)S(1)} collective-permute-done((bf16[256,2560]{1,0:T(8,128)(2,1)}, bf16[256,2560]{1,0:T(8,128)(2,1)S(1)}, u32[]{:S(2)}, u32[]{:S(2)}) %collective-permute-start.36) | collective-permute-done | bytes 1310752 | tf_op jit(solution)/shard_map/ppermute | solution.py:226
  805.7 2.6 slice_dynamic-update-slice_fusion.6
  808.3 19.4 %collective-permute-done.41.refs_12_ = bf16[256,2560]{1,0:T(8,128)(2,1)S(1)} collective-permute-done((bf16[256,2560]{1,0:T(8,128)(2,1)S(1)}, bf16[256,2560]{1,0:T(8,128)(2,1)S(1)}, u32[]{:S(2)}, u32[]{:S(2)}) %collective-permute-start.41) | collective-permute-done | bytes 1310752 | tf_op jit(solution)/shard_map/ppermute | solution.py:226
  827.7 27.6 %collective-permute-done.43.refs_14_ = bf16[256,2560]{1,0:T(8,128)(2,1)S(1)} collective-permute-done((bf16[256,2560]{1,0:T(8,128)(2,1)S(1)}, bf16[256,2560]{1,0:T(8,128)(2,1)S(1)}, u32[]{:S(2)}, u32[]{:S(2)}) %collective-permute-start.43) | collective-permute-done | bytes 1310752 | tf_op jit(solution)/shard_map/ppermute | solution.py:226
  858.6 41.6 %shard_map.95 = (bf16[2048,1280]{1,0:T(8,128)(2,1)}, bf16[2048,1280]{1,0:T(8,128)(2,1)}, bf16[1280,1024]{1,0:T(8,128)(2,1)}, bf16[1280,1024]{1,0:T(8,128)(2,1)}) custom-call(bf16[256,2560]{1,0:T(8,128)(2,1)} %get-tuple-element.221.refs_0_, bf16[256,2560]{1,0:T(8,128)(2,1)} %get-tuple-element.220.refs_1_, bf16[256,2560]{1,0:T(8,128)(2,1)} %collective-permute-done.32.refs_2_, ...), custom_call_target="tpu_custom_call" | custom-call | flops 26843545600 | bytes 80000000 | tf_op jit(solution)/shard_map/pallas_call | solution.py:105
  900.3 2.6 slice_dynamic-update-slice_fusion.5
  917.0 42.4 %shard_map.96 = (bf16[2048,1280]{1,0:T(8,128)(2,1)}, bf16[2048,1280]{1,0:T(8,128)(2,1)}, bf16[1280,1024]{1,0:T(8,128)(2,1)}, bf16[1280,1024]{1,0:T(8,128)(2,1)}) custom-call(bf16[256,2560]{1,0:T(8,128)(2,1)} %get-tuple-element.221.refs_0_, bf16[256,2560]{1,0:T(8,128)(2,1)} %get-tuple-element.220.refs_1_, bf16[256,2560]{1,0:T(8,128)(2,1)} %collective-permute-done.32.refs_2_, ...), custom_call_target="tpu_custom_call" | custom-call | flops 26843545600 | bytes 80000000 | tf_op jit(solution)/shard_map/pallas_call | solution.py:105
  959.4 10.8 collective-permute-done.28
  971.1 54.6 %collective-permute-done.30 = f32[1280,512]{1,0:T(8,128)} collective-permute-done((f32[1280,512]{1,0:T(8,128)}, f32[1280,512]{1,0:T(8,128)}, u32[]{:S(2)}, u32[]{:S(2)}) %collective-permute-start.30) | collective-permute-done | bytes 2621472 | tf_op jit(solution)/shard_map/ppermute | solution.py:226
  1026.5 3.3 slice_add_fusion.14
  1030.9 3.6 slice_add_fusion.10
  1034.4 3.3 slice_add_fusion.8
  1037.7 3.6 slice_add_fusion.12
  1042.3 35.1 %shard_map.97 = (bf16[2048,896]{1,0:T(8,128)(2,1)}, bf16[2048,896]{1,0:T(8,128)(2,1)}, bf16[896,1024]{1,0:T(8,128)(2,1)}, bf16[896,1024]{1,0:T(8,128)(2,1)}) custom-call(bf16[256,2560]{1,0:T(8,128)(2,1)} %get-tuple-element.221.refs_0_, bf16[256,2560]{1,0:T(8,128)(2,1)} %get-tuple-element.220.refs_1_, bf16[256,2560]{1,0:T(8,128)(2,1)} %collective-permute-done.32.refs_2_, ...), custom_call_target="tpu_custom_call" | custom-call | flops 18790481920 | bytes 80000000 | tf_op jit(solution)/shard_map/pallas_call | solution.py:105
  1077.4 27.0 %partial_sums.12 = (f32[1280,512]{1,0:T(8,128)}, f32[1280,512]{1,0:T(8,128)}) custom-call(bf16[1280,3456]{1,0:T(8,128)(2,1)} %refs_0_.1, bf16[1280,3456]{1,0:T(8,128)(2,1)} %refs_1_.1, bf16[1280,1024]{1,0:T(8,128)(2,1)} %get-tuple-element.160.refs_2_.refs_6_, bf16[1280,1024]{1,0:T(8,128)(2,1)} %get-tuple-element.161.refs_3_.refs_7_, ...), custom_call_target="tpu_custom_call" | custom-call | flops 18119393280 | bytes 30000000 | tf_op jit(solution)/shard_map/partial_sums/pallas_call | solution.py:158
  1104.4 26.8 %partial_sums.13 = (f32[1280,512]{1,0:T(8,128)}, f32[1280,512]{1,0:T(8,128)}) custom-call(bf16[1280,3456]{1,0:T(8,128)(2,1)} %collective-permute-done.13.refs_17_.refs_0_, bf16[1280,3456]{1,0:T(8,128)(2,1)} %collective-permute-done.19.refs_21_.refs_1_, bf16[1280,1024]{1,0:T(8,128)(2,1)} %get-tuple-element.160.refs_2_.refs_6_, ...), custom_call_target="tpu_custom_call" | custom-call | flops 18119393280 | bytes 30000000 | tf_op jit(solution)/shard_map/partial_sums/pallas_call | solution.py:158
  1132.2 27.6 %partial_sums.14 = (f32[1280,512]{1,0:T(8,128)}, f32[1280,512]{1,0:T(8,128)}) custom-call(bf16[1280,1280]{1,0:T(8,128)(2,1)} %collective-permute-done.16.refs_18_.refs_0_, bf16[1280,1280]{1,0:T(8,128)(2,1)} %collective-permute-done.21.refs_18_.refs_1_, bf16[1280,896]{1,0:T(8,128)(2,1)} %collective-permute-done.14.refs_18_.refs_2_, ...), custom_call_target="tpu_custom_call" | custom-call | flops 18119393280 | bytes 30000000 | tf_op jit(solution)/shard_map/partial_sums/pallas_call | solution.py:158
  1159.8 2.9 collective-permute-done.51
  1163.7 27.2 %partial_sums.15 = (f32[1280,512]{1,0:T(8,128)}, f32[1280,512]{1,0:T(8,128)}) custom-call(bf16[1280,1280]{1,0:T(8,128)(2,1)} %collective-permute-done.18.refs_19_.refs_0_, bf16[1280,1280]{1,0:T(8,128)(2,1)} %collective-permute-done.23.refs_19_.refs_1_, bf16[1280,896]{1,0:T(8,128)(2,1)} %collective-permute-done.26.refs_19_.refs_2_, ...), custom_call_target="tpu_custom_call" | custom-call | flops 18119393280 | bytes 30000000 | tf_op jit(solution)/shard_map/partial_sums/pallas_call | solution.py:158
  1193.3 3.2 copy.81
  1204.9 48.4 %weight_grad.5 = f32[3456,1280]{1,0:T(8,128)} custom-call(bf16[2048,1280]{1,0:T(8,128)(2,1)} %get-tuple-element.184.refs_0_, bf16[2048,1280]{1,0:T(8,128)(2,1)} %collective-permute-done.71.refs_1_, bf16[1280,2048]{1,0:T(8,128)(2,1)} %get-tuple-element.97.refs_1_.refs_2_, bf16[1280,2048]{1,0:T(8,128)(2,1)} %collective-permute-done.72.refs_3_, ...), custom_call_target="tpu_custom_call" | custom-call | flops 37580963840 | bytes 50000000 | tf_op jit(solution)/shard_map/weight_grad/pallas_call | solution.py:206
  1253.3 3.5 copy.78
  1256.8 3.3 copy.75
  1264.7 3.2 copy.80
  1267.9 3.4 copy.77
  1275.5 3.2 copy.72
  1282.6 6.2 fusion.12
  1290.4 4.4 copy.83
  1294.8 3.1 slice_add_fusion
  1297.8 22.3 %collective-permute-done.60 = f32[1280,512]{0,1:T(8,128)} collective-permute-done((f32[1280,512]{0,1:T(8,128)}, f32[1280,512]{0,1:T(8,128)}, u32[]{:S(2)}, u32[]{:S(2)}) %collective-permute-start.60) | collective-permute-done | bytes 2621472 | tf_op jit(solution)/shard_map/ppermute | solution.py:226
  1325.7 49.5 %collective-permute-done.56 = f32[1280,512]{0,1:T(8,128)} collective-permute-done((f32[1280,512]{0,1:T(8,128)}, f32[1280,512]{0,1:T(8,128)}, u32[]{:S(2)}, u32[]{:S(2)}) %collective-permute-start.56) | collective-permute-done | bytes 2621472 | tf_op jit(solution)/shard_map/ppermute | solution.py:226
  1379.8 49.2 %weight_grad.3 = f32[1280,3456]{1,0:T(8,128)} custom-call(bf16[1280,2048]{1,0:T(8,128)(2,1)} %bitcast.28, bf16[1280,2048]{1,0:T(8,128)(2,1)} %collective-permute-done.64.refs_1_, bf16[2048,1280]{1,0:T(8,128)(2,1)} %get-tuple-element.126.refs_2_, bf16[2048,1280]{1,0:T(8,128)(2,1)} %collective-permute-done.65.refs_3_, ...), custom_call_target="tpu_custom_call" | custom-call | flops 37580963840 | bytes 50000000 | tf_op jit(solution)/shard_map/weight_grad/pallas_call | solution.py:206
  1431.0 49.0 %weight_grad.4 = f32[1280,3456]{1,0:T(8,128)} custom-call(bf16[1280,2048]{1,0:T(8,128)(2,1)} %bitcast.29, bf16[1280,2048]{1,0:T(8,128)(2,1)} %collective-permute-done.64.refs_1_, bf16[2048,1280]{1,0:T(8,128)(2,1)} %get-tuple-element.181.refs_2_, bf16[2048,1280]{1,0:T(8,128)(2,1)} %collective-permute-done.68.refs_3_, ...), custom_call_target="tpu_custom_call" | custom-call | flops 37580963840 | bytes 50000000 | tf_op jit(solution)/shard_map/weight_grad/pallas_call | solution.py:206
  (313 shorter events, 164.2 us)
Async XLA Ops:
  6.6 33.2 %collective-permute-start = (bf16[256,2560]{0,1:T(8,128)(2,1)}, bf16[256,2560]{0,1:T(8,128)(2,1)}, u32[]{:S(2)}, u32[]{:S(2)}) collective-permute-start(bf16[256,2560]{0,1:T(8,128)(2,1)} %pad_maximum_fusion.4), channel_id=1, source_target_pairs={{0,4},{4,0},{8,12},{12,8},{1,5},{5,1},{9,13},{13,9},{2,6},{6,2},{1... | collective-permute-start | bytes 3932168 | tf_op jit(solution)/shard_map/ppermute | solution.py:226
  9.8 58.8 %collective-permute-start.2 = (bf16[256,2560]{0,1:T(8,128)(2,1)}, bf16[256,2560]{0,1:T(8,128)(2,1)}, u32[]{:S(2)}, u32[]{:S(2)}) collective-permute-start(bf16[256,2560]{0,1:T(8,128)(2,1)} %pad_maximum_fusion.4), channel_id=1, source_target_pairs={{0,8},{4,12},{8,0},{12,4},{1,9},{5,13},{9,1},{13,5},{2,10},{6,14},... | collective-permute-start | bytes 3932168 | tf_op jit(solution)/shard_map/ppermute | solution.py:226
  11.9 54.9 %collective-permute-start.1 = (bf16[256,2560]{0,1:T(8,128)(2,1)S(1)}, bf16[256,2560]{0,1:T(8,128)(2,1)S(1)}, u32[]{:S(2)}, u32[]{:S(2)}) collective-permute-start(bf16[256,2560]{0,1:T(8,128)(2,1)S(1)} %pad_maximum_fusion.5), channel_id=1, source_target_pairs={{0,4},{4,0},{8,12},{12,8},{1,5},{5,1},{9,13},{13,9},{2,6},{6,2},{1... | collective-permute-start | bytes 3932168 | tf_op jit(solution)/shard_map/ppermute | solution.py:226
  12.5 57.2 %collective-permute-start.3 = (bf16[256,2560]{0,1:T(8,128)(2,1)S(1)}, bf16[256,2560]{0,1:T(8,128)(2,1)S(1)}, u32[]{:S(2)}, u32[]{:S(2)}) collective-permute-start(bf16[256,2560]{0,1:T(8,128)(2,1)S(1)} %pad_maximum_fusion.5), channel_id=1, source_target_pairs={{0,8},{4,12},{8,0},{12,4},{1,9},{5,13},{9,1},{13,5},{2,10},{6,14},... | collective-permute-start | bytes 3932168 | tf_op jit(solution)/shard_map/ppermute | solution.py:226
  13.0 83.4 %collective-permute-start.6 = (bf16[256,5120]{0,1:T(8,128)(2,1)S(1)}, bf16[256,5120]{0,1:T(8,128)(2,1)S(1)}, u32[]{:S(2)}, u32[]{:S(2)}) collective-permute-start(bf16[256,5120]{0,1:T(8,128)(2,1)S(1)} %pad_maximum_fusion), channel_id=1, source_target_pairs={{0,2},{1,3},{2,0},{3,1},{4,6},{5,7},{6,4},{7,5},{8,10},{9,11},{10,... | collective-permute-start | bytes 7864328 | tf_op jit(solution)/shard_map/ppermute | solution.py:226
  39.7 56.7 %collective-permute-start.4 = (bf16[256,2560]{0,1:T(8,128)(2,1)}, bf16[256,2560]{0,1:T(8,128)(2,1)S(1)}, u32[]{:S(2)}, u32[]{:S(2)}) collective-permute-start(bf16[256,2560]{0,1:T(8,128)(2,1)} %collective-permute-done), channel_id=1, source_target_pairs={{0,8},{4,12},{8,0},{12,4},{1,9},{5,13},{9,1},{13,5},{2,10},{6,14},... | collective-permute-start | bytes 3932168 | tf_op jit(solution)/shard_map/ppermute | solution.py:226
  66.9 76.2 %collective-permute-start.16 = (bf16[1280,1280]{1,0:T(8,128)(2,1)S(1)}, bf16[1280,1280]{1,0:T(8,128)(2,1)}, u32[]{:S(2)}, u32[]{:S(2)}) collective-permute-start(bf16[1280,1280]{1,0:T(8,128)(2,1)S(1)} %get-tuple-element.195), channel_id=1, source_target_pairs={{0,2},{1,3},{2,0},{3,1},{4,6},{5,7},{6,4},{7,5},{8,10},{9,11},{10,... | collective-permute-start | bytes 9830408 | tf_op jit(solution)/shard_map/ppermute | solution.py:226
  68.6 142.8 %collective-permute-start.17 = (bf16[1280,1280]{1,0:T(8,128)(2,1)S(1)}, bf16[1280,1280]{1,0:T(8,128)(2,1)}, u32[]{:S(2)}, u32[]{:S(2)}) collective-permute-start(bf16[1280,1280]{1,0:T(8,128)(2,1)S(1)} %get-tuple-element.193), channel_id=1, source_target_pairs={{0,2},{1,3},{2,0},{3,1},{4,6},{5,7},{6,4},{7,5},{8,10},{9,11},{10,... | collective-permute-start | bytes 9830408 | tf_op jit(solution)/shard_map/ppermute | solution.py:226
  69.7 262.3 %collective-permute-start.13 = (bf16[1280,3456]{1,0:T(8,128)(2,1)}, bf16[1280,3456]{1,0:T(8,128)(2,1)}, u32[]{:S(2)}, u32[]{:S(2)}) collective-permute-start(bf16[1280,3456]{1,0:T(8,128)(2,1)} %refs_0_.1), channel_id=1, source_target_pairs={{0,1},{1,0},{2,3},{3,2},{4,5},{5,4},{6,7},{7,6},{8,9},{9,8},{10,11... | collective-permute-start | bytes 26542088 | tf_op jit(solution)/shard_map/ppermute | solution.py:226
  96.4 235.6 %collective-permute-start.19 = (bf16[1280,3456]{1,0:T(8,128)(2,1)}, bf16[1280,3456]{1,0:T(8,128)(2,1)}, u32[]{:S(2)}, u32[]{:S(2)}) collective-permute-start(bf16[1280,3456]{1,0:T(8,128)(2,1)} %refs_1_.1), channel_id=1, source_target_pairs={{0,1},{1,0},{2,3},{3,2},{4,5},{5,4},{6,7},{7,6},{8,9},{9,8},{10,11... | collective-permute-start | bytes 26542088 | tf_op jit(solution)/shard_map/ppermute | solution.py:226
  128.7 84.3 %collective-permute-start.7 = (bf16[256,2560]{0,1:T(8,128)(2,1)S(1)}, bf16[256,2560]{0,1:T(8,128)(2,1)S(1)}, u32[]{:S(2)}, u32[]{:S(2)}) collective-permute-start(bf16[256,2560]{0,1:T(8,128)(2,1)S(1)} %get-tuple-element.227), channel_id=1, source_target_pairs={{0,4},{4,0},{8,12},{12,8},{1,5},{5,1},{9,13},{13,9},{2,6},{6,2},{1... | collective-permute-start | bytes 3932168 | tf_op jit(solution)/shard_map/ppermute | solution.py:226
  143.1 70.3 %collective-permute-start.8 = (bf16[256,2560]{0,1:T(8,128)(2,1)S(1)}, bf16[256,2560]{0,1:T(8,128)(2,1)S(1)}, u32[]{:S(2)}, u32[]{:S(2)}) collective-permute-start(bf16[256,2560]{0,1:T(8,128)(2,1)S(1)} %get-tuple-element.226), channel_id=1, source_target_pairs={{0,4},{4,0},{8,12},{12,8},{1,5},{5,1},{9,13},{13,9},{2,6},{6,2},{1... | collective-permute-start | bytes 3932168 | tf_op jit(solution)/shard_map/ppermute | solution.py:226
  213.1 58.0 %collective-permute-start.9 = (bf16[256,2560]{0,1:T(8,128)(2,1)S(1)}, bf16[256,2560]{0,1:T(8,128)(2,1)S(1)}, u32[]{:S(2)}, u32[]{:S(2)}) collective-permute-start(bf16[256,2560]{0,1:T(8,128)(2,1)S(1)} %get-tuple-element.227), channel_id=1, source_target_pairs={{0,8},{4,12},{8,0},{12,4},{1,9},{5,13},{9,1},{13,5},{2,10},{6,14},... | collective-permute-start | bytes 3932168 | tf_op jit(solution)/shard_map/ppermute | solution.py:226
  213.4 83.1 %collective-permute-start.11 = (bf16[256,2560]{0,1:T(8,128)(2,1)S(1)}, bf16[256,2560]{0,1:T(8,128)(2,1)}, u32[]{:S(2)}, u32[]{:S(2)}) collective-permute-start(bf16[256,2560]{0,1:T(8,128)(2,1)S(1)} %collective-permute-done.7), channel_id=1, source_target_pairs={{0,8},{4,12},{8,0},{12,4},{1,9},{5,13},{9,1},{13,5},{2,10},{6,14},... | collective-permute-start | bytes 3932168 | tf_op jit(solution)/shard_map/ppermute | solution.py:226
  243.0 53.5 %collective-permute-start.12 = (bf16[256,2560]{0,1:T(8,128)(2,1)S(1)}, bf16[256,2560]{0,1:T(8,128)(2,1)S(1)}, u32[]{:S(2)}, u32[]{:S(2)}) collective-permute-start(bf16[256,2560]{0,1:T(8,128)(2,1)S(1)} %collective-permute-done.10), channel_id=1, source_target_pairs={{0,4},{4,0},{8,12},{12,8},{1,5},{5,1},{9,13},{13,9},{2,6},{6,2},{1... | collective-permute-start | bytes 3932168 | tf_op jit(solution)/shard_map/ppermute | solution.py:226
  296.4 34.9 %collective-permute-start.18 = (bf16[1280,1280]{1,0:T(8,128)(2,1)}, bf16[1280,1280]{1,0:T(8,128)(2,1)}, u32[]{:S(2)}, u32[]{:S(2)}) collective-permute-start(bf16[1280,1280]{1,0:T(8,128)(2,1)} %collective-permute-done.16.refs_18_.refs_0_), channel_id=1, source_target_pairs={{0,1},{1,0},{2,3},{3,2},{4,5},{5,4},{6,7},{7,6},{8,9},{9,8},{10,11... | collective-permute-start | bytes 9830408 | tf_op jit(solution)/shard_map/ppermute | solution.py:226
  296.5 35.5 %collective-permute-start.20 = (bf16[1280,1280]{1,0:T(8,128)(2,1)}, bf16[1280,1280]{1,0:T(8,128)(2,1)}, u32[]{:S(2)}, u32[]{:S(2)}) collective-permute-start(bf16[1280,1280]{1,0:T(8,128)(2,1)} %collective-permute-done.17.refs_22_.refs_3_), channel_id=1, source_target_pairs={{0,1},{1,0},{2,3},{3,2},{4,5},{5,4},{6,7},{7,6},{8,9},{9,8},{10,11... | collective-permute-start | bytes 9830408 | tf_op jit(solution)/shard_map/ppermute | solution.py:226
  297.5 101.0 %collective-permute-start.21 = (bf16[1280,1280]{1,0:T(8,128)(2,1)}, bf16[1280,1280]{1,0:T(8,128)(2,1)}, u32[]{:S(2)}, u32[]{:S(2)}) collective-permute-start(bf16[1280,1280]{1,0:T(8,128)(2,1)} %get-tuple-element.194), channel_id=1, source_target_pairs={{0,2},{1,3},{2,0},{3,1},{4,6},{5,7},{6,4},{7,5},{8,10},{9,11},{10,... | collective-permute-start | bytes 9830408 | tf_op jit(solution)/shard_map/ppermute | solution.py:226
  331.3 109.1 %collective-permute-start.22 = (bf16[1280,1280]{1,0:T(8,128)(2,1)}, bf16[1280,1280]{1,0:T(8,128)(2,1)}, u32[]{:S(2)}, u32[]{:S(2)}) collective-permute-start(bf16[1280,1280]{1,0:T(8,128)(2,1)} %get-tuple-element.192), channel_id=1, source_target_pairs={{0,2},{1,3},{2,0},{3,1},{4,6},{5,7},{6,4},{7,5},{8,10},{9,11},{10,... | collective-permute-start | bytes 9830408 | tf_op jit(solution)/shard_map/ppermute | solution.py:226
  453.6 105.0 %collective-permute-start.25 = (bf16[1280,3456]{1,0:T(8,128)(2,1)}, bf16[1280,3456]{1,0:T(8,128)(2,1)}, u32[]{:S(2)}, u32[]{:S(2)}) collective-permute-start(bf16[1280,3456]{1,0:T(8,128)(2,1)} %bitcast.19), channel_id=1, source_target_pairs={{0,1},{1,0},{2,3},{3,2},{4,5},{5,4},{6,7},{7,6},{8,9},{9,8},{10,11... | collective-permute-start | bytes 26542088 | tf_op jit(solution)/shard_map/ppermute | solution.py:226
  455.6 159.6 %collective-permute-start.38 = (bf16[256,5120]{1,0:T(8,128)(2,1)S(1)}, bf16[256,5120]{1,0:T(8,128)(2,1)}, u32[]{:S(2)}, u32[]{:S(2)}) collective-permute-start(bf16[256,5120]{1,0:T(8,128)(2,1)S(1)} %pad_maximum_fusion.1), channel_id=1, source_target_pairs={{0,2},{1,3},{2,0},{3,1},{4,6},{5,7},{6,4},{7,5},{8,10},{9,11},{10,... | collective-permute-start | bytes 7864328 | tf_op jit(solution)/shard_map/ppermute | solution.py:226
  460.3 118.1 %collective-permute-start.14 = (bf16[1280,896]{1,0:T(8,128)(2,1)}, bf16[1280,896]{1,0:T(8,128)(2,1)}, u32[]{:S(2)}, u32[]{:S(2)}) collective-permute-start(bf16[1280,896]{1,0:T(8,128)(2,1)} %slice.246), channel_id=1, source_target_pairs={{0,2},{1,3},{2,0},{3,1},{4,6},{5,7},{6,4},{7,5},{8,10},{9,11},{10,... | collective-permute-start | bytes 6881288 | tf_op jit(solution)/shard_map/ppermute | solution.py:226
  470.0 143.8 %collective-permute-start.15 = (bf16[1280,896]{1,0:T(8,128)(2,1)}, bf16[1280,896]{1,0:T(8,128)(2,1)}, u32[]{:S(2)}, u32[]{:S(2)}) collective-permute-start(bf16[1280,896]{1,0:T(8,128)(2,1)} %slice.247), channel_id=1, source_target_pairs={{0,2},{1,3},{2,0},{3,1},{4,6},{5,7},{6,4},{7,5},{8,10},{9,11},{10,... | collective-permute-start | bytes 6881288 | tf_op jit(solution)/shard_map/ppermute | solution.py:226
  471.3 265.7 %collective-permute-start.46 = (bf16[1280,1280]{1,0:T(8,128)(2,1)}, bf16[1280,1280]{1,0:T(8,128)(2,1)}, u32[]{:S(2)}, u32[]{:S(2)}) collective-permute-start(bf16[1280,1280]{1,0:T(8,128)(2,1)} %get-tuple-element.190), channel_id=1, source_target_pairs={{0,2},{1,3},{2,0},{3,1},{4,6},{5,7},{6,4},{7,5},{8,10},{9,11},{10,... | collective-permute-start | bytes 9830408 | tf_op jit(solution)/shard_map/ppermute | solution.py:226
  613.7 37.1 %collective-permute-start.26 = (bf16[1280,896]{1,0:T(8,128)(2,1)}, bf16[1280,896]{1,0:T(8,128)(2,1)}, u32[]{:S(2)}, u32[]{:S(2)}) collective-permute-start(bf16[1280,896]{1,0:T(8,128)(2,1)} %collective-permute-done.14.refs_18_.refs_2_), channel_id=1, source_target_pairs={{0,1},{1,0},{2,3},{3,2},{4,5},{5,4},{6,7},{7,6},{8,9},{9,8},{10,11... | collective-permute-start | bytes 6881288 | tf_op jit(solution)/shard_map/ppermute | solution.py:226
  613.7 38.1 %collective-permute-start.27 = (bf16[1280,896]{1,0:T(8,128)(2,1)}, bf16[1280,896]{1,0:T(8,128)(2,1)}, u32[]{:S(2)}, u32[]{:S(2)}) collective-permute-start(bf16[1280,896]{1,0:T(8,128)(2,1)} %collective-permute-done.15.refs_22_.refs_5_), channel_id=1, source_target_pairs={{0,1},{1,0},{2,3},{3,2},{4,5},{5,4},{6,7},{7,6},{8,9},{9,8},{10,11... | collective-permute-start | bytes 6881288 | tf_op jit(solution)/shard_map/ppermute | solution.py:226
  647.8 96.3 %collective-permute-start.33 = (bf16[256,2560]{1,0:T(8,128)(2,1)}, bf16[256,2560]{1,0:T(8,128)(2,1)}, u32[]{:S(2)}, u32[]{:S(2)}) collective-permute-start(bf16[256,2560]{1,0:T(8,128)(2,1)} %get-tuple-element.220.refs_1_), channel_id=1, source_target_pairs={{0,4},{4,0},{8,12},{12,8},{1,5},{5,1},{9,13},{13,9},{2,6},{6,2},{1... | collective-permute-start | bytes 3932168 | tf_op jit(solution)/shard_map/ppermute | solution.py:226
  649.2 92.5 %collective-permute-start.35 = (bf16[256,2560]{1,0:T(8,128)(2,1)}, bf16[256,2560]{1,0:T(8,128)(2,1)}, u32[]{:S(2)}, u32[]{:S(2)}) collective-permute-start(bf16[256,2560]{1,0:T(8,128)(2,1)} %get-tuple-element.220.refs_1_), channel_id=1, source_target_pairs={{0,8},{4,12},{8,0},{12,4},{1,9},{5,13},{9,1},{13,5},{2,10},{6,14},... | collective-permute-start | bytes 3932168 | tf_op jit(solution)/shard_map/ppermute | solution.py:226
  650.8 90.0 %collective-permute-start.32 = (bf16[256,2560]{1,0:T(8,128)(2,1)}, bf16[256,2560]{1,0:T(8,128)(2,1)}, u32[]{:S(2)}, u32[]{:S(2)}) collective-permute-start(bf16[256,2560]{1,0:T(8,128)(2,1)} %get-tuple-element.221.refs_0_), channel_id=1, source_target_pairs={{0,4},{4,0},{8,12},{12,8},{1,5},{5,1},{9,13},{13,9},{2,6},{6,2},{1... | collective-permute-start | bytes 3932168 | tf_op jit(solution)/shard_map/ppermute | solution.py:226
  737.0 119.5 %collective-permute-start.47 = (bf16[1280,1280]{1,0:T(8,128)(2,1)}, bf16[1280,1280]{1,0:T(8,128)(2,1)S(1)}, u32[]{:S(2)}, u32[]{:S(2)}) collective-permute-start(bf16[1280,1280]{1,0:T(8,128)(2,1)} %collective-permute-done.46.refs_18_), channel_id=1, source_target_pairs={{0,1},{1,0},{2,3},{3,2},{4,5},{5,4},{6,7},{7,6},{8,9},{9,8},{10,11... | collective-permute-start | bytes 9830408 | tf_op jit(solution)/shard_map/ppermute | solution.py:226
  740.8 58.8 %collective-permute-start.36 = (bf16[256,2560]{1,0:T(8,128)(2,1)}, bf16[256,2560]{1,0:T(8,128)(2,1)S(1)}, u32[]{:S(2)}, u32[]{:S(2)}) collective-permute-start(bf16[256,2560]{1,0:T(8,128)(2,1)} %collective-permute-done.32.refs_2_), channel_id=1, source_target_pairs={{0,8},{4,12},{8,0},{12,4},{1,9},{5,13},{9,1},{13,5},{2,10},{6,14},... | collective-permute-start | bytes 3932168 | tf_op jit(solution)/shard_map/ppermute | solution.py:226
  741.7 59.0 %collective-permute-start.37 = (bf16[256,2560]{1,0:T(8,128)(2,1)}, bf16[256,2560]{1,0:T(8,128)(2,1)S(1)}, u32[]{:S(2)}, u32[]{:S(2)}) collective-permute-start(bf16[256,2560]{1,0:T(8,128)(2,1)} %collective-permute-done.35.refs_5_), channel_id=1, source_target_pairs={{0,4},{4,0},{8,12},{12,8},{1,5},{5,1},{9,13},{13,9},{2,6},{6,2},{1... | collective-permute-start | bytes 3932168 | tf_op jit(solution)/shard_map/ppermute | solution.py:226
  744.1 59.0 %collective-permute-start.40 = (bf16[256,2560]{1,0:T(8,128)(2,1)S(1)}, bf16[256,2560]{1,0:T(8,128)(2,1)S(1)}, u32[]{:S(2)}, u32[]{:S(2)}) collective-permute-start(bf16[256,2560]{1,0:T(8,128)(2,1)S(1)} %copy-done.34), channel_id=1, source_target_pairs={{0,4},{4,0},{8,12},{12,8},{1,5},{5,1},{9,13},{13,9},{2,6},{6,2},{1... | collective-permute-start | bytes 3932168 | tf_op jit(solution)/shard_map/ppermute | solution.py:226
  771.6 56.2 %collective-permute-start.41 = (bf16[256,2560]{1,0:T(8,128)(2,1)S(1)}, bf16[256,2560]{1,0:T(8,128)(2,1)S(1)}, u32[]{:S(2)}, u32[]{:S(2)}) collective-permute-start(bf16[256,2560]{1,0:T(8,128)(2,1)S(1)} %copy-done.36), channel_id=1, source_target_pairs={{0,8},{4,12},{8,0},{12,4},{1,9},{5,13},{9,1},{13,5},{2,10},{6,14},... | collective-permute-start | bytes 3932168 | tf_op jit(solution)/shard_map/ppermute | solution.py:226
  799.7 55.7 %collective-permute-start.43 = (bf16[256,2560]{1,0:T(8,128)(2,1)S(1)}, bf16[256,2560]{1,0:T(8,128)(2,1)S(1)}, u32[]{:S(2)}, u32[]{:S(2)}) collective-permute-start(bf16[256,2560]{1,0:T(8,128)(2,1)S(1)} %copy-done.38), channel_id=1, source_target_pairs={{0,8},{4,12},{8,0},{12,4},{1,9},{5,13},{9,1},{13,5},{2,10},{6,14},... | collective-permute-start | bytes 3932168 | tf_op jit(solution)/shard_map/ppermute | solution.py:226
  800.8 54.6 %collective-permute-start.44 = (bf16[256,2560]{1,0:T(8,128)(2,1)}, bf16[256,2560]{1,0:T(8,128)(2,1)S(1)}, u32[]{:S(2)}, u32[]{:S(2)}) collective-permute-start(bf16[256,2560]{1,0:T(8,128)(2,1)} %copy-done.59), channel_id=1, source_target_pairs={{0,4},{4,0},{8,12},{12,8},{1,5},{5,1},{9,13},{13,9},{2,6},{6,2},{1... | collective-permute-start | bytes 3932168 | tf_op jit(solution)/shard_map/ppermute | solution.py:226
  803.0 97.2 %collective-permute-start.45 = (bf16[1280,1280]{1,0:T(8,128)(2,1)}, bf16[1280,1280]{1,0:T(8,128)(2,1)}, u32[]{:S(2)}, u32[]{:S(2)}) collective-permute-start(bf16[1280,1280]{1,0:T(8,128)(2,1)} %get-tuple-element.191), channel_id=1, source_target_pairs={{0,2},{1,3},{2,0},{3,1},{4,6},{5,7},{6,4},{7,5},{8,10},{9,11},{10,... | collective-permute-start | bytes 9830408 | tf_op jit(solution)/shard_map/ppermute | solution.py:226
  910.0 60.1 %collective-permute-start.28 = (f32[1280,512]{1,0:T(8,128)}, f32[1280,512]{1,0:T(8,128)}, u32[]{:S(2)}, u32[]{:S(2)}) collective-permute-start(f32[1280,512]{1,0:T(8,128)} %get-tuple-element.110), channel_id=1, source_target_pairs={{0,4},{4,0},{8,12},{12,8},{1,5},{5,1},{9,13},{13,9},{2,6},{6,2},{1... | collective-permute-start | bytes 7864328 | tf_op jit(solution)/shard_map/ppermute | solution.py:226
  911.1 60.1 %collective-permute-start.29 = (f32[1280,512]{1,0:T(8,128)}, f32[1280,512]{1,0:T(8,128)}, u32[]{:S(2)}, u32[]{:S(2)}) collective-permute-start(f32[1280,512]{1,0:T(8,128)} %get-tuple-element.114), channel_id=1, source_target_pairs={{0,8},{4,12},{8,0},{12,4},{1,9},{5,13},{9,1},{13,5},{2,10},{6,14},... | collective-permute-start | bytes 7864328 | tf_op jit(solution)/shard_map/ppermute | solution.py:226
  912.1 113.6 %collective-permute-start.30 = (f32[1280,512]{1,0:T(8,128)}, f32[1280,512]{1,0:T(8,128)}, u32[]{:S(2)}, u32[]{:S(2)}) collective-permute-start(f32[1280,512]{1,0:T(8,128)} %get-tuple-element.115), channel_id=1, source_target_pairs={{0,4},{4,0},{8,12},{12,8},{1,5},{5,1},{9,13},{13,9},{2,6},{6,2},{1... | collective-permute-start | bytes 7864328 | tf_op jit(solution)/shard_map/ppermute | solution.py:226
  913.2 113.3 %collective-permute-start.31 = (f32[1280,512]{1,0:T(8,128)}, f32[1280,512]{1,0:T(8,128)}, u32[]{:S(2)}, u32[]{:S(2)}) collective-permute-start(f32[1280,512]{1,0:T(8,128)} %get-tuple-element.116), channel_id=1, source_target_pairs={{0,8},{4,12},{8,0},{12,4},{1,9},{5,13},{9,1},{13,5},{2,10},{6,14},... | collective-permute-start | bytes 7864328 | tf_op jit(solution)/shard_map/ppermute | solution.py:226
  915.3 111.2 %collective-permute-start.53 = (bf16[1280,896]{1,0:T(8,128)(2,1)}, bf16[1280,896]{1,0:T(8,128)(2,1)}, u32[]{:S(2)}, u32[]{:S(2)}) collective-permute-start(bf16[1280,896]{1,0:T(8,128)(2,1)} %slice.325), channel_id=1, source_target_pairs={{0,2},{1,3},{2,0},{3,1},{4,6},{5,7},{6,4},{7,5},{8,10},{9,11},{10,... | collective-permute-start | bytes 6881288 | tf_op jit(solution)/shard_map/ppermute | solution.py:226
  970.1 226.4 %collective-permute-start.72 = (bf16[1280,2048]{1,0:T(8,128)(2,1)}, bf16[1280,2048]{1,0:T(8,128)(2,1)}, u32[]{:S(2)}, u32[]{:S(2)}) collective-permute-start(bf16[1280,2048]{1,0:T(8,128)(2,1)} %get-tuple-element.97.refs_1_.refs_2_), channel_id=1, source_target_pairs={{0,1},{1,0},{2,3},{3,2},{4,5},{5,4},{6,7},{7,6},{8,9},{9,8},{10,11... | collective-permute-start | bytes 15728648 | tf_op jit(solution)/shard_map/ppermute | solution.py:226
  971.1 231.4 %collective-permute-start.73 = (bf16[1280,2048]{1,0:T(8,128)(2,1)}, bf16[1280,2048]{1,0:T(8,128)(2,1)}, u32[]{:S(2)}, u32[]{:S(2)}) collective-permute-start(bf16[1280,2048]{1,0:T(8,128)(2,1)} %get-tuple-element.100.refs_2_.refs_4_), channel_id=1, source_target_pairs={{0,1},{1,0},{2,3},{3,2},{4,5},{5,4},{6,7},{7,6},{8,9},{9,8},{10,11... | collective-permute-start | bytes 15728648 | tf_op jit(solution)/shard_map/ppermute | solution.py:226
  1025.8 176.7 %collective-permute-start.74 = (bf16[896,2048]{1,0:T(8,128)(2,1)}, bf16[896,2048]{1,0:T(8,128)(2,1)}, u32[]{:S(2)}, u32[]{:S(2)}) collective-permute-start(bf16[896,2048]{1,0:T(8,128)(2,1)} %get-tuple-element.105.refs_1_.refs_6_), channel_id=1, source_target_pairs={{0,1},{1,0},{2,3},{3,2},{4,5},{5,4},{6,7},{7,6},{8,9},{9,8},{10,11... | collective-permute-start | bytes 11010056 | tf_op jit(solution)/shard_map/ppermute | solution.py:226
  1029.8 101.4 %collective-permute-start.49 = (f32[1280,256]{1,0:T(8,128)}, f32[1280,256]{1,0:T(8,128)}, u32[]{:S(2)}, u32[]{:S(2)}) collective-permute-start(f32[1280,256]{1,0:T(8,128)} %get-tuple-element.202), channel_id=1, source_target_pairs={{0,8},{4,12},{8,0},{12,4},{1,9},{5,13},{9,1},{13,5},{2,10},{6,14},... | collective-permute-start | bytes 3932168 | tf_op jit(solution)/shard_map/ppermute | solution.py:226
  1041.3 89.9 %collective-permute-start.50 = (f32[1280,256]{1,0:T(8,128)}, f32[1280,256]{1,0:T(8,128)}, u32[]{:S(2)}, u32[]{:S(2)}) collective-permute-start(f32[1280,256]{1,0:T(8,128)} %get-tuple-element.200), channel_id=1, source_target_pairs={{0,4},{4,0},{8,12},{12,8},{1,5},{5,1},{9,13},{13,9},{2,6},{6,2},{1... | collective-permute-start | bytes 3932168 | tf_op jit(solution)/shard_map/ppermute | solution.py:226
  1131.2 72.8 %collective-permute-start.71 = (bf16[2048,1280]{1,0:T(8,128)(2,1)}, bf16[2048,1280]{1,0:T(8,128)(2,1)}, u32[]{:S(2)}, u32[]{:S(2)}) collective-permute-start(bf16[2048,1280]{1,0:T(8,128)(2,1)} %get-tuple-element.232), channel_id=1, source_target_pairs={{0,1},{1,0},{2,3},{3,2},{4,5},{5,4},{6,7},{7,6},{8,9},{9,8},{10,11... | collective-permute-start | bytes 15728648 | tf_op jit(solution)/shard_map/ppermute | solution.py:226
  1193.3 66.8 %collective-permute-start.64 = (bf16[1280,2048]{1,0:T(8,128)(2,1)}, bf16[1280,2048]{1,0:T(8,128)(2,1)}, u32[]{:S(2)}, u32[]{:S(2)}) collective-permute-start(bf16[1280,2048]{1,0:T(8,128)(2,1)} %bitcast.27), channel_id=1, source_target_pairs={{0,1},{1,0},{2,3},{3,2},{4,5},{5,4},{6,7},{7,6},{8,9},{9,8},{10,11... | collective-permute-start | bytes 15728648 | tf_op jit(solution)/shard_map/ppermute | solution.py:226
  1196.5 64.5 %collective-permute-start.65 = (bf16[2048,1280]{1,0:T(8,128)(2,1)}, bf16[2048,1280]{1,0:T(8,128)(2,1)}, u32[]{:S(2)}, u32[]{:S(2)}) collective-permute-start(bf16[2048,1280]{1,0:T(8,128)(2,1)} %get-tuple-element.126.refs_2_), channel_id=1, source_target_pairs={{0,1},{1,0},{2,3},{3,2},{4,5},{5,4},{6,7},{7,6},{8,9},{9,8},{10,11... | collective-permute-start | bytes 15728648 | tf_op jit(solution)/shard_map/ppermute | solution.py:226
  1202.5 175.3 %collective-permute-start.66 = (bf16[2048,1280]{1,0:T(8,128)(2,1)}, bf16[2048,1280]{1,0:T(8,128)(2,1)}, u32[]{:S(2)}, u32[]{:S(2)}) collective-permute-start(bf16[2048,1280]{1,0:T(8,128)(2,1)} %get-tuple-element.130.refs_4_), channel_id=1, source_target_pairs={{0,1},{1,0},{2,3},{3,2},{4,5},{5,4},{6,7},{7,6},{8,9},{9,8},{10,11... | collective-permute-start | bytes 15728648 | tf_op jit(solution)/shard_map/ppermute | solution.py:226
  1202.5 78.2 %collective-permute-start.55 = (bf16[256,2560]{0,1:T(8,128)(2,1)}, bf16[256,2560]{0,1:T(8,128)(2,1)}, u32[]{:S(2)}, u32[]{:S(2)}) collective-permute-start(bf16[256,2560]{0,1:T(8,128)(2,1)} %fusion.2), channel_id=1, source_target_pairs={{0,2},{1,3},{2,0},{3,1},{4,6},{5,7},{6,4},{7,5},{8,10},{9,11},{10,... | collective-permute-start | bytes 3932168 | tf_op jit(solution)/shard_map/ppermute | solution.py:226
  1204.0 77.5 %collective-permute-start.62 = (f32[1280,512]{0,1:T(8,128)}, f32[1280,512]{0,1:T(8,128)}, u32[]{:S(2)}, u32[]{:S(2)}) collective-permute-start(f32[1280,512]{0,1:T(8,128)} %copy.81), channel_id=1, source_target_pairs={{0,8},{4,12},{8,0},{12,4},{1,9},{5,13},{9,1},{13,5},{2,10},{6,14},... | collective-permute-start | bytes 7864328 | tf_op jit(solution)/shard_map/ppermute | solution.py:226
  1260.1 60.1 %collective-permute-start.60 = (f32[1280,512]{0,1:T(8,128)}, f32[1280,512]{0,1:T(8,128)}, u32[]{:S(2)}, u32[]{:S(2)}) collective-permute-start(f32[1280,512]{0,1:T(8,128)} %copy.78), channel_id=1, source_target_pairs={{0,4},{4,0},{8,12},{12,8},{1,5},{5,1},{9,13},{13,9},{2,6},{6,2},{1... | collective-permute-start | bytes 7864328 | tf_op jit(solution)/shard_map/ppermute | solution.py:226
  1261.1 59.1 %collective-permute-start.58 = (f32[1280,512]{0,1:T(8,128)}, f32[1280,512]{0,1:T(8,128)}, u32[]{:S(2)}, u32[]{:S(2)}) collective-permute-start(f32[1280,512]{0,1:T(8,128)} %copy.75), channel_id=1, source_target_pairs={{0,8},{4,12},{8,0},{12,4},{1,9},{5,13},{9,1},{13,5},{2,10},{6,14},... | collective-permute-start | bytes 7864328 | tf_op jit(solution)/shard_map/ppermute | solution.py:226
  1280.7 98.0 %collective-permute-start.67 = (bf16[2048,896]{1,0:T(8,128)(2,1)}, bf16[2048,896]{1,0:T(8,128)(2,1)}, u32[]{:S(2)}, u32[]{:S(2)}) collective-permute-start(bf16[2048,896]{1,0:T(8,128)(2,1)} %get-tuple-element.180.refs_6_), channel_id=1, source_target_pairs={{0,1},{1,0},{2,3},{3,2},{4,5},{5,4},{6,7},{7,6},{8,9},{9,8},{10,11... | collective-permute-start | bytes 11010056 | tf_op jit(solution)/shard_map/ppermute | solution.py:226
  1281.5 93.8 %collective-permute-start.56 = (f32[1280,512]{0,1:T(8,128)}, f32[1280,512]{0,1:T(8,128)}, u32[]{:S(2)}, u32[]{:S(2)}) collective-permute-start(f32[1280,512]{0,1:T(8,128)} %copy.72), channel_id=1, source_target_pairs={{0,4},{4,0},{8,12},{12,8},{1,5},{5,1},{9,13},{13,9},{2,6},{6,2},{1... | collective-permute-start | bytes 7864328 | tf_op jit(solution)/shard_map/ppermute | solution.py:226
  1320.1 108.9 %collective-permute-start.68 = (bf16[2048,1280]{1,0:T(8,128)(2,1)}, bf16[2048,1280]{1,0:T(8,128)(2,1)}, u32[]{:S(2)}, u32[]{:S(2)}) collective-permute-start(bf16[2048,1280]{1,0:T(8,128)(2,1)} %get-tuple-element.181.refs_2_), channel_id=1, source_target_pairs={{0,1},{1,0},{2,3},{3,2},{4,5},{5,4},{6,7},{7,6},{8,9},{9,8},{10,11... | collective-permute-start | bytes 15728648 | tf_op jit(solution)/shard_map/ppermute | solution.py:226
  1320.1 109.9 %collective-permute-start.69 = (bf16[2048,1280]{1,0:T(8,128)(2,1)}, bf16[2048,1280]{1,0:T(8,128)(2,1)}, u32[]{:S(2)}, u32[]{:S(2)}) collective-permute-start(bf16[2048,1280]{1,0:T(8,128)(2,1)} %get-tuple-element.182.refs_4_), channel_id=1, source_target_pairs={{0,1},{1,0},{2,3},{3,2},{4,5},{5,4},{6,7},{7,6},{8,9},{9,8},{10,11... | collective-permute-start | bytes 15728648 | tf_op jit(solution)/shard_map/ppermute | solution.py:226
  1375.2 55.8 %collective-permute-start.70 = (bf16[2048,896]{1,0:T(8,128)(2,1)}, bf16[2048,896]{1,0:T(8,128)(2,1)}, u32[]{:S(2)}, u32[]{:S(2)}) collective-permute-start(bf16[2048,896]{1,0:T(8,128)(2,1)} %get-tuple-element.183.refs_6_), channel_id=1, source_target_pairs={{0,1},{1,0},{2,3},{3,2},{4,5},{5,4},{6,7},{7,6},{8,9},{9,8},{10,11... | collective-permute-start | bytes 11010056 | tf_op jit(solution)/shard_map/ppermute | solution.py:226
  1377.7 102.2 %collective-permute-start.63 = (f32[1280,256]{0,1:T(8,128)}, f32[1280,256]{0,1:T(8,128)}, u32[]{:S(2)}, u32[]{:S(2)}) collective-permute-start(f32[1280,256]{0,1:T(8,128)} %slice_add_fusion), channel_id=1, source_target_pairs={{0,4},{4,0},{8,12},{12,8},{1,5},{5,1},{9,13},{13,9},{2,6},{6,2},{1... | collective-permute-start | bytes 3932168 | tf_op jit(solution)/shard_map/ppermute | solution.py:226
  1378.7 103.7 %collective-permute-start.61 = (f32[1280,256]{0,1:T(8,128)}, f32[1280,256]{0,1:T(8,128)}, u32[]{:S(2)}, u32[]{:S(2)}) collective-permute-start(f32[1280,256]{0,1:T(8,128)} %slice_add_fusion.2), channel_id=1, source_target_pairs={{0,8},{4,12},{8,0},{12,4},{1,9},{5,13},{9,1},{13,5},{2,10},{6,14},... | collective-permute-start | bytes 3932168 | tf_op jit(solution)/shard_map/ppermute | solution.py:226
  1429.0 56.1 %collective-permute-start.59 = (f32[1280,256]{0,1:T(8,128)}, f32[1280,256]{0,1:T(8,128)}, u32[]{:S(2)}, u32[]{:S(2)}) collective-permute-start(f32[1280,256]{0,1:T(8,128)} %slice_add_fusion.4), channel_id=1, source_target_pairs={{0,4},{4,0},{8,12},{12,8},{1,5},{5,1},{9,13},{13,9},{2,6},{6,2},{1... | collective-permute-start | bytes 3932168 | tf_op jit(solution)/shard_map/ppermute | solution.py:226
  1430.1 57.1 %collective-permute-start.57 = (f32[1280,256]{0,1:T(8,128)}, f32[1280,256]{0,1:T(8,128)}, u32[]{:S(2)}, u32[]{:S(2)}) collective-permute-start(f32[1280,256]{0,1:T(8,128)} %slice_add_fusion.6), channel_id=1, source_target_pairs={{0,8},{4,12},{8,0},{12,4},{1,9},{5,13},{9,1},{13,5},{2,10},{6,14},... | collective-permute-start | bytes 3932168 | tf_op jit(solution)/shard_map/ppermute | solution.py:226
  (74 other events, 1894.6 us)

commit v2 on v1

--- a/solution.py
+++ b/solution.py
@@ -3,6 +3,7 @@
 import jax
 import jax.numpy as jnp
 from jax import lax
+from jax.experimental.layout import Layout, with_layout_constraint
 from jax.experimental import pallas as pl
 from jax.experimental.pallas import tpu as pltpu
 from jax.sharding import PartitionSpec as P
@@ -26,52 +27,54 @@
     return pl.CostEstimate(flops=int(flops), bytes_accessed=int(nbytes), transcendentals=0)
 
 
-def quarters(buf, m, ws):
-    dq = ws[0].shape[0]
-    acc = dot(buf[m, :, :dq], ws[0][...])
-    for k in range(1, 4):
-        acc += dot(buf[m, :, k * dq : (k + 1) * dq], ws[k][...])
-    return acc
-
-
 def load(pieces, buf, sems):
     m, n = pl.program_id(0), pl.program_id(1)
-    r, w = pieces[0].shape
+    r = pieces[0].shape[0]
     copies = []
     for k, p in enumerate(pieces):
-        g, row, col = k // 8, k % 8 // 2, k % 2
-        dst = buf.at[g, pl.ds(row * r, r), pl.ds(col * w, w)]
-        copies.append(pltpu.make_async_copy(p, dst, sems.at[k]))
+        copies.append(pltpu.make_async_copy(p, buf.at[k // 4, pl.ds(k % 4 * r, r)], sems.at[k]))
 
     @pl.when((m == 0) & (n == 0))
     def _():
         for c in copies:
             c.start()
-        for c in copies[:8]:
+        for c in copies[:4]:
             c.wait()
 
     @pl.when((m == 1) & (n == 0))
     def _():
-        for c in copies[8:]:
+        for c in copies[4:]:
             c.wait()
 
     return m
 
 
+def pair(buf, m, w0, w1):
+    dq = w0.shape[0]
+    return dot(buf[m, :, :dq], w0[...]) + dot(buf[m, :, dq:], w1[...])
+
+
+def near_body(n_out, *refs):
+    pieces, ws, outs, (buf, sems) = refs[:8], refs[8 : 8 + 2 * n_out], refs[8 + 2 * n_out : -2], refs[-2:]
+    m = load(pieces, buf, sems)
+    for k in range(n_out):
+        outs[k][...] = pair(buf, m, ws[2 * k], ws[2 * k + 1])
+
+
 def fwd_body(*refs):
-    pieces, ws, (a_ref, b_ref, ht_ref), (buf, sems) = refs[:16], refs[16:24], refs[24:27], refs[27:]
+    pieces, ws, (a0, b0, a_ref, b_ref, ht_ref), (buf, sems) = refs[:8], refs[8:12], refs[12:17], refs[17:]
     m = load(pieces, buf, sems)
-    a = quarters(buf, m, ws[:4])
-    b = quarters(buf, m, ws[4:])
+    a = a0[...] + pair(buf, m, ws[0], ws[1])
+    b = b0[...] + pair(buf, m, ws[2], ws[3])
     a_ref[...] = a
     b_ref[...] = b
     ht_ref[...] = (a * jax.nn.sigmoid(a) * b).T.astype(bf)
 
 
 def bwd_body(*refs):
-    pieces, ws, (a_ref, b_ref, da_ref, db_ref, dat_ref, dbt_ref), (buf, sems) = refs[:16], refs[16:20], refs[20:26], refs[26:]
+    pieces, ws, (g0, a_ref, b_ref, da_ref, db_ref, dat_ref, dbt_ref), (buf, sems) = refs[:8], refs[8:10], refs[10:17], refs[17:]
     m = load(pieces, buf, sems)
-    g = quarters(buf, m, ws)
+    g = g0[...] + pair(buf, m, ws[0], ws[1])
     a = a_ref[...]
     s = jax.nn.sigmoid(a)
     da = g * b_ref[...] * s * (1.0 + a * (1.0 - s))
@@ -85,45 +88,45 @@
         dbt_ref[...] = db.T.astype(bf)
 
 
-def weight_specs(own, c):
-    dq = own.shape[0]
-    first = c * (CHUNK // TILE)
-    whole = pl.BlockSpec((dq, TILE), lambda m, n: (0, first + n))
-    piece = pl.BlockSpec((dq, TILE), lambda m, n: (0, n))
-    return [whole, whole, piece, piece]
-
-
-def grouped(body, pieces, ws, wspecs, extra, fc, outs, flops):
+def grouped(body, pieces, ws, first, extra, fc, outs, aliases={}):
     tm = 4 * pieces[0].shape[0]
-    d = 2 * pieces[0].shape[1]
+    d = pieces[0].shape[1]
+    dq = ws[0].shape[0]
     nt = pl.cdiv(fc, TILE)
     specs = {
         "mn": (pl.BlockSpec((tm, TILE), lambda m, n: (m, n)), (2 * tm, fc)),
         "nm": (pl.BlockSpec((TILE, tm), lambda m, n: (n, m)), (fc, 2 * tm)),
         "n0": (pl.BlockSpec((TILE, tm), lambda m, n: (n + m * (nt - 1 - n), 0)), (fc, tm)),
     }
+    wspec = pl.BlockSpec((dq, TILE), lambda m, n: (0, first + n))
     return pl.pallas_call(
         body,
         grid=(2, nt),
-        in_specs=[pl.BlockSpec(memory_space=pl.ANY)] * 16 + wspecs + [specs["mn"][0]] * len(extra),
+        in_specs=[pl.BlockSpec(memory_space=pltpu.HBM)] * 8 + [wspec] * len(ws) + [specs["mn"][0]] * len(extra),
         out_specs=[specs[k][0] for k, _ in outs],
         out_shape=[jax.ShapeDtypeStruct(specs[k][1], t) for k, t in outs],
-        scratch_shapes=[pltpu.VMEM((2, tm, d), bf), pltpu.SemaphoreType.DMA((16,))],
+        scratch_shapes=[pltpu.VMEM((2, tm, d), bf), pltpu.SemaphoreType.DMA((8,))],
+        input_output_aliases=aliases,
         compiler_params=params(),
-        cost_estimate=cost(flops * tm * d * fc, 8e7),
+        cost_estimate=cost(2 * len(ws) * tm * d * fc, 8e7),
     )(*pieces, *ws, *extra)
 
 
-def forward(xp, wg, wu, c):
-    fc = wg[2].shape[1]
+def near(pieces, ws, c, fc):
+    n_out = len(ws) // 2
+    return grouped(functools.partial(near_body, n_out), pieces, ws, c * (CHUNK // TILE), [], fc, [("mn", f32)] * n_out)
+
+
+def forward(pieces, ws, acc):
+    fc = ws[0].shape[1]
     outs = [("mn", f32), ("mn", f32), ("nm", bf)]
-    return grouped(fwd_body, xp, wg + wu, weight_specs(wg[0], c) * 2, [], fc, outs, 8)
-
-
-def backward(dyp, wd, a, b, c):
-    fc = wd[2].shape[1]
+    return grouped(fwd_body, pieces, ws, 0, acc, fc, outs, {12: 0, 13: 1})
+
+
+def backward(pieces, ws, extra):
+    fc = ws[0].shape[1]
     outs = [("mn", bf), ("mn", bf), ("n0", bf), ("n0", bf)]
-    return grouped(bwd_body, dyp, wd, weight_specs(wd[0], c), [a, b], fc, outs, 4)
+    return grouped(bwd_body, pieces, ws, 0, extra, fc, outs)
 
 
 def part_body(axis, terms, nw, nt, groups, has_acc, *refs):
@@ -216,6 +219,40 @@
     )(*fixed, *[v for p in streams for v in p], *([] if prev is None else [prev]))
 
 
+def finish_body(n_sums, natural, *refs):
+    base, sums, rest, out = refs[0], refs[1 : 1 + 3 * n_sums], refs[1 + 3 * n_sums : -1], refs[-1]
+    dq = sums[0].shape[0]
+    i = lax.axis_index("dp") if natural else 0
+
+    def at(k):
+        return pl.ds(pl.multiple_of((i ^ k) * dq, 128), dq) if natural else pl.ds(k * dq, dq)
+
+    for k in range(n_sums):
+        keep, r1, r2 = sums[3 * k : 3 * k + 3]
+        v = (keep[...] + r1[...] + r2[...]).T
+        out[:, at(k)] = (base[:, at(k)].astype(f32) + v).astype(bf)
+    for k in range(n_sums, n_sums + 2 * len(rest)):
+        p = k - n_sums
+        out[:, at(k)] = rest[0][:, p * dq : (p + 1) * dq]
+
+
+def finish(base, sums, rest=(), natural=True):
+    blk = base.shape[0]
+    dq = sums[0][0].shape[0]
+    sspec = pl.BlockSpec((dq, blk), lambda j: (0, 0))
+    whole = lambda v: pl.BlockSpec(v.shape, lambda j: (0, 0))
+    return pl.pallas_call(
+        functools.partial(finish_body, len(sums), natural),
+        grid=(1,),
+        in_specs=[whole(base)] + [sspec] * (3 * len(sums)) + [whole(v) for v in rest],
+        out_specs=whole(base),
+        out_shape=jax.ShapeDtypeStruct(base.shape, bf),
+        compiler_params=params(),
+        cost_estimate=cost(1e8, 2e7),
+        name="finish",
+    )(base, *[v for t in sums for v in t], *rest)
+
+
 def solution(mesh):
     rows = P(("dp", "tp"), None)
     wsp = P("dp", "tp")
@@ -227,9 +264,6 @@
 
     px, pc = hop("dp", 2), hop("dp", 1)
     py, pz = hop("tp", 1), hop("tp", 2)
-
-    def after(v, *deps):
-        return lax.optimization_barrier((v, deps))[0]
 
     def cross(v):
         return px(v)
@@ -243,11 +277,10 @@
         def reorder(v):
             return jnp.concatenate([lax.dynamic_slice_in_dim(v, (i ^ k) * dq, dq, 1) for k in range(4)], axis=1)
 
-        def gather(v, dep=None):
+        def gather(v):
             va, vb = v[:, : 2 * dq], v[:, 2 * dq :]
             a_y, b_z, b_y, a_z = py(va), pz(vb), py(vb), pz(va)
-            a1, b1 = (a_y, b_z) if dep is None else after((a_y, b_z), *dep)
-            a_yz, b_yz = pz(a1), py(b1)
+            a_yz, b_yz = pz(a_y), py(b_z)
             return [va, vb, a_y, b_y, a_z, b_z, a_yz, b_yz]
 
         def swap(v):
@@ -256,65 +289,64 @@
         piece = lambda w, c: w[:, starts[c] : starts[c] + CHUNK]
         wgx, wux, wdx = [None] * nc, [None] * nc, [None] * nc
         xo, dyo = reorder(x), reorder(dy)
-        x_other = swap(cross(xo))
-        for c in range(nc):
-            if c == nc - 1:
-                dy_other = cross(dyo)
+        x_cross, dy_cross = cross(xo), cross(dyo)
+        for c in range(nc):
             wgx[c] = cross(piece(w_gate, c))
             wux[c] = cross(piece(w_up, c))
         wd_t = w_down.T
         for c in range(nc):
             wdx[c] = cross(piece(wd_t, c))
         wg_s, wu_s, wd_s = pc(w_gate), pc(w_up), pc(wd_t)
-
+        width = lambda c: wgx[c].shape[1]
+
+        x_other = swap(x_cross)
         xp = gather(xo) + gather(x_other)
-        dyp = gather(after(dyo, *xp[8:]))
+        dyp = gather(dyo) + gather(swap(dy_cross))
         blk = xo.shape[0]
         col = lambda ps, k: jnp.concatenate([p[:, k * dq : (k + 1) * dq] for p in ps[0::2]], axis=0)
-        xq, xq_s = col(xp, 0).T, pc(col(xp, 1).T)
-
-        a, b, ht, ht_s, across = [], [], [], [], []
-        done = xp
-        for c in range(nc):
-            gx, ux = after((wgx[c], wux[c]), *done)
+        row_major = lambda v: with_layout_constraint(v, Layout(major_to_minor=(0, 1)))
+        xq, xq_out = row_major(col(xp, 0)).T, row_major(col(xp, 1)).T
+        xq_s = pc(xq_out)
+        dyq, dyq_s = col(dyp, 0), pc(col(dyp, 1))
+
+        acc = [None] * nc
+        xa = xp[0::2]
+        for c in range(nc):
+            acc[c] = near(xa, [w_gate, wg_s, w_up, wu_s], c, width(c))
+        a, b, ht, ht_s, across, g0 = [], [], [], [], [], [None] * nc
+        for c in range(nc):
+            gx, ux = wgx[c], wux[c]
             gs, us = pc(gx), pc(ux)
             across.append([(gx, ux), (gs, us)])
-            ac, bc, htc = forward(xp, [w_gate, wg_s, gx, gs], [w_up, wu_s, ux, us], c)
+            ac, bc, htc = forward(xp[1::2], [gx, gs, ux, us], acc[c])
             a.append(ac)
             b.append(bc)
             ht.append(htc)
             ht_s.append(pc(htc))
-            done = [htc]
+            if c == 0:
+                for k in range(nc):
+                    (g0[k],) = near(dyp[0::2], [wd_t, wd_s], k, width(k))
             if c == nc - 2:
                 terms = [(0, starts[k], k) for k in range(nc - 1)]
-                dy_other = swap(after(dy_other, htc))
                 yacc = [partial_sums([w], ht, terms, "yz"[q], 2) for q, w in enumerate((wd_t, wd_s))]
-                dyp += gather(dy_other, [yacc[0][0], yacc[1][0]])
-                dyq, dyq_s = col(dyp, 0), pc(col(dyp, 1))
-                done = [yacc[0][0], yacc[1][0]]
         yacc = [partial_sums([w], ht[-1:], [(0, starts[-1], 0)], "yz"[q], 2, yacc[q]) for q, w in enumerate((wd_t, wd_s))]
-        done = [yacc[0][0], yacc[1][0]]
 
         def first_hop(axis, send):
             return (py if axis == "y" else pz)(send)
 
         def second_hop(axis, keep, r):
-            s = keep[:, blk:] + r[:, blk:]
-            return keep[:, :blk] + r[:, :blk], (pz if axis == "y" else py)(s)
+            return (pz if axis == "y" else py)(keep[:, blk:] + r[:, blk:])
 
         order = [(1, 0), (1, 1), (0, 0), (0, 1)]
         y_first = {(g, q): first_hop("yz"[q], yacc[q][2 * g + 1]) for g, q in order}
 
         da, db, dat, dbt = [], [], [], []
         for c in range(nc):
-            dx_ = after(wdx[c], *done)
-            grads = backward(dyp, [wd_t, wd_s, dx_, pc(dx_)], a[c], b[c], c)
+            grads = backward(dyp[1::2], [wdx[c], pc(wdx[c])], [g0[c], a[c], b[c]])
             for lst, v in zip((da, db, dat, dbt), grads):
                 lst.append(v)
-            done = [da[c]]
-            if c == nc - 2:
-                y_first = dict(zip(order, after([y_first[k] for k in order], *done)))
-                y_second = {(g, q): second_hop("yz"[q], yacc[q][2 * g], y_first[g, q]) for g, q in order}
+        dwd = weight_grad((dyq, dyq_s), list(zip(ht, ht_s)), True, fl, 0)
+        y_second = {(g, q): second_hop("yz"[q], yacc[q][2 * g], y_first[g, q]) for g, q in order}
         da_s, db_s = [pc(v) for v in da], [pc(v) for v in db]
 
         dx_keep, dx_first = [], []
@@ -325,30 +357,22 @@
             else:
                 ws = [across[c][q - 2][0] for c in range(nc)] + [across[c][q - 2][1] for c in range(nc)]
                 terms = [(k, 0, k) for k in range(2 * nc)]
-            ts = dat + dbt
-            if q:
-                ts = after(ts, dx_keep[-1])
-            keep, send = partial_sums(list(ws), ts, terms, "yzyz"[q], 1)
+            keep, send = partial_sums(list(ws), dat + dbt, terms, "yzyz"[q], 1)
             dx_keep.append(keep)
             dx_first.append(first_hop("yzyz"[q], send))
 
-        y_second = dict(zip(order, after([y_second[k] for k in order], *dx_keep)))
-        part = lambda g: jnp.concatenate([(s + r).T for s, r in (y_second[g, 0], y_second[g, 1])], axis=1)
-        y_out = (x_other[:, : 2 * dq].astype(f32) + part(1)).astype(bf)
+        sums = lambda g: [(yacc[q][2 * g], y_first[g, q], y_second[g, q]) for q in range(2)]
+        y_out = finish(x_other[:, : 2 * dq], sums(1), natural=False)
         y_in = px(y_out)
-        y_own = (xo[:, : 2 * dq].astype(f32) + part(0)).astype(bf)
-        y = reorder(jnp.concatenate([y_own, y_in], axis=1))
-
-        xq, dyq = after((xq, dyq), *dx_keep)
-        dwd = weight_grad((dyq, dyq_s), list(zip(ht, ht_s)), True, fl, 0)
+
         dwg = weight_grad((xq, xq_s), list(zip(da, da_s)), False, fl, 0)
         dwu = weight_grad((xq, xq_s), list(zip(db, db_s)), False, fl, 0)
-
-        sums = []
+        y = finish(x, sums(0), [y_in])
+
+        dx_sums = []
         for q in range(4):
-            sums.append(second_hop("yzyz"[q], dx_keep[q], dx_first[q]))
-        dx = jnp.concatenate([(s + r).T for s, r in sums], axis=1)
-        dx = reorder((dyo.astype(f32) + dx).astype(bf))
+            dx_sums.append((dx_keep[q], dx_first[q], second_hop("yzyz"[q], dx_keep[q], dx_first[q])))
+        dx = finish(dy, dx_sums)
         return y, dx, dwg, dwu, dwd
 
     return jax.shard_map(body, mesh=mesh, in_specs=(rows, wsp, wsp, dsp, rows), out_specs=(rows, rows, wsp, wsp, dsp), check_vma=False)

time: 1500 us -> 1600 us (1.067)
  waiting for transfers between devices: 599 us -> 725 us
  Pallas kernels: 632 us -> 699 us
  local copies, waits for them, and re-layouts: 139 us -> 83.2 us
  other arithmetic: 56.8 us -> 16 us
    ppermute x75, waiting for transfers between devices: 599 us -> 725 us  [hop(): return lambda v: lax.ppermute(v, axis, pairs)]
    pallas_call x6 -> x12, Pallas kernels: 308 us -> 352 us  [grouped(): pl.pallas_call(body, grid=(2, nt), in_specs=[pl.BlockSpec(memory_space=pl...]
    ppermute x12 -> x0, local copies, waits for them, and re-layouts: 24.3 us -> none  [hop(): return lambda v: lax.ppermute(v, axis, pairs)]
    pallas_call x8 -> x0, local copies, waits for them, and re-layouts: 24 us -> none  [partial_sums(): pl.pallas_call(functools.partial(part_body, axis, terms, len(ws), len(ts)...]
    pallas_call x0 -> x3, Pallas kernels: none -> 21.8 us  [finish(): pl.pallas_call(functools.partial(finish_body, len(sums), natural), grid=(...]
    transpose x8 -> x0, other arithmetic: 16.8 us -> none  [the longest x4 8.77 us: body(): dx = jnp.concatenate([(s + r).T for s, r in sums], axis=1)]
    unnamed x147 -> x128, local copies, waits for them, and re-layouts: 49.1 us -> 39.3 us
  transfers between devices with their start and end apart: 75 -> 75, of which waited for: 25 -> 29; matrix products, arithmetic and copies ran while one was open for 12% -> 6% of each run, Pallas kernels for 42% -> 41%
where the time goes in v2:
time: 1600 us; the launch traced here: 1590 us
  waiting for transfers between devices  725 us (45%)
  Pallas kernels  699 us (44%)
  local copies, waits for them, and re-layouts  83.2 us (5%)
  starting transfers between devices  65.4 us (4%)
  other arithmetic  16 us (1%)
    ppermute x75, waiting for transfers between devices, hop(): return lambda v: lax.ppermute(v, axis, pairs)  725 us
    pallas_call x12, Pallas kernels, grouped(): pl.pallas_call(body, grid=(2, nt), in_specs=[pl.BlockSpec(memory_space=pl...  352 us
    pallas_call x8, Pallas kernels, partial_sums(): pl.pallas_call(functools.partial(part_body, axis, terms, len(ws), len(ts)...  179 us
    pallas_call x3, Pallas kernels, weight_grad(): pl.pallas_call(functools.partial(dw_body, counts, rows), grid=(n,), in_sp...  147 us
    ppermute x75, starting transfers between devices, hop(): return lambda v: lax.ppermute(v, axis, pairs)  65.4 us
    unnamed x128, local copies, waits for them, and re-layouts  39.3 us
  transfers between devices with their start and end apart: 75, of which 29 were waited for; matrix products, arithmetic and copies ran while one was open for 6% of the time, Pallas kernels for 41%

profile of v2, /device:TPU:0, one launch (start us, length us, event | category | flops | bytes accessed | tf_op | source)
XLA Modules:
  0.0 1590.3 jit_solution(4704626391145322055)
XLA Ops:
  0.7 4.4 constant_dynamic-update-slice_fusion
  5.1 3.3 collective-permute-start.46
  13.8 24.3 %collective-permute-done.46.refs_1_ = bf16[256,2560]{1,0:T(8,128)(2,1)} collective-permute-done((bf16[256,2560]{1,0:T(8,128)(2,1)S(1)}, bf16[256,2560]{1,0:T(8,128)(2,1)}, u32[]{:S(2)}, u32[]{:S(2)}) %collective-permute-start.46) | collective-permute-done | bytes 1310752 | tf_op jit(solution)/shard_map/ppermute | solution.py:263
  40.1 3.2 slice.189
  43.4 3.2 slice.188
  48.1 18.0 %collective-permute-done.11.refs_1_ = bf16[256,2560]{1,0:T(8,128)(2,1)S(1)} collective-permute-done((bf16[256,2560]{1,0:T(8,128)(2,1)S(1)}, bf16[256,2560]{1,0:T(8,128)(2,1)S(1)}, u32[]{:S(2)}, u32[]{:S(2)}) %collective-permute-start.11) | collective-permute-done | bytes 1310752 | tf_op jit(solution)/shard_map/ppermute | solution.py:263
  70.9 25.3 %collective-permute-done.1.refs_2_ = bf16[256,2560]{1,0:T(8,128)(2,1)S(1)} collective-permute-done((bf16[256,2560]{1,0:T(8,128)(2,1)}, bf16[256,2560]{1,0:T(8,128)(2,1)S(1)}, u32[]{:S(2)}, u32[]{:S(2)}) %collective-permute-start.1) | collective-permute-done | bytes 1310752 | tf_op jit(solution)/shard_map/ppermute | solution.py:263
  97.4 12.7 copy.24
  110.1 3.4 slice.254
  118.7 4.3 collective-permute-done.38.refs_2_
  127.2 21.5 %collective-permute-done.7.refs_8_.refs_2_ = bf16[1280,896]{1,0:T(8,128)(2,1)} collective-permute-done((bf16[1280,896]{1,0:T(8,128)(2,1)}, bf16[1280,896]{1,0:T(8,128)(2,1)}, u32[]{:S(2)}, u32[]{:S(2)}) %collective-permute-start.7) | collective-permute-done | bytes 2293792 | tf_op jit(solution)/shard_map/ppermute | solution.py:263
  150.3 5.1 fusion.2
  155.3 42.6 %collective-permute-done.54.refs_8_ = bf16[1280,896]{1,0:T(8,128)(2,1)} collective-permute-done((bf16[1280,896]{1,0:T(8,128)(2,1)}, bf16[1280,896]{1,0:T(8,128)(2,1)}, u32[]{:S(2)}, u32[]{:S(2)}) %collective-permute-start.54) | collective-permute-done | bytes 2293792 | tf_op jit(solution)/shard_map/ppermute | solution.py:263
  199.5 3.2 fusion.1
  202.7 19.4 %collective-permute-done.48.refs_3_ = bf16[256,2560]{1,0:T(8,128)(2,1)S(1)} collective-permute-done((bf16[256,2560]{1,0:T(8,128)(2,1)}, bf16[256,2560]{1,0:T(8,128)(2,1)S(1)}, u32[]{:S(2)}, u32[]{:S(2)}) %collective-permute-start.48) | collective-permute-done | bytes 1310752 | tf_op jit(solution)/shard_map/ppermute | solution.py:263
  223.6 30.4 %collective-permute-done.40 = bf16[256,5120]{1,0:T(8,128)(2,1)S(1)} collective-permute-done((bf16[256,5120]{1,0:T(8,128)(2,1)}, bf16[256,5120]{1,0:T(8,128)(2,1)S(1)}, u32[]{:S(2)}, u32[]{:S(2)}) %collective-permute-start.40) | collective-permute-done | bytes 2621472 | tf_op jit(solution)/shard_map/ppermute | solution.py:263
  255.5 54.7 %collective-permute-done.3 = bf16[256,5120]{1,0:T(8,128)(2,1)S(1)} collective-permute-done((bf16[256,5120]{1,0:T(8,128)(2,1)}, bf16[256,5120]{1,0:T(8,128)(2,1)S(1)}, u32[]{:S(2)}, u32[]{:S(2)}) %collective-permute-start.3) | collective-permute-done | bytes 2621472 | tf_op jit(solution)/shard_map/ppermute | solution.py:263
  311.7 6.1 fusion
  317.8 16.3 %collective-permute-done.13.refs_3_ = bf16[256,2560]{1,0:T(8,128)(2,1)S(1)} collective-permute-done((bf16[256,2560]{1,0:T(8,128)(2,1)S(1)}, bf16[256,2560]{1,0:T(8,128)(2,1)S(1)}, u32[]{:S(2)}, u32[]{:S(2)}) %collective-permute-start.13) | collective-permute-done | bytes 1310752 | tf_op jit(solution)/shard_map/ppermute | solution.py:263
  336.7 25.7 %collective-permute-done.2.refs_3_ = bf16[256,2560]{1,0:T(8,128)(2,1)S(1)} collective-permute-done((bf16[256,2560]{1,0:T(8,128)(2,1)S(1)}, bf16[256,2560]{1,0:T(8,128)(2,1)S(1)}, u32[]{:S(2)}, u32[]{:S(2)}) %collective-permute-start.2) | collective-permute-done | bytes 1310752 | tf_op jit(solution)/shard_map/ppermute | solution.py:263
  365.3 15.2 collective-permute-done.23.refs_8_.refs_1_
  382.3 65.0 %collective-permute-done.25.refs_10_.refs_4_ = bf16[1280,1280]{1,0:T(8,128)(2,1)} collective-permute-done((bf16[1280,1280]{1,0:T(8,128)(2,1)}, bf16[1280,1280]{1,0:T(8,128)(2,1)}, u32[]{:S(2)}, u32[]{:S(2)}) %collective-permute-start.25) | collective-permute-done | bytes 3276832 | tf_op jit(solution)/shard_map/ppermute | solution.py:263
  453.4 25.5 %collective-permute-done.5.refs_6_ = bf16[256,2560]{1,0:T(8,128)(2,1)S(1)} collective-permute-done((bf16[256,2560]{1,0:T(8,128)(2,1)S(1)}, bf16[256,2560]{1,0:T(8,128)(2,1)S(1)}, u32[]{:S(2)}, u32[]{:S(2)}) %collective-permute-start.5) | collective-permute-done | bytes 1310752 | tf_op jit(solution)/shard_map/ppermute | solution.py:263
  480.9 21.9 %collective-permute-done.16.refs_7_ = bf16[256,2560]{1,0:T(8,128)(2,1)S(1)} collective-permute-done((bf16[256,2560]{1,0:T(8,128)(2,1)S(1)}, bf16[256,2560]{1,0:T(8,128)(2,1)S(1)}, u32[]{:S(2)}, u32[]{:S(2)}) %collective-permute-start.16) | collective-permute-done | bytes 1310752 | tf_op jit(solution)/shard_map/ppermute | solution.py:263
  505.1 7.9 copy.26
  515.0 35.1 %shard_map.96 = (f32[2048,1280]{1,0:T(8,128)}, f32[2048,1280]{1,0:T(8,128)}) custom-call(bf16[256,2560]{1,0:T(8,128)(2,1)} %copy-done.34, bf16[256,2560]{1,0:T(8,128)(2,1)} %copy-done.35, bf16[256,2560]{1,0:T(8,128)(2,1)} %copy-done.37, bf16[256,2560]{1,0:T(8,128)(2,1)} %copy-done.39, bf16[256,2560]{1,0:T(8,128)(2,1)} %copy-done.28, ...), custom_call_target="tpu_custom_call" | custom-call | flops 26843545600 | bytes 80000000 | tf_op jit(solution)/shard_map/pallas_call | solution.py:102
  552.2 38.0 %shard_map.97 = (f32[2048,1280]{1,0:T(8,128)}, f32[2048,1280]{1,0:T(8,128)}, bf16[1280,2048]{1,0:T(8,128)(2,1)}) custom-call(bf16[256,2560]{1,0:T(8,128)(2,1)} %pad_maximum_fusion.2.refs_0_, bf16[256,2560]{1,0:T(8,128)(2,1)} %collective-permute-done.refs_1_, bf16[256,2560]{1,0:T(8,128)(2,1)} %copy-done.49, ...), custom_call_target="tpu_custom_call", output_to_operand_aliasing={{0}: (12, {}), {1}: (13, {})} | custom-call | flops 26843545600 | bytes 80000000 | tf_op jit(solution)/shard_map/pallas_call | solution.py:102
  592.0 29.1 %shard_map.92 = (f32[2048,896]{1,0:T(8,128)}, f32[2048,896]{1,0:T(8,128)}) custom-call(bf16[256,2560]{1,0:T(8,128)(2,1)} %copy-done.34, bf16[256,2560]{1,0:T(8,128)(2,1)} %copy-done.35, bf16[256,2560]{1,0:T(8,128)(2,1)} %copy-done.37, bf16[256,2560]{1,0:T(8,128)(2,1)} %copy-done.39, bf16[256,2560]{1,0:T(8,128)(2,1)} %copy-done.28, ...), custom_call_target="tpu_custom_call" | custom-call | flops 18790481920 | bytes 80000000 | tf_op jit(solution)/shard_map/pallas_call | solution.py:102
  625.0 31.8 %shard_map.93 = (f32[2048,896]{1,0:T(8,128)}, f32[2048,896]{1,0:T(8,128)}, bf16[896,2048]{1,0:T(8,128)(2,1)}) custom-call(bf16[256,2560]{1,0:T(8,128)(2,1)} %pad_maximum_fusion.2.refs_0_, bf16[256,2560]{1,0:T(8,128)(2,1)} %collective-permute-done.refs_1_, bf16[256,2560]{1,0:T(8,128)(2,1)} %copy-done.49, ...), custom_call_target="tpu_custom_call", output_to_operand_aliasing={{0}: (12, {}), {1}: (13, {})} | custom-call | flops 18790481920 | bytes 80000000 | tf_op jit(solution)/shard_map/pallas_call | solution.py:102
  658.4 49.2 %collective-permute-done.51.refs_7_ = bf16[256,2560]{1,0:T(8,128)(2,1)} collective-permute-done((bf16[256,2560]{1,0:T(8,128)(2,1)}, bf16[256,2560]{1,0:T(8,128)(2,1)}, u32[]{:S(2)}, u32[]{:S(2)}) %collective-permute-start.51) | collective-permute-done | bytes 1310752 | tf_op jit(solution)/shard_map/ppermute | solution.py:263
  708.8 21.0 %shard_map.100.refs_10_ = f32[2048,1280]{1,0:T(8,128)} custom-call(bf16[256,2560]{1,0:T(8,128)(2,1)} %copy-done.27, bf16[256,2560]{1,0:T(8,128)(2,1)} %collective-permute-done.46.refs_1_, bf16[256,2560]{1,0:T(8,128)(2,1)} %copy-done.23, bf16[256,2560]{1,0:T(8,128)(2,1)} %copy-done.25, bf16[256,2560]{1,0:T(8,128)(2,1)} %copy-done.22, ...), custom_call_target="tpu_custom_call" | custom-call | flops 13421772800 | bytes 80000000 | tf_op jit(solution)/shard_map/pallas_call | solution.py:102
  731.9 17.6 %shard_map.102.refs_10_ = f32[2048,896]{1,0:T(8,128)} custom-call(bf16[256,2560]{1,0:T(8,128)(2,1)} %copy-done.27, bf16[256,2560]{1,0:T(8,128)(2,1)} %collective-permute-done.46.refs_1_, bf16[256,2560]{1,0:T(8,128)(2,1)} %copy-done.23, bf16[256,2560]{1,0:T(8,128)(2,1)} %copy-done.25, bf16[256,2560]{1,0:T(8,128)(2,1)} %copy-done.22, ...), custom_call_target="tpu_custom_call" | custom-call | flops 9395240960 | bytes 80000000 | tf_op jit(solution)/shard_map/pallas_call | solution.py:102
  749.4 21.0 %shard_map.98.refs_10_ = f32[2048,1280]{1,0:T(8,128)} custom-call(bf16[256,2560]{1,0:T(8,128)(2,1)} %copy-done.27, bf16[256,2560]{1,0:T(8,128)(2,1)} %collective-permute-done.46.refs_1_, bf16[256,2560]{1,0:T(8,128)(2,1)} %copy-done.23, bf16[256,2560]{1,0:T(8,128)(2,1)} %copy-done.25, bf16[256,2560]{1,0:T(8,128)(2,1)} %copy-done.22, ...), custom_call_target="tpu_custom_call" | custom-call | flops 13421772800 | bytes 80000000 | tf_op jit(solution)/shard_map/pallas_call | solution.py:102
  770.5 33.5 %collective-permute-done.44.refs_8_ = bf16[1280,1280]{1,0:T(8,128)(2,1)} collective-permute-done((bf16[1280,1280]{1,0:T(8,128)(2,1)}, bf16[1280,1280]{1,0:T(8,128)(2,1)}, u32[]{:S(2)}, u32[]{:S(2)}) %collective-permute-start.44) | collective-permute-done | bytes 3276832 | tf_op jit(solution)/shard_map/ppermute | solution.py:263
  805.0 30.2 %shard_map.101 = (bf16[2048,1280]{1,0:T(8,128)(2,1)}, bf16[2048,1280]{1,0:T(8,128)(2,1)}, bf16[1280,1024]{1,0:T(8,128)(2,1)}, bf16[1280,1024]{1,0:T(8,128)(2,1)}) custom-call(bf16[256,2560]{1,0:T(8,128)(2,1)} %pad_maximum_fusion.4.refs_0_, bf16[256,2560]{1,0:T(8,128)(2,1)} %collective-permute-done.37.refs_1_, ...), custom_call_target="tpu_custom_call" | custom-call | flops 13421772800 | bytes 80000000 | tf_op jit(solution)/shard_map/pallas_call | solution.py:102
  835.2 35.2 %shard_map.94 = (f32[2048,1280]{1,0:T(8,128)}, f32[2048,1280]{1,0:T(8,128)}) custom-call(bf16[256,2560]{1,0:T(8,128)(2,1)} %copy-done.34, bf16[256,2560]{1,0:T(8,128)(2,1)} %copy-done.35, bf16[256,2560]{1,0:T(8,128)(2,1)} %copy-done.37, bf16[256,2560]{1,0:T(8,128)(2,1)} %copy-done.39, bf16[256,2560]{1,0:T(8,128)(2,1)} %copy-done.28, ...), custom_call_target="tpu_custom_call" | custom-call | flops 26843545600 | bytes 80000000 | tf_op jit(solution)/shard_map/pallas_call | solution.py:102
  870.4 24.6 %shard_map.103 = (bf16[2048,896]{1,0:T(8,128)(2,1)}, bf16[2048,896]{1,0:T(8,128)(2,1)}, bf16[896,1024]{1,0:T(8,128)(2,1)}, bf16[896,1024]{1,0:T(8,128)(2,1)}) custom-call(bf16[256,2560]{1,0:T(8,128)(2,1)} %pad_maximum_fusion.4.refs_0_, bf16[256,2560]{1,0:T(8,128)(2,1)} %collective-permute-done.37.refs_1_, bf16[256,2560]{1,0:T(8,128)(2,1)} %collective-permute-done.38.refs_2_, ...), custom_call_target="tpu_custom_call" | custom-call | flops 9395240960 | bytes 80000000 | tf_op jit(solution)/shard_map/pallas_call | solution.py:102
  895.0 38.1 %shard_map.95 = (f32[2048,1280]{1,0:T(8,128)}, f32[2048,1280]{1,0:T(8,128)}, bf16[1280,2048]{1,0:T(8,128)(2,1)}) custom-call(bf16[256,2560]{1,0:T(8,128)(2,1)} %pad_maximum_fusion.2.refs_0_, bf16[256,2560]{1,0:T(8,128)(2,1)} %collective-permute-done.refs_1_, bf16[256,2560]{1,0:T(8,128)(2,1)} %copy-done.49, ...), custom_call_target="tpu_custom_call", output_to_operand_aliasing={{0}: (12, {}), {1}: (13, {})} | custom-call | flops 26843545600 | bytes 80000000 | tf_op jit(solution)/shard_map/pallas_call | solution.py:102
  933.1 30.3 %shard_map.99 = (bf16[2048,1280]{1,0:T(8,128)(2,1)}, bf16[2048,1280]{1,0:T(8,128)(2,1)}, bf16[1280,1024]{1,0:T(8,128)(2,1)}, bf16[1280,1024]{1,0:T(8,128)(2,1)}) custom-call(bf16[256,2560]{1,0:T(8,128)(2,1)} %pad_maximum_fusion.4.refs_0_, bf16[256,2560]{1,0:T(8,128)(2,1)} %collective-permute-done.37.refs_1_, ...), custom_call_target="tpu_custom_call" | custom-call | flops 13421772800 | bytes 80000000 | tf_op jit(solution)/shard_map/pallas_call | solution.py:102
  963.4 27.5 %partial_sums.15 = (f32[1280,512]{1,0:T(8,128)}, f32[1280,512]{1,0:T(8,128)}) custom-call(bf16[1280,1280]{1,0:T(8,128)(2,1)} %collective-permute-done.20.refs_9_.refs_0_, bf16[1280,1280]{1,0:T(8,128)(2,1)} %collective-permute-done.24.refs_9_.refs_1_, bf16[1280,896]{1,0:T(8,128)(2,1)} %collective-permute-done.8.refs_9_.refs_2_, ...), custom_call_target="tpu_custom_call" | custom-call | flops 18119393280 | bytes 30000000 | tf_op jit(solution)/shard_map/partial_sums/pallas_call | solution.py:161
  992.5 27.5 %partial_sums.14 = (f32[1280,512]{1,0:T(8,128)}, f32[1280,512]{1,0:T(8,128)}) custom-call(bf16[1280,1280]{1,0:T(8,128)(2,1)} %collective-permute-done.19.refs_8_.refs_0_, bf16[1280,1280]{1,0:T(8,128)(2,1)} %collective-permute-done.23.refs_8_.refs_1_, bf16[1280,896]{1,0:T(8,128)(2,1)} %collective-permute-done.7.refs_8_.refs_2_, ...), custom_call_target="tpu_custom_call" | custom-call | flops 18119393280 | bytes 30000000 | tf_op jit(solution)/shard_map/partial_sums/pallas_call | solution.py:161
  1020.5 26.8 %partial_sums.13 = (f32[1280,512]{1,0:T(8,128)}, f32[1280,512]{1,0:T(8,128)}) custom-call(bf16[1280,3456]{1,0:T(8,128)(2,1)} %collective-permute-done.17.refs_9_.refs_0_, bf16[1280,3456]{1,0:T(8,128)(2,1)} %collective-permute-done.18.refs_11_.refs_1_, bf16[1280,1024]{1,0:T(8,128)(2,1)} %get-tuple-element.83.refs_2_.refs_6_, ...), custom_call_target="tpu_custom_call" | custom-call | flops 18119393280 | bytes 30000000 | tf_op jit(solution)/shard_map/partial_sums/pallas_call | solution.py:161
  1047.7 26.9 %partial_sums.12 = (f32[1280,512]{1,0:T(8,128)}, f32[1280,512]{1,0:T(8,128)}) custom-call(bf16[1280,3456]{1,0:T(8,128)(2,1)} %refs_0_.4, bf16[1280,3456]{1,0:T(8,128)(2,1)} %refs_1_.1, bf16[1280,1024]{1,0:T(8,128)(2,1)} %get-tuple-element.83.refs_2_.refs_6_, bf16[1280,1024]{1,0:T(8,128)(2,1)} %get-tuple-element.86.refs_3_.refs_7_, ...), custom_call_target="tpu_custom_call" | custom-call | flops 18119393280 | bytes 30000000 | tf_op jit(solution)/shard_map/partial_sums/pallas_call | solution.py:161
  1076.1 20.2 %partial_sums.10 = (f32[1280,512]{1,0:T(8,128)}, f32[1280,512]{1,0:T(8,128)}, f32[1280,512]{1,0:T(8,128)}, f32[1280,512]{1,0:T(8,128)}) custom-call(bf16[1280,3456]{1,0:T(8,128)(2,1)} %collective-permute-done.29.refs_0_.refs_9_, bf16[1280,2048]{1,0:T(8,128)(2,1)} %get-tuple-element.61.refs_1_.refs_2_, bf16[1280,2048]{1,0:T(8,128)(2,1)} %get-tuple-element.64.refs_2_.refs_4_), custom_call_target="tpu_custom_call" | custom-call | flops 13421772800 | bytes 30000000 | tf_op jit(solution)/shard_map/partial_sums/pallas_call | solution.py:161
  1096.3 15.1 partial_sums.11
  1113.1 19.9 %partial_sums.8 = (f32[1280,512]{1,0:T(8,128)}, f32[1280,512]{1,0:T(8,128)}, f32[1280,512]{1,0:T(8,128)}, f32[1280,512]{1,0:T(8,128)}) custom-call(bf16[1280,3456]{1,0:T(8,128)(2,1)} %bitcast.refs_0_.refs_8_, bf16[1280,2048]{1,0:T(8,128)(2,1)} %get-tuple-element.61.refs_1_.refs_2_, bf16[1280,2048]{1,0:T(8,128)(2,1)} %get-tuple-element.64.refs_2_.refs_4_), custom_call_target="tpu_custom_call" | custom-call | flops 13421772800 | bytes 30000000 | tf_op jit(solution)/shard_map/partial_sums/pallas_call | solution.py:161
  1133.0 14.8 partial_sums.9
  1156.2 15.3 collective-permute-done.34.refs_5_
  1173.6 34.2 %collective-permute-done.32.refs_2_ = f32[1280,512]{1,0:T(8,128)S(1)} collective-permute-done((f32[1280,512]{1,0:T(8,128)}, f32[1280,512]{1,0:T(8,128)S(1)}, u32[]{:S(2)}, u32[]{:S(2)}) %collective-permute-start.32) | collective-permute-done | bytes 2621472 | tf_op jit(solution)/shard_map/ppermute | solution.py:263
  1208.7 18.9 %collective-permute-done.30.refs_5_ = f32[1280,512]{1,0:T(8,128)S(1)} collective-permute-done((f32[1280,512]{1,0:T(8,128)}, f32[1280,512]{1,0:T(8,128)S(1)}, u32[]{:S(2)}, u32[]{:S(2)}) %collective-permute-start.30) | collective-permute-done | bytes 2621472 | tf_op jit(solution)/shard_map/ppermute | solution.py:263
  1228.1 35.9 %collective-permute-done.27.refs_2_ = f32[1280,512]{1,0:T(8,128)S(1)} collective-permute-done((f32[1280,512]{1,0:T(8,128)}, f32[1280,512]{1,0:T(8,128)S(1)}, u32[]{:S(2)}, u32[]{:S(2)}) %collective-permute-start.27) | collective-permute-done | bytes 2621472 | tf_op jit(solution)/shard_map/ppermute | solution.py:263
  1267.4 24.7 %collective-permute-done.63.refs_12_ = f32[1280,256]{1,0:T(8,128)S(1)} collective-permute-done((f32[1280,256]{1,0:T(8,128)S(1)}, f32[1280,256]{1,0:T(8,128)S(1)}, u32[]{:S(2)}, u32[]{:S(2)}) %collective-permute-start.63) | collective-permute-done | bytes 1310752 | tf_op jit(solution)/shard_map/ppermute | solution.py:263
  1293.4 26.8 %collective-permute-done.59.refs_6_ = f32[1280,256]{1,0:T(8,128)S(1)} collective-permute-done((f32[1280,256]{1,0:T(8,128)S(1)}, f32[1280,256]{1,0:T(8,128)S(1)}, u32[]{:S(2)}, u32[]{:S(2)}) %collective-permute-start.59) | collective-permute-done | bytes 1310752 | tf_op jit(solution)/shard_map/ppermute | solution.py:263
  1320.7 26.8 %collective-permute-done.35.refs_6_ = f32[1280,256]{1,0:T(8,128)S(1)} collective-permute-done((f32[1280,256]{1,0:T(8,128)S(1)}, f32[1280,256]{1,0:T(8,128)S(1)}, u32[]{:S(2)}, u32[]{:S(2)}) %collective-permute-start.35) | collective-permute-done | bytes 1310752 | tf_op jit(solution)/shard_map/ppermute | solution.py:263
  1351.7 5.5 finish.3
  1357.2 20.2 %collective-permute-done.31.refs_6_ = f32[1280,256]{1,0:T(8,128)S(1)} collective-permute-done((f32[1280,256]{1,0:T(8,128)S(1)}, f32[1280,256]{1,0:T(8,128)S(1)}, u32[]{:S(2)}, u32[]{:S(2)}) %collective-permute-start.31) | collective-permute-done | bytes 1310752 | tf_op jit(solution)/shard_map/ppermute | solution.py:263
  1377.5 3.0 collective-permute-done.28.refs_3_
  1386.4 23.2 %collective-permute-done.36.refs_7_ = bf16[256,2560]{1,0:T(8,128)(2,1)S(1)} collective-permute-done((bf16[256,2560]{1,0:T(8,128)(2,1)}, bf16[256,2560]{1,0:T(8,128)(2,1)S(1)}, u32[]{:S(2)}, u32[]{:S(2)}) %collective-permute-start.36) | collective-permute-done | bytes 1310752 | tf_op jit(solution)/shard_map/ppermute | solution.py:263
  1415.7 7.9 copy.25
  1426.0 9.4 finish.5
  1435.4 6.9 finish.4
  1443.4 48.9 %weight_grad.4 = f32[1280,3456]{1,0:T(8,128)} custom-call(bf16[1280,2048]{1,0:T(8,128)(2,1)} %bitcast.6, bf16[1280,2048]{1,0:T(8,128)(2,1)} %collective-permute-done.64.refs_1_, bf16[2048,1280]{1,0:T(8,128)(2,1)} %get-tuple-element.104.refs_2_, bf16[2048,1280]{1,0:T(8,128)(2,1)} %collective-permute-done.68.refs_3_, ...), custom_call_target="tpu_custom_call" | custom-call | flops 37580963840 | bytes 50000000 | tf_op jit(solution)/shard_map/weight_grad/pallas_call | solution.py:209
  1492.3 49.0 %weight_grad.3 = f32[1280,3456]{1,0:T(8,128)} custom-call(bf16[1280,2048]{1,0:T(8,128)(2,1)} %bitcast.7, bf16[1280,2048]{1,0:T(8,128)(2,1)} %collective-permute-done.64.refs_1_, bf16[2048,1280]{1,0:T(8,128)(2,1)} %get-tuple-element.101.refs_2_, bf16[2048,1280]{1,0:T(8,128)(2,1)} %collective-permute-done.65.refs_3_, ...), custom_call_target="tpu_custom_call" | custom-call | flops 37580963840 | bytes 50000000 | tf_op jit(solution)/shard_map/weight_grad/pallas_call | solution.py:209
  1541.4 48.7 %weight_grad.5 = f32[3456,1280]{1,0:T(8,128)} custom-call(bf16[2048,1280]{1,0:T(8,128)(2,1)} %get-tuple-element.138.refs_0_, bf16[2048,1280]{1,0:T(8,128)(2,1)} %collective-permute-done.71.refs_1_, bf16[1280,2048]{1,0:T(8,128)(2,1)} %get-tuple-element.61.refs_1_.refs_2_, bf16[1280,2048]{1,0:T(8,128)(2,1)} %collective-permute-done.72.refs_3_, ...), custom_call_target="tpu_custom_call" | custom-call | flops 37580963840 | bytes 50000000 | tf_op jit(solution)/shard_map/weight_grad/pallas_call | solution.py:209
  (267 shorter events, 107.5 us)
Async XLA Ops:
  8.4 38.2 %collective-permute-start.47 = (bf16[256,2560]{1,0:T(8,128)(2,1)S(1)}, bf16[256,2560]{1,0:T(8,128)(2,1)S(1)}, u32[]{:S(2)}, u32[]{:S(2)}) collective-permute-start(bf16[256,2560]{1,0:T(8,128)(2,1)S(1)} %pad_maximum_fusion.5.refs_0_), channel_id=1, source_target_pairs={{0,8},{4,12},{8,0},{12,4},{1,9},{5,13},{9,1},{13,5},{2,10},{6,14},... | collective-permute-start | bytes 3932168 | tf_op jit(solution)/shard_map/ppermute | solution.py:263
  10.1 56.0 %collective-permute-start.11 = (bf16[256,2560]{1,0:T(8,128)(2,1)S(1)}, bf16[256,2560]{1,0:T(8,128)(2,1)S(1)}, u32[]{:S(2)}, u32[]{:S(2)}) collective-permute-start(bf16[256,2560]{1,0:T(8,128)(2,1)S(1)} %pad_maximum_fusion.3.refs_0_), channel_id=1, source_target_pairs={{0,4},{4,0},{8,12},{12,8},{1,5},{5,1},{9,13},{13,9},{2,6},{6,2},{1... | collective-permute-start | bytes 3932168 | tf_op jit(solution)/shard_map/ppermute | solution.py:263
  10.6 58.7 %collective-permute-start.12 = (bf16[256,2560]{1,0:T(8,128)(2,1)S(1)}, bf16[256,2560]{1,0:T(8,128)(2,1)S(1)}, u32[]{:S(2)}, u32[]{:S(2)}) collective-permute-start(bf16[256,2560]{1,0:T(8,128)(2,1)S(1)} %pad_maximum_fusion.3.refs_0_), channel_id=1, source_target_pairs={{0,8},{4,12},{8,0},{12,4},{1,9},{5,13},{9,1},{13,5},{2,10},{6,14},... | collective-permute-start | bytes 3932168 | tf_op jit(solution)/shard_map/ppermute | solution.py:263
  12.3 84.0 %collective-permute-start.1 = (bf16[256,2560]{1,0:T(8,128)(2,1)}, bf16[256,2560]{1,0:T(8,128)(2,1)S(1)}, u32[]{:S(2)}, u32[]{:S(2)}) collective-permute-start(bf16[256,2560]{1,0:T(8,128)(2,1)} %pad_maximum_fusion.2.refs_0_), channel_id=1, source_target_pairs={{0,8},{4,12},{8,0},{12,4},{1,9},{5,13},{9,1},{13,5},{2,10},{6,14},... | collective-permute-start | bytes 3932168 | tf_op jit(solution)/shard_map/ppermute | solution.py:263
  38.1 75.4 %collective-permute-start = (bf16[256,2560]{1,0:T(8,128)(2,1)}, bf16[256,2560]{1,0:T(8,128)(2,1)}, u32[]{:S(2)}, u32[]{:S(2)}) collective-permute-start(bf16[256,2560]{1,0:T(8,128)(2,1)} %pad_maximum_fusion.2.refs_0_), channel_id=1, source_target_pairs={{0,4},{4,0},{8,12},{12,8},{1,5},{5,1},{9,13},{13,9},{2,6},{6,2},{1... | collective-permute-start | bytes 3932168 | tf_op jit(solution)/shard_map/ppermute | solution.py:263
  46.6 79.2 %collective-permute-start.9 = (bf16[1280,896]{1,0:T(8,128)(2,1)}, bf16[1280,896]{1,0:T(8,128)(2,1)}, u32[]{:S(2)}, u32[]{:S(2)}) collective-permute-start(bf16[1280,896]{1,0:T(8,128)(2,1)} %slice.189), channel_id=1, source_target_pairs={{0,2},{1,3},{2,0},{3,1},{4,6},{5,7},{6,4},{7,5},{8,10},{9,11},{10,... | collective-permute-start | bytes 6881288 | tf_op jit(solution)/shard_map/ppermute | solution.py:263
  66.1 82.7 %collective-permute-start.7 = (bf16[1280,896]{1,0:T(8,128)(2,1)}, bf16[1280,896]{1,0:T(8,128)(2,1)}, u32[]{:S(2)}, u32[]{:S(2)}) collective-permute-start(bf16[1280,896]{1,0:T(8,128)(2,1)} %slice.188), channel_id=1, source_target_pairs={{0,2},{1,3},{2,0},{3,1},{4,6},{5,7},{6,4},{7,5},{8,10},{9,11},{10,... | collective-permute-start | bytes 6881288 | tf_op jit(solution)/shard_map/ppermute | solution.py:263
  69.3 53.7 %collective-permute-start.38 = (bf16[256,2560]{1,0:T(8,128)(2,1)}, bf16[256,2560]{1,0:T(8,128)(2,1)}, u32[]{:S(2)}, u32[]{:S(2)}) collective-permute-start(bf16[256,2560]{1,0:T(8,128)(2,1)} %pad_maximum_fusion.4.refs_0_), channel_id=1, source_target_pairs={{0,8},{4,12},{8,0},{12,4},{1,9},{5,13},{9,1},{13,5},{2,10},{6,14},... | collective-permute-start | bytes 3932168 | tf_op jit(solution)/shard_map/ppermute | solution.py:263
  113.5 84.4 %collective-permute-start.54 = (bf16[1280,896]{1,0:T(8,128)(2,1)}, bf16[1280,896]{1,0:T(8,128)(2,1)}, u32[]{:S(2)}, u32[]{:S(2)}) collective-permute-start(bf16[1280,896]{1,0:T(8,128)(2,1)} %slice.254), channel_id=1, source_target_pairs={{0,2},{1,3},{2,0},{3,1},{4,6},{5,7},{6,4},{7,5},{8,10},{9,11},{10,... | collective-permute-start | bytes 6881288 | tf_op jit(solution)/shard_map/ppermute | solution.py:263
  123.0 390.0 %collective-permute-start.17 = (bf16[1280,3456]{1,0:T(8,128)(2,1)}, bf16[1280,3456]{1,0:T(8,128)(2,1)}, u32[]{:S(2)}, u32[]{:S(2)}) collective-permute-start(bf16[1280,3456]{1,0:T(8,128)(2,1)} %refs_0_.4), channel_id=1, source_target_pairs={{0,1},{1,0},{2,3},{3,2},{4,5},{5,4},{6,7},{7,6},{8,9},{9,8},{10,11... | collective-permute-start | bytes 26542088 | tf_op jit(solution)/shard_map/ppermute | solution.py:263
  125.7 388.7 %collective-permute-start.18 = (bf16[1280,3456]{1,0:T(8,128)(2,1)}, bf16[1280,3456]{1,0:T(8,128)(2,1)}, u32[]{:S(2)}, u32[]{:S(2)}) collective-permute-start(bf16[1280,3456]{1,0:T(8,128)(2,1)} %refs_1_.1), channel_id=1, source_target_pairs={{0,1},{1,0},{2,3},{3,2},{4,5},{5,4},{6,7},{7,6},{8,9},{9,8},{10,11... | collective-permute-start | bytes 26542088 | tf_op jit(solution)/shard_map/ppermute | solution.py:263
  125.7 128.2 %collective-permute-start.40 = (bf16[256,5120]{1,0:T(8,128)(2,1)}, bf16[256,5120]{1,0:T(8,128)(2,1)S(1)}, u32[]{:S(2)}, u32[]{:S(2)}) collective-permute-start(bf16[256,5120]{1,0:T(8,128)(2,1)} %pad_maximum_fusion.1), channel_id=1, source_target_pairs={{0,2},{1,3},{2,0},{3,1},{4,6},{5,7},{6,4},{7,5},{8,10},{9,11},{10,... | collective-permute-start | bytes 7864328 | tf_op jit(solution)/shard_map/ppermute | solution.py:263
  148.8 161.4 %collective-permute-start.3 = (bf16[256,5120]{1,0:T(8,128)(2,1)}, bf16[256,5120]{1,0:T(8,128)(2,1)S(1)}, u32[]{:S(2)}, u32[]{:S(2)}) collective-permute-start(bf16[256,5120]{1,0:T(8,128)(2,1)} %pad_maximum_fusion), channel_id=1, source_target_pairs={{0,2},{1,3},{2,0},{3,1},{4,6},{5,7},{6,4},{7,5},{8,10},{9,11},{10,... | collective-permute-start | bytes 7864328 | tf_op jit(solution)/shard_map/ppermute | solution.py:263
  222.1 158.4 %collective-permute-start.23 = (bf16[1280,1280]{1,0:T(8,128)(2,1)S(1)}, bf16[1280,1280]{1,0:T(8,128)(2,1)}, u32[]{:S(2)}, u32[]{:S(2)}) collective-permute-start(bf16[1280,1280]{1,0:T(8,128)(2,1)S(1)} %get-tuple-element.119), channel_id=1, source_target_pairs={{0,2},{1,3},{2,0},{3,1},{4,6},{5,7},{6,4},{7,5},{8,10},{9,11},{10,... | collective-permute-start | bytes 9830408 | tf_op jit(solution)/shard_map/ppermute | solution.py:263
  254.0 193.3 %collective-permute-start.25 = (bf16[1280,1280]{1,0:T(8,128)(2,1)}, bf16[1280,1280]{1,0:T(8,128)(2,1)}, u32[]{:S(2)}, u32[]{:S(2)}) collective-permute-start(bf16[1280,1280]{1,0:T(8,128)(2,1)} %get-tuple-element.117), channel_id=1, source_target_pairs={{0,2},{1,3},{2,0},{3,1},{4,6},{5,7},{6,4},{7,5},{8,10},{9,11},{10,... | collective-permute-start | bytes 9830408 | tf_op jit(solution)/shard_map/ppermute | solution.py:263
  362.4 86.5 %collective-permute-start.14 = (bf16[256,2560]{1,0:T(8,128)(2,1)S(1)}, bf16[256,2560]{1,0:T(8,128)(2,1)S(1)}, u32[]{:S(2)}, u32[]{:S(2)}) collective-permute-start(bf16[256,2560]{1,0:T(8,128)(2,1)S(1)} %get-tuple-element.131.refs_4_.refs_0_), channel_id=1, source_target_pairs={{0,4},{4,0},{8,12},{12,8},{1,5},{5,1},{9,13},{13,9},{2,6},{6,2},{1... | collective-permute-start | bytes 3932168 | tf_op jit(solution)/shard_map/ppermute | solution.py:263
  380.5 70.1 %collective-permute-start.15 = (bf16[256,2560]{1,0:T(8,128)(2,1)S(1)}, bf16[256,2560]{1,0:T(8,128)(2,1)S(1)}, u32[]{:S(2)}, u32[]{:S(2)}) collective-permute-start(bf16[256,2560]{1,0:T(8,128)(2,1)S(1)} %get-tuple-element.131.refs_4_.refs_0_), channel_id=1, source_target_pairs={{0,8},{4,12},{8,0},{12,4},{1,9},{5,13},{9,1},{13,5},{2,10},{6,14},... | collective-permute-start | bytes 3932168 | tf_op jit(solution)/shard_map/ppermute | solution.py:263
  450.6 52.2 %collective-permute-start.16 = (bf16[256,2560]{1,0:T(8,128)(2,1)S(1)}, bf16[256,2560]{1,0:T(8,128)(2,1)S(1)}, u32[]{:S(2)}, u32[]{:S(2)}) collective-permute-start(bf16[256,2560]{1,0:T(8,128)(2,1)S(1)} %collective-permute-done.14.refs_5_), channel_id=1, source_target_pairs={{0,8},{4,12},{8,0},{12,4},{1,9},{5,13},{9,1},{13,5},{2,10},{6,14},... | collective-permute-start | bytes 3932168 | tf_op jit(solution)/shard_map/ppermute | solution.py:263
  479.0 72.7 %collective-permute-start.24 = (bf16[1280,1280]{1,0:T(8,128)(2,1)}, bf16[1280,1280]{1,0:T(8,128)(2,1)}, u32[]{:S(2)}, u32[]{:S(2)}) collective-permute-start(bf16[1280,1280]{1,0:T(8,128)(2,1)} %collective-permute-done.23.refs_8_.refs_1_), channel_id=1, source_target_pairs={{0,1},{1,0},{2,3},{3,2},{4,5},{5,4},{6,7},{7,6},{8,9},{9,8},{10,11... | collective-permute-start | bytes 9830408 | tf_op jit(solution)/shard_map/ppermute | solution.py:263
  479.0 72.7 %collective-permute-start.26 = (bf16[1280,1280]{1,0:T(8,128)(2,1)}, bf16[1280,1280]{1,0:T(8,128)(2,1)}, u32[]{:S(2)}, u32[]{:S(2)}) collective-permute-start(bf16[1280,1280]{1,0:T(8,128)(2,1)} %collective-permute-done.25.refs_10_.refs_4_), channel_id=1, source_target_pairs={{0,1},{1,0},{2,3},{3,2},{4,5},{5,4},{6,7},{7,6},{8,9},{9,8},{10,11... | collective-permute-start | bytes 9830408 | tf_op jit(solution)/shard_map/ppermute | solution.py:263
  502.8 206.0 %collective-permute-start.29 = (bf16[1280,3456]{1,0:T(8,128)(2,1)}, bf16[1280,3456]{1,0:T(8,128)(2,1)}, u32[]{:S(2)}, u32[]{:S(2)}) collective-permute-start(bf16[1280,3456]{1,0:T(8,128)(2,1)} %bitcast.refs_0_.refs_8_), channel_id=1, source_target_pairs={{0,1},{1,0},{2,3},{3,2},{4,5},{5,4},{6,7},{7,6},{8,9},{9,8},{10,11... | collective-permute-start | bytes 26542088 | tf_op jit(solution)/shard_map/ppermute | solution.py:263
  513.0 77.9 %collective-permute-start.52 = (bf16[1280,1280]{1,0:T(8,128)(2,1)}, bf16[1280,1280]{1,0:T(8,128)(2,1)}, u32[]{:S(2)}, u32[]{:S(2)}) collective-permute-start(bf16[1280,1280]{1,0:T(8,128)(2,1)} %get-tuple-element.115), channel_id=1, source_target_pairs={{0,2},{1,3},{2,0},{3,1},{4,6},{5,7},{6,4},{7,5},{8,10},{9,11},{10,... | collective-permute-start | bytes 9830408 | tf_op jit(solution)/shard_map/ppermute | solution.py:263
  514.5 35.7 %collective-permute-start.6 = (bf16[256,2560]{1,0:T(8,128)(2,1)}, bf16[256,2560]{1,0:T(8,128)(2,1)}, u32[]{:S(2)}, u32[]{:S(2)}) collective-permute-start(bf16[256,2560]{1,0:T(8,128)(2,1)} %copy-done.52), channel_id=1, source_target_pairs={{0,4},{4,0},{8,12},{12,8},{1,5},{5,1},{9,13},{13,9},{2,6},{6,2},{1... | collective-permute-start | bytes 3932168 | tf_op jit(solution)/shard_map/ppermute | solution.py:263
  550.1 40.1 %collective-permute-start.39 = (bf16[256,2560]{1,0:T(8,128)(2,1)}, bf16[256,2560]{1,0:T(8,128)(2,1)}, u32[]{:S(2)}, u32[]{:S(2)}) collective-permute-start(bf16[256,2560]{1,0:T(8,128)(2,1)} %collective-permute-done.38.refs_2_), channel_id=1, source_target_pairs={{0,4},{4,0},{8,12},{12,8},{1,5},{5,1},{9,13},{13,9},{2,6},{6,2},{1... | collective-permute-start | bytes 3932168 | tf_op jit(solution)/shard_map/ppermute | solution.py:263
  551.7 71.3 %collective-permute-start.10 = (bf16[1280,896]{1,0:T(8,128)(2,1)}, bf16[1280,896]{1,0:T(8,128)(2,1)}, u32[]{:S(2)}, u32[]{:S(2)}) collective-permute-start(bf16[1280,896]{1,0:T(8,128)(2,1)} %collective-permute-done.9.refs_10_.refs_5_), channel_id=1, source_target_pairs={{0,1},{1,0},{2,3},{3,2},{4,5},{5,4},{6,7},{7,6},{8,9},{9,8},{10,11... | collective-permute-start | bytes 6881288 | tf_op jit(solution)/shard_map/ppermute | solution.py:263
  551.7 71.7 %collective-permute-start.8 = (bf16[1280,896]{1,0:T(8,128)(2,1)}, bf16[1280,896]{1,0:T(8,128)(2,1)}, u32[]{:S(2)}, u32[]{:S(2)}) collective-permute-start(bf16[1280,896]{1,0:T(8,128)(2,1)} %collective-permute-done.7.refs_8_.refs_2_), channel_id=1, source_target_pairs={{0,1},{1,0},{2,3},{3,2},{4,5},{5,4},{6,7},{7,6},{8,9},{9,8},{10,11... | collective-permute-start | bytes 6881288 | tf_op jit(solution)/shard_map/ppermute | solution.py:263
  590.3 139.5 %collective-permute-start.19 = (bf16[1280,1280]{1,0:T(8,128)(2,1)}, bf16[1280,1280]{1,0:T(8,128)(2,1)}, u32[]{:S(2)}, u32[]{:S(2)}) collective-permute-start(bf16[1280,1280]{1,0:T(8,128)(2,1)} %get-tuple-element.120), channel_id=1, source_target_pairs={{0,2},{1,3},{2,0},{3,1},{4,6},{5,7},{6,4},{7,5},{8,10},{9,11},{10,... | collective-permute-start | bytes 9830408 | tf_op jit(solution)/shard_map/ppermute | solution.py:263
  621.4 35.4 %collective-permute-start.50 = (bf16[256,2560]{1,0:T(8,128)(2,1)S(1)}, bf16[256,2560]{1,0:T(8,128)(2,1)}, u32[]{:S(2)}, u32[]{:S(2)}) collective-permute-start(bf16[256,2560]{1,0:T(8,128)(2,1)S(1)} %get-tuple-element.125.refs_4_), channel_id=1, source_target_pairs={{0,8},{4,12},{8,0},{12,4},{1,9},{5,13},{9,1},{13,5},{2,10},{6,14},... | collective-permute-start | bytes 3932168 | tf_op jit(solution)/shard_map/ppermute | solution.py:263
  623.0 108.1 %collective-permute-start.42 = (bf16[256,2560]{1,0:T(8,128)(2,1)S(1)}, bf16[256,2560]{1,0:T(8,128)(2,1)}, u32[]{:S(2)}, u32[]{:S(2)}) collective-permute-start(bf16[256,2560]{1,0:T(8,128)(2,1)S(1)} %get-tuple-element.126.refs_4_), channel_id=1, source_target_pairs={{0,8},{4,12},{8,0},{12,4},{1,9},{5,13},{9,1},{13,5},{2,10},{6,14},... | collective-permute-start | bytes 3932168 | tf_op jit(solution)/shard_map/ppermute | solution.py:263
  623.4 84.2 %collective-permute-start.51 = (bf16[256,2560]{1,0:T(8,128)(2,1)}, bf16[256,2560]{1,0:T(8,128)(2,1)}, u32[]{:S(2)}, u32[]{:S(2)}) collective-permute-start(bf16[256,2560]{1,0:T(8,128)(2,1)} %collective-permute-done.49.refs_5_), channel_id=1, source_target_pairs={{0,8},{4,12},{8,0},{12,4},{1,9},{5,13},{9,1},{13,5},{2,10},{6,14},... | collective-permute-start | bytes 3932168 | tf_op jit(solution)/shard_map/ppermute | solution.py:263
  656.8 113.6 %collective-permute-start.21 = (bf16[1280,1280]{1,0:T(8,128)(2,1)}, bf16[1280,1280]{1,0:T(8,128)(2,1)}, u32[]{:S(2)}, u32[]{:S(2)}) collective-permute-start(bf16[1280,1280]{1,0:T(8,128)(2,1)} %get-tuple-element.118), channel_id=1, source_target_pairs={{0,2},{1,3},{2,0},{3,1},{4,6},{5,7},{6,4},{7,5},{8,10},{9,11},{10,... | collective-permute-start | bytes 9830408 | tf_op jit(solution)/shard_map/ppermute | solution.py:263
  707.6 96.3 %collective-permute-start.44 = (bf16[1280,1280]{1,0:T(8,128)(2,1)}, bf16[1280,1280]{1,0:T(8,128)(2,1)}, u32[]{:S(2)}, u32[]{:S(2)}) collective-permute-start(bf16[1280,1280]{1,0:T(8,128)(2,1)} %get-tuple-element.116), channel_id=1, source_target_pairs={{0,2},{1,3},{2,0},{3,1},{4,6},{5,7},{6,4},{7,5},{8,10},{9,11},{10,... | collective-permute-start | bytes 9830408 | tf_op jit(solution)/shard_map/ppermute | solution.py:263
  708.8 95.7 %collective-permute-start.53 = (bf16[1280,1280]{1,0:T(8,128)(2,1)}, bf16[1280,1280]{1,0:T(8,128)(2,1)}, u32[]{:S(2)}, u32[]{:S(2)}) collective-permute-start(bf16[1280,1280]{1,0:T(8,128)(2,1)} %collective-permute-done.52.refs_8_), channel_id=1, source_target_pairs={{0,1},{1,0},{2,3},{3,2},{4,5},{5,4},{6,7},{7,6},{8,9},{9,8},{10,11... | collective-permute-start | bytes 9830408 | tf_op jit(solution)/shard_map/ppermute | solution.py:263
  729.8 74.1 %collective-permute-start.41 = (bf16[256,2560]{1,0:T(8,128)(2,1)S(1)}, bf16[256,2560]{1,0:T(8,128)(2,1)S(1)}, u32[]{:S(2)}, u32[]{:S(2)}) collective-permute-start(bf16[256,2560]{1,0:T(8,128)(2,1)S(1)} %get-tuple-element.126.refs_4_), channel_id=1, source_target_pairs={{0,4},{4,0},{8,12},{12,8},{1,5},{5,1},{9,13},{13,9},{2,6},{6,2},{1... | collective-permute-start | bytes 3932168 | tf_op jit(solution)/shard_map/ppermute | solution.py:263
  731.1 73.4 %collective-permute-start.43 = (bf16[256,2560]{1,0:T(8,128)(2,1)}, bf16[256,2560]{1,0:T(8,128)(2,1)}, u32[]{:S(2)}, u32[]{:S(2)}) collective-permute-start(bf16[256,2560]{1,0:T(8,128)(2,1)} %collective-permute-done.42.refs_6_), channel_id=1, source_target_pairs={{0,4},{4,0},{8,12},{12,8},{1,5},{5,1},{9,13},{13,9},{2,6},{6,2},{1... | collective-permute-start | bytes 3932168 | tf_op jit(solution)/shard_map/ppermute | solution.py:263
  770.4 100.0 %collective-permute-start.55 = (bf16[1280,896]{1,0:T(8,128)(2,1)}, bf16[1280,896]{1,0:T(8,128)(2,1)}, u32[]{:S(2)}, u32[]{:S(2)}) collective-permute-start(bf16[1280,896]{1,0:T(8,128)(2,1)} %collective-permute-done.54.refs_8_), channel_id=1, source_target_pairs={{0,1},{1,0},{2,3},{3,2},{4,5},{5,4},{6,7},{7,6},{8,9},{9,8},{10,11... | collective-permute-start | bytes 6881288 | tf_op jit(solution)/shard_map/ppermute | solution.py:263
  803.9 91.1 %collective-permute-start.20 = (bf16[1280,1280]{1,0:T(8,128)(2,1)}, bf16[1280,1280]{1,0:T(8,128)(2,1)}, u32[]{:S(2)}, u32[]{:S(2)}) collective-permute-start(bf16[1280,1280]{1,0:T(8,128)(2,1)} %collective-permute-done.19.refs_8_.refs_0_), channel_id=1, source_target_pairs={{0,1},{1,0},{2,3},{3,2},{4,5},{5,4},{6,7},{7,6},{8,9},{9,8},{10,11... | collective-permute-start | bytes 9830408 | tf_op jit(solution)/shard_map/ppermute | solution.py:263
  803.9 91.1 %collective-permute-start.22 = (bf16[1280,1280]{1,0:T(8,128)(2,1)}, bf16[1280,1280]{1,0:T(8,128)(2,1)}, u32[]{:S(2)}, u32[]{:S(2)}) collective-permute-start(bf16[1280,1280]{1,0:T(8,128)(2,1)} %collective-permute-done.21.refs_10_.refs_3_), channel_id=1, source_target_pairs={{0,1},{1,0},{2,3},{3,2},{4,5},{5,4},{6,7},{7,6},{8,9},{9,8},{10,11... | collective-permute-start | bytes 9830408 | tf_op jit(solution)/shard_map/ppermute | solution.py:263
  804.4 128.7 %collective-permute-start.45 = (bf16[1280,1280]{1,0:T(8,128)(2,1)}, bf16[1280,1280]{1,0:T(8,128)(2,1)}, u32[]{:S(2)}, u32[]{:S(2)}) collective-permute-start(bf16[1280,1280]{1,0:T(8,128)(2,1)} %collective-permute-done.44.refs_8_), channel_id=1, source_target_pairs={{0,1},{1,0},{2,3},{3,2},{4,5},{5,4},{6,7},{7,6},{8,9},{9,8},{10,11... | collective-permute-start | bytes 9830408 | tf_op jit(solution)/shard_map/ppermute | solution.py:263
  804.5 306.9 %collective-permute-start.64 = (bf16[1280,2048]{1,0:T(8,128)(2,1)}, bf16[1280,2048]{1,0:T(8,128)(2,1)}, u32[]{:S(2)}, u32[]{:S(2)}) collective-permute-start(bf16[1280,2048]{1,0:T(8,128)(2,1)} %bitcast.5), channel_id=1, source_target_pairs={{0,1},{1,0},{2,3},{3,2},{4,5},{5,4},{6,7},{7,6},{8,9},{9,8},{10,11... | collective-permute-start | bytes 15728648 | tf_op jit(solution)/shard_map/ppermute | solution.py:263
  990.9 120.6 %collective-permute-start.62 = (f32[1280,512]{1,0:T(8,128)}, f32[1280,512]{1,0:T(8,128)S(1)}, u32[]{:S(2)}, u32[]{:S(2)}) collective-permute-start(f32[1280,512]{1,0:T(8,128)} %get-tuple-element.100), channel_id=1, source_target_pairs={{0,8},{4,12},{8,0},{12,4},{1,9},{5,13},{9,1},{13,5},{2,10},{6,14},... | collective-permute-start | bytes 7864328 | tf_op jit(solution)/shard_map/ppermute | solution.py:263
  1019.9 127.9 %collective-permute-start.60 = (f32[1280,512]{1,0:T(8,128)}, f32[1280,512]{1,0:T(8,128)}, u32[]{:S(2)}, u32[]{:S(2)}) collective-permute-start(f32[1280,512]{1,0:T(8,128)} %get-tuple-element.98), channel_id=1, source_target_pairs={{0,4},{4,0},{8,12},{12,8},{1,5},{5,1},{9,13},{13,9},{2,6},{6,2},{1... | collective-permute-start | bytes 7864328 | tf_op jit(solution)/shard_map/ppermute | solution.py:263
  1047.2 101.1 %collective-permute-start.58 = (f32[1280,512]{1,0:T(8,128)}, f32[1280,512]{1,0:T(8,128)}, u32[]{:S(2)}, u32[]{:S(2)}) collective-permute-start(f32[1280,512]{1,0:T(8,128)} %get-tuple-element.96), channel_id=1, source_target_pairs={{0,8},{4,12},{8,0},{12,4},{1,9},{5,13},{9,1},{13,5},{2,10},{6,14},... | collective-permute-start | bytes 7864328 | tf_op jit(solution)/shard_map/ppermute | solution.py:263
  1074.6 74.6 %collective-permute-start.56 = (f32[1280,512]{1,0:T(8,128)}, f32[1280,512]{1,0:T(8,128)}, u32[]{:S(2)}, u32[]{:S(2)}) collective-permute-start(f32[1280,512]{1,0:T(8,128)} %get-tuple-element.94), channel_id=1, source_target_pairs={{0,4},{4,0},{8,12},{12,8},{1,5},{5,1},{9,13},{13,9},{2,6},{6,2},{1... | collective-permute-start | bytes 7864328 | tf_op jit(solution)/shard_map/ppermute | solution.py:263
  1111.4 155.1 %collective-permute-start.70 = (bf16[2048,896]{1,0:T(8,128)(2,1)}, bf16[2048,896]{1,0:T(8,128)(2,1)}, u32[]{:S(2)}, u32[]{:S(2)}) collective-permute-start(bf16[2048,896]{1,0:T(8,128)(2,1)} %get-tuple-element.106.refs_6_), channel_id=1, source_target_pairs={{0,1},{1,0},{2,3},{3,2},{4,5},{5,4},{6,7},{7,6},{8,9},{9,8},{10,11... | collective-permute-start | bytes 11010056 | tf_op jit(solution)/shard_map/ppermute | solution.py:263
  1111.4 60.1 %collective-permute-start.34 = (f32[1280,512]{1,0:T(8,128)}, f32[1280,512]{1,0:T(8,128)}, u32[]{:S(2)}, u32[]{:S(2)}) collective-permute-start(f32[1280,512]{1,0:T(8,128)} %get-tuple-element.80), channel_id=1, source_target_pairs={{0,8},{4,12},{8,0},{12,4},{1,9},{5,13},{9,1},{13,5},{2,10},{6,14},... | collective-permute-start | bytes 7864328 | tf_op jit(solution)/shard_map/ppermute | solution.py:263
  1147.8 60.0 %collective-permute-start.32 = (f32[1280,512]{1,0:T(8,128)}, f32[1280,512]{1,0:T(8,128)S(1)}, u32[]{:S(2)}, u32[]{:S(2)}) collective-permute-start(f32[1280,512]{1,0:T(8,128)} %get-tuple-element.78), channel_id=1, source_target_pairs={{0,4},{4,0},{8,12},{12,8},{1,5},{5,1},{9,13},{13,9},{2,6},{6,2},{1... | collective-permute-start | bytes 7864328 | tf_op jit(solution)/shard_map/ppermute | solution.py:263
  1148.4 79.2 %collective-permute-start.30 = (f32[1280,512]{1,0:T(8,128)}, f32[1280,512]{1,0:T(8,128)S(1)}, u32[]{:S(2)}, u32[]{:S(2)}) collective-permute-start(f32[1280,512]{1,0:T(8,128)} %get-tuple-element.76), channel_id=1, source_target_pairs={{0,8},{4,12},{8,0},{12,4},{1,9},{5,13},{9,1},{13,5},{2,10},{6,14},... | collective-permute-start | bytes 7864328 | tf_op jit(solution)/shard_map/ppermute | solution.py:263
  1149.3 114.8 %collective-permute-start.27 = (f32[1280,512]{1,0:T(8,128)}, f32[1280,512]{1,0:T(8,128)S(1)}, u32[]{:S(2)}, u32[]{:S(2)}) collective-permute-start(f32[1280,512]{1,0:T(8,128)} %get-tuple-element.70), channel_id=1, source_target_pairs={{0,4},{4,0},{8,12},{12,8},{1,5},{5,1},{9,13},{13,9},{2,6},{6,2},{1... | collective-permute-start | bytes 7864328 | tf_op jit(solution)/shard_map/ppermute | solution.py:263
  1171.5 120.6 %collective-permute-start.63 = (f32[1280,256]{1,0:T(8,128)S(1)}, f32[1280,256]{1,0:T(8,128)S(1)}, u32[]{:S(2)}, u32[]{:S(2)}) collective-permute-start(f32[1280,256]{1,0:T(8,128)S(1)} %slice_add_fusion), channel_id=1, source_target_pairs={{0,4},{4,0},{8,12},{12,8},{1,5},{5,1},{9,13},{13,9},{2,6},{6,2},{1... | collective-permute-start | bytes 3932168 | tf_op jit(solution)/shard_map/ppermute | solution.py:263
  1207.8 85.5 %collective-permute-start.61 = (f32[1280,256]{1,0:T(8,128)S(1)}, f32[1280,256]{1,0:T(8,128)S(1)}, u32[]{:S(2)}, u32[]{:S(2)}) collective-permute-start(f32[1280,256]{1,0:T(8,128)S(1)} %slice_add_fusion.1), channel_id=1, source_target_pairs={{0,8},{4,12},{8,0},{12,4},{1,9},{5,13},{9,1},{13,5},{2,10},{6,14},... | collective-permute-start | bytes 3932168 | tf_op jit(solution)/shard_map/ppermute | solution.py:263
  1227.6 92.6 %collective-permute-start.59 = (f32[1280,256]{1,0:T(8,128)S(1)}, f32[1280,256]{1,0:T(8,128)S(1)}, u32[]{:S(2)}, u32[]{:S(2)}) collective-permute-start(f32[1280,256]{1,0:T(8,128)S(1)} %slice_add_fusion.2), channel_id=1, source_target_pairs={{0,4},{4,0},{8,12},{12,8},{1,5},{5,1},{9,13},{13,9},{2,6},{6,2},{1... | collective-permute-start | bytes 3932168 | tf_op jit(solution)/shard_map/ppermute | solution.py:263
  1264.0 56.2 %collective-permute-start.57 = (f32[1280,256]{1,0:T(8,128)S(1)}, f32[1280,256]{1,0:T(8,128)S(1)}, u32[]{:S(2)}, u32[]{:S(2)}) collective-permute-start(f32[1280,256]{1,0:T(8,128)S(1)} %slice_add_fusion.3), channel_id=1, source_target_pairs={{0,8},{4,12},{8,0},{12,4},{1,9},{5,13},{9,1},{13,5},{2,10},{6,14},... | collective-permute-start | bytes 3932168 | tf_op jit(solution)/shard_map/ppermute | solution.py:263
  1266.5 81.0 %collective-permute-start.35 = (f32[1280,256]{1,0:T(8,128)S(1)}, f32[1280,256]{1,0:T(8,128)S(1)}, u32[]{:S(2)}, u32[]{:S(2)}) collective-permute-start(f32[1280,256]{1,0:T(8,128)S(1)} %slice_add_fusion.4), channel_id=1, source_target_pairs={{0,4},{4,0},{8,12},{12,8},{1,5},{5,1},{9,13},{13,9},{2,6},{6,2},{1... | collective-permute-start | bytes 3932168 | tf_op jit(solution)/shard_map/ppermute | solution.py:263
  1292.1 57.3 %collective-permute-start.33 = (f32[1280,256]{1,0:T(8,128)S(1)}, f32[1280,256]{1,0:T(8,128)S(1)}, u32[]{:S(2)}, u32[]{:S(2)}) collective-permute-start(f32[1280,256]{1,0:T(8,128)S(1)} %slice_add_fusion.5), channel_id=1, source_target_pairs={{0,8},{4,12},{8,0},{12,4},{1,9},{5,13},{9,1},{13,5},{2,10},{6,14},... | collective-permute-start | bytes 3932168 | tf_op jit(solution)/shard_map/ppermute | solution.py:263
  1293.3 149.5 %collective-permute-start.69 = (bf16[2048,1280]{1,0:T(8,128)(2,1)}, bf16[2048,1280]{1,0:T(8,128)(2,1)}, u32[]{:S(2)}, u32[]{:S(2)}) collective-permute-start(bf16[2048,1280]{1,0:T(8,128)(2,1)} %get-tuple-element.105.refs_4_), channel_id=1, source_target_pairs={{0,1},{1,0},{2,3},{3,2},{4,5},{5,4},{6,7},{7,6},{8,9},{9,8},{10,11... | collective-permute-start | bytes 15728648 | tf_op jit(solution)/shard_map/ppermute | solution.py:263
  1320.2 122.7 %collective-permute-start.68 = (bf16[2048,1280]{1,0:T(8,128)(2,1)}, bf16[2048,1280]{1,0:T(8,128)(2,1)}, u32[]{:S(2)}, u32[]{:S(2)}) collective-permute-start(bf16[2048,1280]{1,0:T(8,128)(2,1)} %get-tuple-element.104.refs_2_), channel_id=1, source_target_pairs={{0,1},{1,0},{2,3},{3,2},{4,5},{5,4},{6,7},{7,6},{8,9},{9,8},{10,11... | collective-permute-start | bytes 15728648 | tf_op jit(solution)/shard_map/ppermute | solution.py:263
  1320.2 123.1 %collective-permute-start.66 = (bf16[2048,1280]{1,0:T(8,128)(2,1)}, bf16[2048,1280]{1,0:T(8,128)(2,1)}, u32[]{:S(2)}, u32[]{:S(2)}) collective-permute-start(bf16[2048,1280]{1,0:T(8,128)(2,1)} %get-tuple-element.102.refs_4_), channel_id=1, source_target_pairs={{0,1},{1,0},{2,3},{3,2},{4,5},{5,4},{6,7},{7,6},{8,9},{9,8},{10,11... | collective-permute-start | bytes 15728648 | tf_op jit(solution)/shard_map/ppermute | solution.py:263
  1377.5 64.9 %collective-permute-start.67 = (bf16[2048,896]{1,0:T(8,128)(2,1)}, bf16[2048,896]{1,0:T(8,128)(2,1)}, u32[]{:S(2)}, u32[]{:S(2)}) collective-permute-start(bf16[2048,896]{1,0:T(8,128)(2,1)} %get-tuple-element.103.refs_6_), channel_id=1, source_target_pairs={{0,1},{1,0},{2,3},{3,2},{4,5},{5,4},{6,7},{7,6},{8,9},{9,8},{10,11... | collective-permute-start | bytes 11010056 | tf_op jit(solution)/shard_map/ppermute | solution.py:263
  1409.5 82.8 %collective-permute-start.65 = (bf16[2048,1280]{1,0:T(8,128)(2,1)}, bf16[2048,1280]{1,0:T(8,128)(2,1)}, u32[]{:S(2)}, u32[]{:S(2)}) collective-permute-start(bf16[2048,1280]{1,0:T(8,128)(2,1)} %get-tuple-element.101.refs_2_), channel_id=1, source_target_pairs={{0,1},{1,0},{2,3},{3,2},{4,5},{5,4},{6,7},{7,6},{8,9},{9,8},{10,11... | collective-permute-start | bytes 15728648 | tf_op jit(solution)/shard_map/ppermute | solution.py:263
  1442.4 99.0 %collective-permute-start.71 = (bf16[2048,1280]{1,0:T(8,128)(2,1)}, bf16[2048,1280]{1,0:T(8,128)(2,1)}, u32[]{:S(2)}, u32[]{:S(2)}) collective-permute-start(bf16[2048,1280]{1,0:T(8,128)(2,1)} %get-tuple-element.137), channel_id=1, source_target_pairs={{0,1},{1,0},{2,3},{3,2},{4,5},{5,4},{6,7},{7,6},{8,9},{9,8},{10,11... | collective-permute-start | bytes 15728648 | tf_op jit(solution)/shard_map/ppermute | solution.py:263
  1442.8 98.6 %collective-permute-start.73 = (bf16[1280,2048]{1,0:T(8,128)(2,1)}, bf16[1280,2048]{1,0:T(8,128)(2,1)}, u32[]{:S(2)}, u32[]{:S(2)}) collective-permute-start(bf16[1280,2048]{1,0:T(8,128)(2,1)} %get-tuple-element.64.refs_2_.refs_4_), channel_id=1, source_target_pairs={{0,1},{1,0},{2,3},{3,2},{4,5},{5,4},{6,7},{7,6},{8,9},{9,8},{10,11... | collective-permute-start | bytes 15728648 | tf_op jit(solution)/shard_map/ppermute | solution.py:263
  1442.9 98.5 %collective-permute-start.72 = (bf16[1280,2048]{1,0:T(8,128)(2,1)}, bf16[1280,2048]{1,0:T(8,128)(2,1)}, u32[]{:S(2)}, u32[]{:S(2)}) collective-permute-start(bf16[1280,2048]{1,0:T(8,128)(2,1)} %get-tuple-element.61.refs_1_.refs_2_), channel_id=1, source_target_pairs={{0,1},{1,0},{2,3},{3,2},{4,5},{5,4},{6,7},{7,6},{8,9},{9,8},{10,11... | collective-permute-start | bytes 15728648 | tf_op jit(solution)/shard_map/ppermute | solution.py:263
  1443.3 98.1 %collective-permute-start.74 = (bf16[896,2048]{1,0:T(8,128)(2,1)S(1)}, bf16[896,2048]{1,0:T(8,128)(2,1)}, u32[]{:S(2)}, u32[]{:S(2)}) collective-permute-start(bf16[896,2048]{1,0:T(8,128)(2,1)S(1)} %copy-done.4), channel_id=1, source_target_pairs={{0,1},{1,0},{2,3},{3,2},{4,5},{5,4},{6,7},{7,6},{8,9},{9,8},{10,11... | collective-permute-start | bytes 11010056 | tf_op jit(solution)/shard_map/ppermute | solution.py:263
  (68 other events, 3072.3 us)

commit v3 on v2

--- a/solution.py
+++ b/solution.py
@@ -55,10 +55,20 @@
 
 
 def near_body(n_out, *refs):
-    pieces, ws, outs, (buf, sems) = refs[:8], refs[8 : 8 + 2 * n_out], refs[8 + 2 * n_out : -2], refs[-2:]
-    m = load(pieces, buf, sems)
+    pieces, ws, outs, (buf, sems) = refs[:4], refs[4 : 4 + 2 * n_out], refs[-2 - n_out : -2], refs[-2:]
+    r = pieces[0].shape[0]
+    dq = ws[0].shape[0]
+    copies = [pltpu.make_async_copy(p, buf.at[pl.ds(k * r, r)], sems.at[k]) for k, p in enumerate(pieces)]
+
+    @pl.when(pl.program_id(0) == 0)
+    def _():
+        for c in copies:
+            c.start()
+        for c in copies:
+            c.wait()
+
     for k in range(n_out):
-        outs[k][...] = pair(buf, m, ws[2 * k], ws[2 * k + 1])
+        outs[k][...] = dot(buf[:, :dq], ws[2 * k][...]) + dot(buf[:, dq:], ws[2 * k + 1][...])
 
 
 def fwd_body(*refs):
@@ -112,9 +122,35 @@
     )(*pieces, *ws, *extra)
 
 
-def near(pieces, ws, c, fc):
+def near_both_body(*refs):
+    pieces, ws, out, (buf, sems) = refs[:8], refs[8:10], refs[10], refs[11:]
+    m = load(pieces, buf, sems)
+    out[...] = pair(buf, m, ws[0], ws[1])
+
+
+def near_both(pieces, ws, c, fc):
+    return grouped(near_both_body, pieces, ws, c * (CHUNK // TILE), [], fc, [("mn", f32)])
+
+
+def near(pieces, ws, c, fc, group, prev):
     n_out = len(ws) // 2
-    return grouped(functools.partial(near_body, n_out), pieces, ws, c * (CHUNK // TILE), [], fc, [("mn", f32)] * n_out)
+    r, d = pieces[0].shape
+    dq = ws[0].shape[0]
+    first = c * (CHUNK // TILE)
+    n_in = 4 + len(ws)
+    hbm = pl.BlockSpec(memory_space=pltpu.HBM)
+    return pl.pallas_call(
+        functools.partial(near_body, n_out),
+        grid=(pl.cdiv(fc, TILE),),
+        in_specs=[hbm] * 4 + [pl.BlockSpec((dq, TILE), lambda n: (0, first + n))] * len(ws) + [hbm] * len(prev),
+        out_specs=[pl.BlockSpec((4 * r, TILE), lambda n: (group, n))] * n_out,
+        out_shape=[jax.ShapeDtypeStruct((8 * r, fc), f32)] * n_out,
+        scratch_shapes=[pltpu.VMEM((4 * r, d), bf), pltpu.SemaphoreType.DMA((4,))],
+        input_output_aliases={n_in + k: k for k in range(len(prev))},
+        compiler_params=params(),
+        cost_estimate=cost(8 * len(ws) * r * d * fc, 4e7),
+        name="near",
+    )(*pieces, *ws, *prev)
 
 
 def forward(pieces, ws, acc):
@@ -309,11 +345,12 @@
         xq_s = pc(xq_out)
         dyq, dyq_s = col(dyp, 0), pc(col(dyp, 1))
 
-        acc = [None] * nc
-        xa = xp[0::2]
-        for c in range(nc):
-            acc[c] = near(xa, [w_gate, wg_s, w_up, wu_s], c, width(c))
-        a, b, ht, ht_s, across, g0 = [], [], [], [], [], [None] * nc
+        acc = [[]] * nc
+        for g in range(2):
+            for c in range(nc):
+                acc[c] = near(xp[8 * g : 8 * g + 8 : 2], [w_gate, wg_s, w_up, wu_s], c, width(c), g, acc[c])
+        a, b, ht, ht_s, across, g0 = [], [], [], [], [], [[]] * nc
+        dwd = None
         for c in range(nc):
             gx, ux = wgx[c], wux[c]
             gs, us = pc(gx), pc(ux)
@@ -323,9 +360,10 @@
             b.append(bc)
             ht.append(htc)
             ht_s.append(pc(htc))
+            dwd = weight_grad((dyq, dyq_s), [(htc, ht_s[c])], True, fl, c, dwd)
             if c == 0:
                 for k in range(nc):
-                    (g0[k],) = near(dyp[0::2], [wd_t, wd_s], k, width(k))
+                    g0[k] = near_both(dyp[0::2], [wd_t, wd_s], k, width(k))
             if c == nc - 2:
                 terms = [(0, starts[k], k) for k in range(nc - 1)]
                 yacc = [partial_sums([w], ht, terms, "yz"[q], 2) for q, w in enumerate((wd_t, wd_s))]
@@ -342,10 +380,9 @@
 
         da, db, dat, dbt = [], [], [], []
         for c in range(nc):
-            grads = backward(dyp[1::2], [wdx[c], pc(wdx[c])], [g0[c], a[c], b[c]])
+            grads = backward(dyp[1::2], [wdx[c], pc(wdx[c])], [*g0[c], a[c], b[c]])
             for lst, v in zip((da, db, dat, dbt), grads):
                 lst.append(v)
-        dwd = weight_grad((dyq, dyq_s), list(zip(ht, ht_s)), True, fl, 0)
         y_second = {(g, q): second_hop("yz"[q], yacc[q][2 * g], y_first[g, q]) for g, q in order}
         da_s, db_s = [pc(v) for v in da], [pc(v) for v in db]
 

time: 1600 us -> 1610 us (level)
  Pallas kernels: 699 us -> 725 us
  waiting for transfers between devices: 725 us -> 699 us
    pallas_call x0 -> x6, Pallas kernels: none -> 116 us  [near(): pl.pallas_call(functools.partial(near_body, n_out), grid=(pl.cdiv(fc, TIL...]
    pallas_call x12 -> x9, Pallas kernels: 352 us -> 253 us  [grouped(): pl.pallas_call(body, grid=(2, nt), in_specs=[pl.BlockSpec(memory_space=pl...]
    ppermute x75, waiting for transfers between devices: 725 us -> 699 us  [hop(): return lambda v: lax.ppermute(v, axis, pairs)]
    pallas_call x3 -> x5, Pallas kernels: 147 us -> 156 us  [weight_grad(): pl.pallas_call(functools.partial(dw_body, counts, rows), grid=(n,), in_sp...]
    unnamed x128 -> x110, local copies, waits for them, and re-layouts: 39.3 us -> 38.3 us
  transfers between devices with their start and end apart: 75 -> 75, of which waited for: 29 -> 28; matrix products, arithmetic and copies ran while one was open for 6% -> 6% of each run, Pallas kernels for 41% -> 42%
where the time goes in v3:
time: 1610 us; the launch traced here: 1600 us
  Pallas kernels  725 us (45%)
  waiting for transfers between devices  699 us (43%)
  local copies, waits for them, and re-layouts  87.3 us (5%)
  starting transfers between devices  66.3 us (4%)
  other arithmetic  19.4 us (1%)
    ppermute x75, waiting for transfers between devices, hop(): return lambda v: lax.ppermute(v, axis, pairs)  699 us
    pallas_call x9, Pallas kernels, grouped(): pl.pallas_call(body, grid=(2, nt), in_specs=[pl.BlockSpec(memory_space=pl...  253 us
    pallas_call x8, Pallas kernels, partial_sums(): pl.pallas_call(functools.partial(part_body, axis, terms, len(ws), len(ts)...  179 us
    pallas_call x5, Pallas kernels, weight_grad(): pl.pallas_call(functools.partial(dw_body, counts, rows), grid=(n,), in_sp...  156 us
    pallas_call x6, Pallas kernels, near(): pl.pallas_call(functools.partial(near_body, n_out), grid=(pl.cdiv(fc, TIL...  116 us
    ppermute x75, starting transfers between devices, hop(): return lambda v: lax.ppermute(v, axis, pairs)  66.3 us
    unnamed x110, local copies, waits for them, and re-layouts  38.3 us
  transfers between devices with their start and end apart: 75, of which 28 were waited for; matrix products, arithmetic and copies ran while one was open for 6% of the time, Pallas kernels for 42%

profile of v3, /device:TPU:0, one launch (start us, length us, event | category | flops | bytes accessed | tf_op | source)
XLA Modules:
  0.0 1598.4 jit_solution(8934972004385535703)
XLA Ops:
  0.7 4.5 constant_dynamic-update-slice_fusion
  16.1 6.2 fusion.2
  22.3 6.2 fusion.1
  28.4 12.8 copy.32
  41.2 6.1 fusion
  53.7 3.4 slice.254
  68.7 4.2 collective-permute-done.40
  76.9 21.8 %collective-permute-done.17.refs_2_ = bf16[256,2560]{1,0:T(8,128)(2,1)S(1)} collective-permute-done((bf16[256,2560]{1,0:T(8,128)(2,1)}, bf16[256,2560]{1,0:T(8,128)(2,1)S(1)}, u32[]{:S(2)}, u32[]{:S(2)}) %collective-permute-start.17) | collective-permute-done | bytes 1310752 | tf_op jit(solution)/shard_map/ppermute | solution.py:299
  100.5 26.3 %collective-permute-done.48.refs_3_ = bf16[256,2560]{1,0:T(8,128)(2,1)S(1)} collective-permute-done((bf16[256,2560]{1,0:T(8,128)(2,1)}, bf16[256,2560]{1,0:T(8,128)(2,1)S(1)}, u32[]{:S(2)}, u32[]{:S(2)}) %collective-permute-start.48) | collective-permute-done | bytes 1310752 | tf_op jit(solution)/shard_map/ppermute | solution.py:299
  132.5 22.4 %collective-permute-done.18.refs_3_ = bf16[256,2560]{1,0:T(8,128)(2,1)S(1)} collective-permute-done((bf16[256,2560]{1,0:T(8,128)(2,1)}, bf16[256,2560]{1,0:T(8,128)(2,1)S(1)}, u32[]{:S(2)}, u32[]{:S(2)}) %collective-permute-start.18) | collective-permute-done | bytes 1310752 | tf_op jit(solution)/shard_map/ppermute | solution.py:299
  159.4 23.6 %collective-permute-done.50.refs_6_ = bf16[256,2560]{1,0:T(8,128)(2,1)S(1)} collective-permute-done((bf16[256,2560]{1,0:T(8,128)(2,1)S(1)}, bf16[256,2560]{1,0:T(8,128)(2,1)S(1)}, u32[]{:S(2)}, u32[]{:S(2)}) %collective-permute-start.50) | collective-permute-done | bytes 1310752 | tf_op jit(solution)/shard_map/ppermute | solution.py:299
  188.7 22.4 %collective-permute-done.12.refs_2_ = bf16[256,2560]{1,0:T(8,128)(2,1)S(1)} collective-permute-done((bf16[256,2560]{1,0:T(8,128)(2,1)S(1)}, bf16[256,2560]{1,0:T(8,128)(2,1)S(1)}, u32[]{:S(2)}, u32[]{:S(2)}) %collective-permute-start.12) | collective-permute-done | bytes 1310752 | tf_op jit(solution)/shard_map/ppermute | solution.py:299
  213.9 23.6 %collective-permute-done.51.refs_7_ = bf16[256,2560]{1,0:T(8,128)(2,1)S(1)} collective-permute-done((bf16[256,2560]{1,0:T(8,128)(2,1)S(1)}, bf16[256,2560]{1,0:T(8,128)(2,1)S(1)}, u32[]{:S(2)}, u32[]{:S(2)}) %collective-permute-start.51) | collective-permute-done | bytes 1310752 | tf_op jit(solution)/shard_map/ppermute | solution.py:299
  242.5 24.4 %collective-permute-done.13.refs_3_ = bf16[256,2560]{1,0:T(8,128)(2,1)S(1)} collective-permute-done((bf16[256,2560]{1,0:T(8,128)(2,1)S(1)}, bf16[256,2560]{1,0:T(8,128)(2,1)S(1)}, u32[]{:S(2)}, u32[]{:S(2)}) %collective-permute-start.13) | collective-permute-done | bytes 1310752 | tf_op jit(solution)/shard_map/ppermute | solution.py:299
  270.3 8.0 copy.34
  279.4 16.3 %collective-permute-done.1.refs_2_ = bf16[256,2560]{1,0:T(8,128)(2,1)} collective-permute-done((bf16[256,2560]{1,0:T(8,128)(2,1)}, bf16[256,2560]{1,0:T(8,128)(2,1)}, u32[]{:S(2)}, u32[]{:S(2)}) %collective-permute-start.1) | collective-permute-done | bytes 1310752 | tf_op jit(solution)/shard_map/ppermute | solution.py:299
  297.8 28.6 %collective-permute-done.25.refs_10_.refs_4_ = bf16[1280,1280]{1,0:T(8,128)(2,1)} collective-permute-done((bf16[1280,1280]{1,0:T(8,128)(2,1)}, bf16[1280,1280]{1,0:T(8,128)(2,1)}, u32[]{:S(2)}, u32[]{:S(2)}) %collective-permute-start.25) | collective-permute-done | bytes 3276832 | tf_op jit(solution)/shard_map/ppermute | solution.py:299
  327.9 20.3 %near.8 = (f32[2048,1280]{1,0:T(8,128)}, f32[2048,1280]{1,0:T(8,128)}) custom-call(bf16[256,2560]{1,0:T(8,128)(2,1)} %pad_maximum_fusion.3.refs_0_, bf16[256,2560]{1,0:T(8,128)(2,1)} %collective-permute-done.16.refs_1_, bf16[256,2560]{1,0:T(8,128)(2,1)} %copy-done.38, bf16[256,2560]{1,0:T(8,128)(2,1)} %copy-done.39, bf16[1280,3456]{1,0:T(8,128)(2,1)} %refs_0_.4, ...), custom_call_target="tpu_custom_call" | custom-call | flops 26843545600 | bytes 40000000 | tf_op jit(solution)/shard_map/near/pallas_call | solution.py:142
  348.2 20.4 %near.10 = (f32[2048,1280]{1,0:T(8,128)}, f32[2048,1280]{1,0:T(8,128)}) custom-call(bf16[256,2560]{1,0:T(8,128)(2,1)} %pad_maximum_fusion.3.refs_0_, bf16[256,2560]{1,0:T(8,128)(2,1)} %collective-permute-done.16.refs_1_, bf16[256,2560]{1,0:T(8,128)(2,1)} %copy-done.38, bf16[256,2560]{1,0:T(8,128)(2,1)} %copy-done.39, bf16[1280,3456]{1,0:T(8,128)(2,1)} %refs_0_.4, ...), custom_call_target="tpu_custom_call" | custom-call | flops 26843545600 | bytes 40000000 | tf_op jit(solution)/shard_map/near/pallas_call | solution.py:142
  370.7 20.5 %near.11 = (f32[2048,1280]{1,0:T(8,128)}, f32[2048,1280]{1,0:T(8,128)}) custom-call(bf16[256,2560]{1,0:T(8,128)(2,1)} %copy-done.27, bf16[256,2560]{1,0:T(8,128)(2,1)} %copy-done.35, bf16[256,2560]{1,0:T(8,128)(2,1)} %copy-done.36, bf16[256,2560]{1,0:T(8,128)(2,1)} %copy-done.37, ...), custom_call_target="tpu_custom_call", output_to_operand_aliasing={{0}: (8, {}), {1}: (9, {})} | custom-call | flops 26843545600 | bytes 40000000 | tf_op jit(solution)/shard_map/near/pallas_call | solution.py:142
  391.3 9.2 collective-permute-done.4.refs_5_
  401.7 26.3 %collective-permute-done.6.refs_7_ = bf16[256,2560]{1,0:T(8,128)(2,1)} collective-permute-done((bf16[256,2560]{1,0:T(8,128)(2,1)}, bf16[256,2560]{1,0:T(8,128)(2,1)}, u32[]{:S(2)}, u32[]{:S(2)}) %collective-permute-start.6) | collective-permute-done | bytes 1310752 | tf_op jit(solution)/shard_map/ppermute | solution.py:299
  431.1 38.5 %shard_map.94 = (f32[2048,1280]{1,0:T(8,128)}, f32[2048,1280]{1,0:T(8,128)}, bf16[1280,2048]{1,0:T(8,128)(2,1)}) custom-call(bf16[256,2560]{1,0:T(8,128)(2,1)} %pad_maximum_fusion.2.refs_0_, bf16[256,2560]{1,0:T(8,128)(2,1)} %copy-done.46, bf16[256,2560]{1,0:T(8,128)(2,1)} %collective-permute-done.1.refs_2_, ...), custom_call_target="tpu_custom_call", output_to_operand_aliasing={{0}: (12, {}), {1}: (13, {})} | custom-call | flops 26843545600 | bytes 80000000 | tf_op jit(solution)/shard_map/pallas_call | solution.py:112
  471.2 31.5 %collective-permute-done.7.refs_8_.refs_2_ = bf16[1280,896]{1,0:T(8,128)(2,1)} collective-permute-done((bf16[1280,896]{1,0:T(8,128)(2,1)}, bf16[1280,896]{1,0:T(8,128)(2,1)}, u32[]{:S(2)}, u32[]{:S(2)}) %collective-permute-start.7) | collective-permute-done | bytes 2293792 | tf_op jit(solution)/shard_map/ppermute | solution.py:299
  502.6 17.2 %near.6 = (f32[2048,896]{1,0:T(8,128)}, f32[2048,896]{1,0:T(8,128)}) custom-call(bf16[256,2560]{1,0:T(8,128)(2,1)} %pad_maximum_fusion.3.refs_0_, bf16[256,2560]{1,0:T(8,128)(2,1)} %collective-permute-done.16.refs_1_, bf16[256,2560]{1,0:T(8,128)(2,1)} %copy-done.38, bf16[256,2560]{1,0:T(8,128)(2,1)} %copy-done.39, bf16[1280,3456]{1,0:T(8,128)(2,1)} %refs_0_.4, ...), custom_call_target="tpu_custom_call" | custom-call | flops 18790481920 | bytes 40000000 | tf_op jit(solution)/shard_map/near/pallas_call | solution.py:142
  521.1 30.7 %collective-permute-done.54.refs_8_ = bf16[1280,896]{1,0:T(8,128)(2,1)} collective-permute-done((bf16[1280,896]{1,0:T(8,128)(2,1)}, bf16[1280,896]{1,0:T(8,128)(2,1)}, u32[]{:S(2)}, u32[]{:S(2)}) %collective-permute-start.54) | collective-permute-done | bytes 2293792 | tf_op jit(solution)/shard_map/ppermute | solution.py:299
  553.1 17.3 %near.7 = (f32[2048,896]{1,0:T(8,128)}, f32[2048,896]{1,0:T(8,128)}) custom-call(bf16[256,2560]{1,0:T(8,128)(2,1)} %copy-done.27, bf16[256,2560]{1,0:T(8,128)(2,1)} %copy-done.35, bf16[256,2560]{1,0:T(8,128)(2,1)} %copy-done.36, bf16[256,2560]{1,0:T(8,128)(2,1)} %copy-done.37, ...), custom_call_target="tpu_custom_call", output_to_operand_aliasing={{0}: (8, {}), {1}: (9, {})} | custom-call | flops 18790481920 | bytes 40000000 | tf_op jit(solution)/shard_map/near/pallas_call | solution.py:142
  573.2 31.7 %shard_map.92 = (f32[2048,896]{1,0:T(8,128)}, f32[2048,896]{1,0:T(8,128)}, bf16[896,2048]{1,0:T(8,128)(2,1)}) custom-call(bf16[256,2560]{1,0:T(8,128)(2,1)} %pad_maximum_fusion.2.refs_0_, bf16[256,2560]{1,0:T(8,128)(2,1)} %copy-done.46, bf16[256,2560]{1,0:T(8,128)(2,1)} %collective-permute-done.1.refs_2_, ...), custom_call_target="tpu_custom_call", output_to_operand_aliasing={{0}: (12, {}), {1}: (13, {})} | custom-call | flops 18790481920 | bytes 80000000 | tf_op jit(solution)/shard_map/pallas_call | solution.py:112
  605.5 86.7 %collective-permute-done.52.refs_8_ = bf16[1280,1280]{1,0:T(8,128)(2,1)} collective-permute-done((bf16[1280,1280]{1,0:T(8,128)(2,1)}, bf16[1280,1280]{1,0:T(8,128)(2,1)}, u32[]{:S(2)}, u32[]{:S(2)}) %collective-permute-start.52) | collective-permute-done | bytes 3276832 | tf_op jit(solution)/shard_map/ppermute | solution.py:299
  693.5 21.0 %shard_map.97.refs_10_ = f32[2048,1280]{1,0:T(8,128)} custom-call(bf16[256,2560]{1,0:T(8,128)(2,1)} %pad_maximum_fusion.5.refs_0_, bf16[256,2560]{1,0:T(8,128)(2,1)} %collective-permute-done.46.refs_1_, bf16[256,2560]{1,0:T(8,128)(2,1)} %collective-permute-done.47.refs_2_, bf16[256,2560]{1,0:T(8,128)(2,1)} %copy-done.22, bf16[256,2560]{1,0:T(8,128)(2,1)} %copy-done.20, ...), custom_call_target="tpu_custom_call" | custom-call | flops 13421772800 | bytes 80000000 | tf_op jit(solution)/shard_map/pallas_call | solution.py:112
  716.6 17.5 %shard_map.99.refs_10_ = f32[2048,896]{1,0:T(8,128)} custom-call(bf16[256,2560]{1,0:T(8,128)(2,1)} %pad_maximum_fusion.5.refs_0_, bf16[256,2560]{1,0:T(8,128)(2,1)} %collective-permute-done.46.refs_1_, bf16[256,2560]{1,0:T(8,128)(2,1)} %collective-permute-done.47.refs_2_, bf16[256,2560]{1,0:T(8,128)(2,1)} %copy-done.22, bf16[256,2560]{1,0:T(8,128)(2,1)} %copy-done.20, ...), custom_call_target="tpu_custom_call" | custom-call | flops 9395240960 | bytes 80000000 | tf_op jit(solution)/shard_map/pallas_call | solution.py:112
  734.2 21.1 %shard_map.95.refs_10_ = f32[2048,1280]{1,0:T(8,128)} custom-call(bf16[256,2560]{1,0:T(8,128)(2,1)} %pad_maximum_fusion.5.refs_0_, bf16[256,2560]{1,0:T(8,128)(2,1)} %collective-permute-done.46.refs_1_, bf16[256,2560]{1,0:T(8,128)(2,1)} %collective-permute-done.47.refs_2_, bf16[256,2560]{1,0:T(8,128)(2,1)} %copy-done.22, bf16[256,2560]{1,0:T(8,128)(2,1)} %copy-done.20, ...), custom_call_target="tpu_custom_call" | custom-call | flops 13421772800 | bytes 80000000 | tf_op jit(solution)/shard_map/pallas_call | solution.py:112
  755.3 7.2 collective-permute-done.21.refs_10_.refs_3_
  762.5 68.3 %collective-permute-done.44.refs_8_ = bf16[1280,1280]{1,0:T(8,128)(2,1)} collective-permute-done((bf16[1280,1280]{1,0:T(8,128)(2,1)}, bf16[1280,1280]{1,0:T(8,128)(2,1)}, u32[]{:S(2)}, u32[]{:S(2)}) %collective-permute-start.44) | collective-permute-done | bytes 3276832 | tf_op jit(solution)/shard_map/ppermute | solution.py:299
  831.8 30.4 %shard_map.98 = (bf16[2048,1280]{1,0:T(8,128)(2,1)}, bf16[2048,1280]{1,0:T(8,128)(2,1)}, bf16[1280,1024]{1,0:T(8,128)(2,1)}, bf16[1280,1024]{1,0:T(8,128)(2,1)}) custom-call(bf16[256,2560]{1,0:T(8,128)(2,1)} %pad_maximum_fusion.4.refs_0_, bf16[256,2560]{1,0:T(8,128)(2,1)} %copy-done.30, bf16[256,2560]{1,0:T(8,128)(2,1)} %copy-done.29, ...), custom_call_target="tpu_custom_call" | custom-call | flops 13421772800 | bytes 80000000 | tf_op jit(solution)/shard_map/pallas_call | solution.py:112
  862.2 20.3 %near.9 = (f32[2048,1280]{1,0:T(8,128)}, f32[2048,1280]{1,0:T(8,128)}) custom-call(bf16[256,2560]{1,0:T(8,128)(2,1)} %copy-done.27, bf16[256,2560]{1,0:T(8,128)(2,1)} %copy-done.35, bf16[256,2560]{1,0:T(8,128)(2,1)} %copy-done.36, bf16[256,2560]{1,0:T(8,128)(2,1)} %copy-done.37, ...), custom_call_target="tpu_custom_call", output_to_operand_aliasing={{0}: (8, {}), {1}: (9, {})} | custom-call | flops 26843545600 | bytes 40000000 | tf_op jit(solution)/shard_map/near/pallas_call | solution.py:142
  883.9 24.5 %shard_map.100 = (bf16[2048,896]{1,0:T(8,128)(2,1)}, bf16[2048,896]{1,0:T(8,128)(2,1)}, bf16[896,1024]{1,0:T(8,128)(2,1)}, bf16[896,1024]{1,0:T(8,128)(2,1)}) custom-call(bf16[256,2560]{1,0:T(8,128)(2,1)} %pad_maximum_fusion.4.refs_0_, bf16[256,2560]{1,0:T(8,128)(2,1)} %copy-done.30, bf16[256,2560]{1,0:T(8,128)(2,1)} %copy-done.29, ...), custom_call_target="tpu_custom_call" | custom-call | flops 9395240960 | bytes 80000000 | tf_op jit(solution)/shard_map/pallas_call | solution.py:112
  908.5 38.0 %shard_map.93 = (f32[2048,1280]{1,0:T(8,128)}, f32[2048,1280]{1,0:T(8,128)}, bf16[1280,2048]{1,0:T(8,128)(2,1)}) custom-call(bf16[256,2560]{1,0:T(8,128)(2,1)} %pad_maximum_fusion.2.refs_0_, bf16[256,2560]{1,0:T(8,128)(2,1)} %copy-done.46, bf16[256,2560]{1,0:T(8,128)(2,1)} %collective-permute-done.1.refs_2_, ...), custom_call_target="tpu_custom_call", output_to_operand_aliasing={{0}: (12, {}), {1}: (13, {})} | custom-call | flops 26843545600 | bytes 80000000 | tf_op jit(solution)/shard_map/pallas_call | solution.py:112
  946.5 30.2 %shard_map.96 = (bf16[2048,1280]{1,0:T(8,128)(2,1)}, bf16[2048,1280]{1,0:T(8,128)(2,1)}, bf16[1280,1024]{1,0:T(8,128)(2,1)}, bf16[1280,1024]{1,0:T(8,128)(2,1)}) custom-call(bf16[256,2560]{1,0:T(8,128)(2,1)} %pad_maximum_fusion.4.refs_0_, bf16[256,2560]{1,0:T(8,128)(2,1)} %copy-done.30, bf16[256,2560]{1,0:T(8,128)(2,1)} %copy-done.29, ...), custom_call_target="tpu_custom_call" | custom-call | flops 13421772800 | bytes 80000000 | tf_op jit(solution)/shard_map/pallas_call | solution.py:112
  976.7 27.3 %partial_sums.15 = (f32[1280,512]{1,0:T(8,128)}, f32[1280,512]{1,0:T(8,128)}) custom-call(bf16[1280,1280]{1,0:T(8,128)(2,1)} %collective-permute-done.20.refs_9_.refs_0_, bf16[1280,1280]{1,0:T(8,128)(2,1)} %collective-permute-done.24.refs_9_.refs_1_, bf16[1280,896]{1,0:T(8,128)(2,1)} %collective-permute-done.8.refs_9_.refs_2_, ...), custom_call_target="tpu_custom_call" | custom-call | flops 18119393280 | bytes 30000000 | tf_op jit(solution)/shard_map/partial_sums/pallas_call | solution.py:197
  1005.1 27.7 %partial_sums.14 = (f32[1280,512]{1,0:T(8,128)}, f32[1280,512]{1,0:T(8,128)}) custom-call(bf16[1280,1280]{1,0:T(8,128)(2,1)} %collective-permute-done.19.refs_8_.refs_0_, bf16[1280,1280]{1,0:T(8,128)(2,1)} %collective-permute-done.23.refs_8_.refs_1_, bf16[1280,896]{1,0:T(8,128)(2,1)} %collective-permute-done.7.refs_8_.refs_2_, ...), custom_call_target="tpu_custom_call" | custom-call | flops 18119393280 | bytes 30000000 | tf_op jit(solution)/shard_map/partial_sums/pallas_call | solution.py:197
  1034.3 26.8 %partial_sums.13 = (f32[1280,512]{1,0:T(8,128)}, f32[1280,512]{1,0:T(8,128)}) custom-call(bf16[1280,3456]{1,0:T(8,128)(2,1)} %collective-permute-done.14.refs_5_.refs_0_, bf16[1280,3456]{1,0:T(8,128)(2,1)} %collective-permute-done.15.refs_7_.refs_1_, bf16[1280,1024]{1,0:T(8,128)(2,1)} %get-tuple-element.95.refs_2_.refs_6_, ...), custom_call_target="tpu_custom_call" | custom-call | flops 18119393280 | bytes 30000000 | tf_op jit(solution)/shard_map/partial_sums/pallas_call | solution.py:197
  1061.8 26.9 %partial_sums.12 = (f32[1280,512]{1,0:T(8,128)}, f32[1280,512]{1,0:T(8,128)}) custom-call(bf16[1280,3456]{1,0:T(8,128)(2,1)} %refs_0_.4, bf16[1280,3456]{1,0:T(8,128)(2,1)} %refs_1_.1, bf16[1280,1024]{1,0:T(8,128)(2,1)} %get-tuple-element.95.refs_2_.refs_6_, bf16[1280,1024]{1,0:T(8,128)(2,1)} %get-tuple-element.98.refs_3_.refs_7_, ...), custom_call_target="tpu_custom_call" | custom-call | flops 18119393280 | bytes 30000000 | tf_op jit(solution)/shard_map/partial_sums/pallas_call | solution.py:197
  1088.8 19.9 %partial_sums.10 = (f32[1280,512]{1,0:T(8,128)}, f32[1280,512]{1,0:T(8,128)}, f32[1280,512]{1,0:T(8,128)}, f32[1280,512]{1,0:T(8,128)}) custom-call(bf16[1280,3456]{1,0:T(8,128)(2,1)} %collective-permute-done.29.refs_0_.refs_9_, bf16[1280,2048]{1,0:T(8,128)(2,1)} %get-tuple-element.71.refs_1_.refs_2_, bf16[1280,2048]{1,0:T(8,128)(2,1)} %get-tuple-element.76.refs_2_), custom_call_target="tpu_custom_call" | custom-call | flops 13421772800 | bytes 30000000 | tf_op jit(solution)/shard_map/partial_sums/pallas_call | solution.py:197
  1108.7 15.2 partial_sums.11
  1125.6 20.3 %partial_sums.8 = (f32[1280,512]{1,0:T(8,128)}, f32[1280,512]{1,0:T(8,128)}, f32[1280,512]{1,0:T(8,128)}, f32[1280,512]{1,0:T(8,128)}) custom-call(bf16[1280,3456]{1,0:T(8,128)(2,1)} %bitcast.9, bf16[1280,2048]{1,0:T(8,128)(2,1)} %get-tuple-element.71.refs_1_.refs_2_, bf16[1280,2048]{1,0:T(8,128)(2,1)} %get-tuple-element.76.refs_2_), custom_call_target="tpu_custom_call" | custom-call | flops 13421772800 | bytes 30000000 | tf_op jit(solution)/shard_map/partial_sums/pallas_call | solution.py:197
  1146.0 14.8 partial_sums.9
  1167.2 16.8 %collective-permute-done.56.refs_2_ = f32[1280,512]{1,0:T(8,128)} collective-permute-done((f32[1280,512]{1,0:T(8,128)}, f32[1280,512]{1,0:T(8,128)}, u32[]{:S(2)}, u32[]{:S(2)}) %collective-permute-start.56) | collective-permute-done | bytes 2621472 | tf_op jit(solution)/shard_map/ppermute | solution.py:299
  1187.5 52.5 %collective-permute-done.32.refs_2_ = f32[1280,512]{1,0:T(8,128)S(1)} collective-permute-done((f32[1280,512]{1,0:T(8,128)}, f32[1280,512]{1,0:T(8,128)S(1)}, u32[]{:S(2)}, u32[]{:S(2)}) %collective-permute-start.32) | collective-permute-done | bytes 2621472 | tf_op jit(solution)/shard_map/ppermute | solution.py:299
  1243.8 52.4 %collective-permute-done.27.refs_2_ = f32[1280,512]{1,0:T(8,128)S(1)} collective-permute-done((f32[1280,512]{1,0:T(8,128)}, f32[1280,512]{1,0:T(8,128)S(1)}, u32[]{:S(2)}, u32[]{:S(2)}) %collective-permute-start.27) | collective-permute-done | bytes 2621472 | tf_op jit(solution)/shard_map/ppermute | solution.py:299
  1297.3 27.0 %collective-permute-done.63.refs_12_ = f32[1280,256]{1,0:T(8,128)S(1)} collective-permute-done((f32[1280,256]{1,0:T(8,128)S(1)}, f32[1280,256]{1,0:T(8,128)S(1)}, u32[]{:S(2)}, u32[]{:S(2)}) %collective-permute-start.63) | collective-permute-done | bytes 1310752 | tf_op jit(solution)/shard_map/ppermute | solution.py:299
  1328.9 23.4 %collective-permute-done.59.refs_6_ = f32[1280,256]{1,0:T(8,128)S(1)} collective-permute-done((f32[1280,256]{1,0:T(8,128)S(1)}, f32[1280,256]{1,0:T(8,128)S(1)}, u32[]{:S(2)}, u32[]{:S(2)}) %collective-permute-start.59) | collective-permute-done | bytes 1310752 | tf_op jit(solution)/shard_map/ppermute | solution.py:299
  1353.9 24.8 %collective-permute-done.35.refs_6_ = f32[1280,256]{1,0:T(8,128)S(1)} collective-permute-done((f32[1280,256]{1,0:T(8,128)S(1)}, f32[1280,256]{1,0:T(8,128)S(1)}, u32[]{:S(2)}, u32[]{:S(2)}) %collective-permute-start.35) | collective-permute-done | bytes 1310752 | tf_op jit(solution)/shard_map/ppermute | solution.py:299
  1382.9 5.5 finish.3
  1389.9 18.1 %collective-permute-done.31.refs_6_ = f32[1280,256]{1,0:T(8,128)S(1)} collective-permute-done((f32[1280,256]{1,0:T(8,128)}, f32[1280,256]{1,0:T(8,128)S(1)}, u32[]{:S(2)}, u32[]{:S(2)}) %collective-permute-start.31) | collective-permute-done | bytes 1310752 | tf_op jit(solution)/shard_map/ppermute | solution.py:299
  1410.9 6.4 collective-permute-done.36.refs_7_
  1417.8 8.0 copy.33
  1425.8 9.3 finish.5
  1435.0 6.8 finish.4
  1441.8 20.2 %weight_grad.7.refs_4_ = f32[3456,1280]{1,0:T(8,128)} custom-call(bf16[2048,1280]{1,0:T(8,128)(2,1)} %get-tuple-element.150.refs_0_, bf16[2048,1280]{1,0:T(8,128)(2,1)} %collective-permute-done.71.refs_1_, bf16[1280,2048]{1,0:T(8,128)(2,1)} %get-tuple-element.71.refs_1_.refs_2_, bf16[1280,2048]{1,0:T(8,128)(2,1)} %collective-permute-done.74.refs_3_), custom_call_target="tpu_custom_call" | custom-call | flops 13421772800 | bytes 50000000 | tf_op jit(solution)/shard_map/weight_grad/pallas_call | solution.py:245
  1462.5 20.6 %weight_grad.8.refs_4_ = f32[3456,1280]{1,0:T(8,128)} custom-call(bf16[2048,1280]{1,0:T(8,128)(2,1)} %get-tuple-element.150.refs_0_, bf16[2048,1280]{1,0:T(8,128)(2,1)} %collective-permute-done.71.refs_1_, bf16[1280,2048]{1,0:T(8,128)(2,1)} %get-tuple-element.76.refs_2_, ...), custom_call_target="tpu_custom_call", output_to_operand_aliasing={{}: (4, {})} | custom-call | flops 13421772800 | bytes 50000000 | tf_op jit(solution)/shard_map/weight_grad/pallas_call | solution.py:245
  1483.2 17.1 %weight_grad.9 = f32[3456,1280]{1,0:T(8,128)} custom-call(bf16[2048,1280]{1,0:T(8,128)(2,1)} %get-tuple-element.150.refs_0_, bf16[2048,1280]{1,0:T(8,128)(2,1)} %collective-permute-done.71.refs_1_, bf16[896,2048]{1,0:T(8,128)(2,1)} %get-tuple-element.66.refs_1_.refs_2_, ...), custom_call_target="tpu_custom_call", output_to_operand_aliasing={{}: (4, {})} | custom-call | flops 10737418240 | bytes 50000000 | tf_op jit(solution)/shard_map/weight_grad/pallas_call | solution.py:245
  1500.4 48.8 %weight_grad.6 = f32[1280,3456]{1,0:T(8,128)} custom-call(bf16[1280,2048]{1,0:T(8,128)(2,1)} %bitcast.12, bf16[1280,2048]{1,0:T(8,128)(2,1)} %collective-permute-done.64.refs_1_, bf16[2048,1280]{1,0:T(8,128)(2,1)} %get-tuple-element.116.refs_2_, bf16[2048,1280]{1,0:T(8,128)(2,1)} %collective-permute-done.68.refs_3_, ...), custom_call_target="tpu_custom_call" | custom-call | flops 37580963840 | bytes 50000000 | tf_op jit(solution)/shard_map/weight_grad/pallas_call | solution.py:245
  1549.2 49.0 %weight_grad.5 = f32[1280,3456]{1,0:T(8,128)} custom-call(bf16[1280,2048]{1,0:T(8,128)(2,1)} %bitcast.13, bf16[1280,2048]{1,0:T(8,128)(2,1)} %collective-permute-done.64.refs_1_, bf16[2048,1280]{1,0:T(8,128)(2,1)} %get-tuple-element.113.refs_2_, bf16[2048,1280]{1,0:T(8,128)(2,1)} %collective-permute-done.65.refs_3_, ...), custom_call_target="tpu_custom_call" | custom-call | flops 37580963840 | bytes 50000000 | tf_op jit(solution)/shard_map/weight_grad/pallas_call | solution.py:245
  (253 shorter events, 122.1 us)
Async XLA Ops:
  6.5 54.1 %collective-permute-start.46 = (bf16[256,2560]{1,0:T(8,128)(2,1)}, bf16[256,2560]{1,0:T(8,128)(2,1)}, u32[]{:S(2)}, u32[]{:S(2)}) collective-permute-start(bf16[256,2560]{1,0:T(8,128)(2,1)} %pad_maximum_fusion.5.refs_0_), channel_id=1, source_target_pairs={{0,4},{4,0},{8,12},{12,8},{1,5},{5,1},{9,13},{13,9},{2,6},{6,2},{1... | collective-permute-start | bytes 3932168 | tf_op jit(solution)/shard_map/ppermute | solution.py:299
  9.7 51.4 %collective-permute-start.47 = (bf16[256,2560]{1,0:T(8,128)(2,1)}, bf16[256,2560]{1,0:T(8,128)(2,1)}, u32[]{:S(2)}, u32[]{:S(2)}) collective-permute-start(bf16[256,2560]{1,0:T(8,128)(2,1)} %pad_maximum_fusion.5.refs_0_), channel_id=1, source_target_pairs={{0,8},{4,12},{8,0},{12,4},{1,9},{5,13},{9,1},{13,5},{2,10},{6,14},... | collective-permute-start | bytes 3932168 | tf_op jit(solution)/shard_map/ppermute | solution.py:299
  12.9 60.0 %collective-permute-start.40 = (bf16[256,5120]{1,0:T(8,128)(2,1)}, bf16[256,5120]{1,0:T(8,128)(2,1)S(1)}, u32[]{:S(2)}, u32[]{:S(2)}) collective-permute-start(bf16[256,5120]{1,0:T(8,128)(2,1)} %pad_maximum_fusion.1), channel_id=1, source_target_pairs={{0,2},{1,3},{2,0},{3,1},{4,6},{5,7},{6,4},{7,5},{8,10},{9,11},{10,... | collective-permute-start | bytes 7864328 | tf_op jit(solution)/shard_map/ppermute | solution.py:299
  15.6 51.3 %collective-permute-start.16 = (bf16[256,2560]{1,0:T(8,128)(2,1)}, bf16[256,2560]{1,0:T(8,128)(2,1)}, u32[]{:S(2)}, u32[]{:S(2)}) collective-permute-start(bf16[256,2560]{1,0:T(8,128)(2,1)} %pad_maximum_fusion.3.refs_0_), channel_id=1, source_target_pairs={{0,4},{4,0},{8,12},{12,8},{1,5},{5,1},{9,13},{13,9},{2,6},{6,2},{1... | collective-permute-start | bytes 3932168 | tf_op jit(solution)/shard_map/ppermute | solution.py:299
  16.1 311.3 %collective-permute-start.14 = (bf16[1280,3456]{1,0:T(8,128)(2,1)}, bf16[1280,3456]{1,0:T(8,128)(2,1)}, u32[]{:S(2)}, u32[]{:S(2)}) collective-permute-start(bf16[1280,3456]{1,0:T(8,128)(2,1)} %refs_0_.4), channel_id=1, source_target_pairs={{0,1},{1,0},{2,3},{3,2},{4,5},{5,4},{6,7},{7,6},{8,9},{9,8},{10,11... | collective-permute-start | bytes 26542088 | tf_op jit(solution)/shard_map/ppermute | solution.py:299
  60.6 266.8 %collective-permute-start.15 = (bf16[1280,3456]{1,0:T(8,128)(2,1)}, bf16[1280,3456]{1,0:T(8,128)(2,1)}, u32[]{:S(2)}, u32[]{:S(2)}) collective-permute-start(bf16[1280,3456]{1,0:T(8,128)(2,1)} %refs_1_.1), channel_id=1, source_target_pairs={{0,1},{1,0},{2,3},{3,2},{4,5},{5,4},{6,7},{7,6},{8,9},{9,8},{10,11... | collective-permute-start | bytes 26542088 | tf_op jit(solution)/shard_map/ppermute | solution.py:299
  61.1 68.6 %collective-permute-start.3 = (bf16[256,5120]{1,0:T(8,128)(2,1)S(1)}, bf16[256,5120]{1,0:T(8,128)(2,1)S(1)}, u32[]{:S(2)}, u32[]{:S(2)}) collective-permute-start(bf16[256,5120]{1,0:T(8,128)(2,1)S(1)} %pad_maximum_fusion), channel_id=1, source_target_pairs={{0,2},{1,3},{2,0},{3,1},{4,6},{5,7},{6,4},{7,5},{8,10},{9,11},{10,... | collective-permute-start | bytes 7864328 | tf_op jit(solution)/shard_map/ppermute | solution.py:299
  72.9 54.0 %collective-permute-start.48 = (bf16[256,2560]{1,0:T(8,128)(2,1)}, bf16[256,2560]{1,0:T(8,128)(2,1)S(1)}, u32[]{:S(2)}, u32[]{:S(2)}) collective-permute-start(bf16[256,2560]{1,0:T(8,128)(2,1)} %collective-permute-done.46.refs_1_), channel_id=1, source_target_pairs={{0,8},{4,12},{8,0},{12,4},{1,9},{5,13},{9,1},{13,5},{2,10},{6,14},... | collective-permute-start | bytes 3932168 | tf_op jit(solution)/shard_map/ppermute | solution.py:299
  98.7 56.2 %collective-permute-start.18 = (bf16[256,2560]{1,0:T(8,128)(2,1)}, bf16[256,2560]{1,0:T(8,128)(2,1)S(1)}, u32[]{:S(2)}, u32[]{:S(2)}) collective-permute-start(bf16[256,2560]{1,0:T(8,128)(2,1)} %collective-permute-done.16.refs_1_), channel_id=1, source_target_pairs={{0,8},{4,12},{8,0},{12,4},{1,9},{5,13},{9,1},{13,5},{2,10},{6,14},... | collective-permute-start | bytes 3932168 | tf_op jit(solution)/shard_map/ppermute | solution.py:299
  129.7 53.3 %collective-permute-start.50 = (bf16[256,2560]{1,0:T(8,128)(2,1)S(1)}, bf16[256,2560]{1,0:T(8,128)(2,1)S(1)}, u32[]{:S(2)}, u32[]{:S(2)}) collective-permute-start(bf16[256,2560]{1,0:T(8,128)(2,1)S(1)} %get-tuple-element.137.refs_4_), channel_id=1, source_target_pairs={{0,8},{4,12},{8,0},{12,4},{1,9},{5,13},{9,1},{13,5},{2,10},{6,14},... | collective-permute-start | bytes 3932168 | tf_op jit(solution)/shard_map/ppermute | solution.py:299
  156.7 54.4 %collective-permute-start.12 = (bf16[256,2560]{1,0:T(8,128)(2,1)S(1)}, bf16[256,2560]{1,0:T(8,128)(2,1)S(1)}, u32[]{:S(2)}, u32[]{:S(2)}) collective-permute-start(bf16[256,2560]{1,0:T(8,128)(2,1)S(1)} %get-tuple-element.143.refs_0_), channel_id=1, source_target_pairs={{0,8},{4,12},{8,0},{12,4},{1,9},{5,13},{9,1},{13,5},{2,10},{6,14},... | collective-permute-start | bytes 3932168 | tf_op jit(solution)/shard_map/ppermute | solution.py:299
  183.0 54.6 %collective-permute-start.51 = (bf16[256,2560]{1,0:T(8,128)(2,1)S(1)}, bf16[256,2560]{1,0:T(8,128)(2,1)S(1)}, u32[]{:S(2)}, u32[]{:S(2)}) collective-permute-start(bf16[256,2560]{1,0:T(8,128)(2,1)S(1)} %collective-permute-done.49.refs_5_), channel_id=1, source_target_pairs={{0,8},{4,12},{8,0},{12,4},{1,9},{5,13},{9,1},{13,5},{2,10},{6,14},... | collective-permute-start | bytes 3932168 | tf_op jit(solution)/shard_map/ppermute | solution.py:299
  187.2 109.6 %collective-permute-start.23 = (bf16[1280,1280]{1,0:T(8,128)(2,1)}, bf16[1280,1280]{1,0:T(8,128)(2,1)}, u32[]{:S(2)}, u32[]{:S(2)}) collective-permute-start(bf16[1280,1280]{1,0:T(8,128)(2,1)} %get-tuple-element.131), channel_id=1, source_target_pairs={{0,2},{1,3},{2,0},{3,1},{4,6},{5,7},{6,4},{7,5},{8,10},{9,11},{10,... | collective-permute-start | bytes 9830408 | tf_op jit(solution)/shard_map/ppermute | solution.py:299
  211.1 115.3 %collective-permute-start.25 = (bf16[1280,1280]{1,0:T(8,128)(2,1)}, bf16[1280,1280]{1,0:T(8,128)(2,1)}, u32[]{:S(2)}, u32[]{:S(2)}) collective-permute-start(bf16[1280,1280]{1,0:T(8,128)(2,1)} %get-tuple-element.129), channel_id=1, source_target_pairs={{0,2},{1,3},{2,0},{3,1},{4,6},{5,7},{6,4},{7,5},{8,10},{9,11},{10,... | collective-permute-start | bytes 9830408 | tf_op jit(solution)/shard_map/ppermute | solution.py:299
  295.7 72.8 %collective-permute-start = (bf16[256,2560]{1,0:T(8,128)(2,1)}, bf16[256,2560]{1,0:T(8,128)(2,1)S(1)}, u32[]{:S(2)}, u32[]{:S(2)}) collective-permute-start(bf16[256,2560]{1,0:T(8,128)(2,1)} %pad_maximum_fusion.2.refs_0_), channel_id=1, source_target_pairs={{0,4},{4,0},{8,12},{12,8},{1,5},{5,1},{9,13},{13,9},{2,6},{6,2},{1... | collective-permute-start | bytes 3932168 | tf_op jit(solution)/shard_map/ppermute | solution.py:299
  296.8 71.9 %collective-permute-start.2 = (bf16[256,2560]{1,0:T(8,128)(2,1)}, bf16[256,2560]{1,0:T(8,128)(2,1)S(1)}, u32[]{:S(2)}, u32[]{:S(2)}) collective-permute-start(bf16[256,2560]{1,0:T(8,128)(2,1)} %collective-permute-done.1.refs_2_), channel_id=1, source_target_pairs={{0,4},{4,0},{8,12},{12,8},{1,5},{5,1},{9,13},{13,9},{2,6},{6,2},{1... | collective-permute-start | bytes 3932168 | tf_op jit(solution)/shard_map/ppermute | solution.py:299
  326.4 43.6 %collective-permute-start.5 = (bf16[256,2560]{1,0:T(8,128)(2,1)S(1)}, bf16[256,2560]{1,0:T(8,128)(2,1)}, u32[]{:S(2)}, u32[]{:S(2)}) collective-permute-start(bf16[256,2560]{1,0:T(8,128)(2,1)S(1)} %copy-done.34), channel_id=1, source_target_pairs={{0,8},{4,12},{8,0},{12,4},{1,9},{5,13},{9,1},{13,5},{2,10},{6,14},... | collective-permute-start | bytes 3932168 | tf_op jit(solution)/shard_map/ppermute | solution.py:299
  327.4 101.9 %collective-permute-start.24 = (bf16[1280,1280]{1,0:T(8,128)(2,1)}, bf16[1280,1280]{1,0:T(8,128)(2,1)}, u32[]{:S(2)}, u32[]{:S(2)}) collective-permute-start(bf16[1280,1280]{1,0:T(8,128)(2,1)} %collective-permute-done.23.refs_8_.refs_1_), channel_id=1, source_target_pairs={{0,1},{1,0},{2,3},{3,2},{4,5},{5,4},{6,7},{7,6},{8,9},{9,8},{10,11... | collective-permute-start | bytes 9830408 | tf_op jit(solution)/shard_map/ppermute | solution.py:299
  327.4 103.2 %collective-permute-start.26 = (bf16[1280,1280]{1,0:T(8,128)(2,1)}, bf16[1280,1280]{1,0:T(8,128)(2,1)}, u32[]{:S(2)}, u32[]{:S(2)}) collective-permute-start(bf16[1280,1280]{1,0:T(8,128)(2,1)} %collective-permute-done.25.refs_10_.refs_4_), channel_id=1, source_target_pairs={{0,1},{1,0},{2,3},{3,2},{4,5},{5,4},{6,7},{7,6},{8,9},{9,8},{10,11... | collective-permute-start | bytes 9830408 | tf_op jit(solution)/shard_map/ppermute | solution.py:299
  368.6 324.9 %collective-permute-start.29 = (bf16[1280,3456]{1,0:T(8,128)(2,1)}, bf16[1280,3456]{1,0:T(8,128)(2,1)}, u32[]{:S(2)}, u32[]{:S(2)}) collective-permute-start(bf16[1280,3456]{1,0:T(8,128)(2,1)} %bitcast.5), channel_id=1, source_target_pairs={{0,1},{1,0},{2,3},{3,2},{4,5},{5,4},{6,7},{7,6},{8,9},{9,8},{10,11... | collective-permute-start | bytes 26542088 | tf_op jit(solution)/shard_map/ppermute | solution.py:299
  370.0 58.0 %collective-permute-start.6 = (bf16[256,2560]{1,0:T(8,128)(2,1)}, bf16[256,2560]{1,0:T(8,128)(2,1)}, u32[]{:S(2)}, u32[]{:S(2)}) collective-permute-start(bf16[256,2560]{1,0:T(8,128)(2,1)} %collective-permute-done.5.refs_6_), channel_id=1, source_target_pairs={{0,4},{4,0},{8,12},{12,8},{1,5},{5,1},{9,13},{13,9},{2,6},{6,2},{1... | collective-permute-start | bytes 3932168 | tf_op jit(solution)/shard_map/ppermute | solution.py:299
  400.5 70.7 %collective-permute-start.9 = (bf16[1280,896]{1,0:T(8,128)(2,1)}, bf16[1280,896]{1,0:T(8,128)(2,1)}, u32[]{:S(2)}, u32[]{:S(2)}) collective-permute-start(bf16[1280,896]{1,0:T(8,128)(2,1)} %slice.189), channel_id=1, source_target_pairs={{0,2},{1,3},{2,0},{3,1},{4,6},{5,7},{6,4},{7,5},{8,10},{9,11},{10,... | collective-permute-start | bytes 6881288 | tf_op jit(solution)/shard_map/ppermute | solution.py:299
  428.0 74.6 %collective-permute-start.7 = (bf16[1280,896]{1,0:T(8,128)(2,1)}, bf16[1280,896]{1,0:T(8,128)(2,1)}, u32[]{:S(2)}, u32[]{:S(2)}) collective-permute-start(bf16[1280,896]{1,0:T(8,128)(2,1)} %slice.188), channel_id=1, source_target_pairs={{0,2},{1,3},{2,0},{3,1},{4,6},{5,7},{6,4},{7,5},{8,10},{9,11},{10,... | collective-permute-start | bytes 6881288 | tf_op jit(solution)/shard_map/ppermute | solution.py:299
  430.6 121.2 %collective-permute-start.54 = (bf16[1280,896]{1,0:T(8,128)(2,1)}, bf16[1280,896]{1,0:T(8,128)(2,1)}, u32[]{:S(2)}, u32[]{:S(2)}) collective-permute-start(bf16[1280,896]{1,0:T(8,128)(2,1)} %slice.254), channel_id=1, source_target_pairs={{0,2},{1,3},{2,0},{3,1},{4,6},{5,7},{6,4},{7,5},{8,10},{9,11},{10,... | collective-permute-start | bytes 6881288 | tf_op jit(solution)/shard_map/ppermute | solution.py:299
  469.6 50.2 %collective-permute-start.37 = (bf16[256,2560]{1,0:T(8,128)(2,1)S(1)}, bf16[256,2560]{1,0:T(8,128)(2,1)S(1)}, u32[]{:S(2)}, u32[]{:S(2)}) collective-permute-start(bf16[256,2560]{1,0:T(8,128)(2,1)S(1)} %copy-done.21), channel_id=1, source_target_pairs={{0,4},{4,0},{8,12},{12,8},{1,5},{5,1},{9,13},{13,9},{2,6},{6,2},{1... | collective-permute-start | bytes 3932168 | tf_op jit(solution)/shard_map/ppermute | solution.py:299
  471.2 99.2 %collective-permute-start.10 = (bf16[1280,896]{1,0:T(8,128)(2,1)}, bf16[1280,896]{1,0:T(8,128)(2,1)}, u32[]{:S(2)}, u32[]{:S(2)}) collective-permute-start(bf16[1280,896]{1,0:T(8,128)(2,1)} %collective-permute-done.9.refs_10_.refs_5_), channel_id=1, source_target_pairs={{0,1},{1,0},{2,3},{3,2},{4,5},{5,4},{6,7},{7,6},{8,9},{9,8},{10,11... | collective-permute-start | bytes 6881288 | tf_op jit(solution)/shard_map/ppermute | solution.py:299
  502.6 69.3 %collective-permute-start.8 = (bf16[1280,896]{1,0:T(8,128)(2,1)}, bf16[1280,896]{1,0:T(8,128)(2,1)}, u32[]{:S(2)}, u32[]{:S(2)}) collective-permute-start(bf16[1280,896]{1,0:T(8,128)(2,1)} %collective-permute-done.7.refs_8_.refs_2_), channel_id=1, source_target_pairs={{0,1},{1,0},{2,3},{3,2},{4,5},{5,4},{6,7},{7,6},{8,9},{9,8},{10,11... | collective-permute-start | bytes 6881288 | tf_op jit(solution)/shard_map/ppermute | solution.py:299
  519.8 194.7 %collective-permute-start.19 = (bf16[1280,1280]{1,0:T(8,128)(2,1)}, bf16[1280,1280]{1,0:T(8,128)(2,1)}, u32[]{:S(2)}, u32[]{:S(2)}) collective-permute-start(bf16[1280,1280]{1,0:T(8,128)(2,1)} %get-tuple-element.132), channel_id=1, source_target_pairs={{0,2},{1,3},{2,0},{3,1},{4,6},{5,7},{6,4},{7,5},{8,10},{9,11},{10,... | collective-permute-start | bytes 9830408 | tf_op jit(solution)/shard_map/ppermute | solution.py:299
  551.8 140.4 %collective-permute-start.52 = (bf16[1280,1280]{1,0:T(8,128)(2,1)}, bf16[1280,1280]{1,0:T(8,128)(2,1)}, u32[]{:S(2)}, u32[]{:S(2)}) collective-permute-start(bf16[1280,1280]{1,0:T(8,128)(2,1)} %get-tuple-element.127), channel_id=1, source_target_pairs={{0,2},{1,3},{2,0},{3,1},{4,6},{5,7},{6,4},{7,5},{8,10},{9,11},{10,... | collective-permute-start | bytes 9830408 | tf_op jit(solution)/shard_map/ppermute | solution.py:299
  571.9 144.2 %collective-permute-start.42 = (bf16[256,2560]{1,0:T(8,128)(2,1)S(1)}, bf16[256,2560]{1,0:T(8,128)(2,1)}, u32[]{:S(2)}, u32[]{:S(2)}) collective-permute-start(bf16[256,2560]{1,0:T(8,128)(2,1)S(1)} %copy-done.19), channel_id=1, source_target_pairs={{0,8},{4,12},{8,0},{12,4},{1,9},{5,13},{9,1},{13,5},{2,10},{6,14},... | collective-permute-start | bytes 3932168 | tf_op jit(solution)/shard_map/ppermute | solution.py:299
  604.9 157.5 %collective-permute-start.21 = (bf16[1280,1280]{1,0:T(8,128)(2,1)}, bf16[1280,1280]{1,0:T(8,128)(2,1)}, u32[]{:S(2)}, u32[]{:S(2)}) collective-permute-start(bf16[1280,1280]{1,0:T(8,128)(2,1)} %get-tuple-element.130), channel_id=1, source_target_pairs={{0,2},{1,3},{2,0},{3,1},{4,6},{5,7},{6,4},{7,5},{8,10},{9,11},{10,... | collective-permute-start | bytes 9830408 | tf_op jit(solution)/shard_map/ppermute | solution.py:299
  692.2 138.5 %collective-permute-start.44 = (bf16[1280,1280]{1,0:T(8,128)(2,1)}, bf16[1280,1280]{1,0:T(8,128)(2,1)}, u32[]{:S(2)}, u32[]{:S(2)}) collective-permute-start(bf16[1280,1280]{1,0:T(8,128)(2,1)} %get-tuple-element.128), channel_id=1, source_target_pairs={{0,2},{1,3},{2,0},{3,1},{4,6},{5,7},{6,4},{7,5},{8,10},{9,11},{10,... | collective-permute-start | bytes 9830408 | tf_op jit(solution)/shard_map/ppermute | solution.py:299
  693.5 137.8 %collective-permute-start.53 = (bf16[1280,1280]{1,0:T(8,128)(2,1)}, bf16[1280,1280]{1,0:T(8,128)(2,1)}, u32[]{:S(2)}, u32[]{:S(2)}) collective-permute-start(bf16[1280,1280]{1,0:T(8,128)(2,1)} %collective-permute-done.52.refs_8_), channel_id=1, source_target_pairs={{0,1},{1,0},{2,3},{3,2},{4,5},{5,4},{6,7},{7,6},{8,9},{9,8},{10,11... | collective-permute-start | bytes 9830408 | tf_op jit(solution)/shard_map/ppermute | solution.py:299
  714.6 116.2 %collective-permute-start.41 = (bf16[256,2560]{1,0:T(8,128)(2,1)S(1)}, bf16[256,2560]{1,0:T(8,128)(2,1)}, u32[]{:S(2)}, u32[]{:S(2)}) collective-permute-start(bf16[256,2560]{1,0:T(8,128)(2,1)S(1)} %copy-done.19), channel_id=1, source_target_pairs={{0,4},{4,0},{8,12},{12,8},{1,5},{5,1},{9,13},{13,9},{2,6},{6,2},{1... | collective-permute-start | bytes 3932168 | tf_op jit(solution)/shard_map/ppermute | solution.py:299
  716.1 115.2 %collective-permute-start.43 = (bf16[256,2560]{1,0:T(8,128)(2,1)}, bf16[256,2560]{1,0:T(8,128)(2,1)}, u32[]{:S(2)}, u32[]{:S(2)}) collective-permute-start(bf16[256,2560]{1,0:T(8,128)(2,1)} %collective-permute-done.42.refs_6_), channel_id=1, source_target_pairs={{0,4},{4,0},{8,12},{12,8},{1,5},{5,1},{9,13},{13,9},{2,6},{6,2},{1... | collective-permute-start | bytes 3932168 | tf_op jit(solution)/shard_map/ppermute | solution.py:299
  762.5 120.0 %collective-permute-start.55 = (bf16[1280,896]{1,0:T(8,128)(2,1)}, bf16[1280,896]{1,0:T(8,128)(2,1)S(1)}, u32[]{:S(2)}, u32[]{:S(2)}) collective-permute-start(bf16[1280,896]{1,0:T(8,128)(2,1)} %collective-permute-done.54.refs_8_), channel_id=1, source_target_pairs={{0,1},{1,0},{2,3},{3,2},{4,5},{5,4},{6,7},{7,6},{8,9},{9,8},{10,11... | collective-permute-start | bytes 6881288 | tf_op jit(solution)/shard_map/ppermute | solution.py:299
  830.8 77.7 %collective-permute-start.20 = (bf16[1280,1280]{1,0:T(8,128)(2,1)}, bf16[1280,1280]{1,0:T(8,128)(2,1)}, u32[]{:S(2)}, u32[]{:S(2)}) collective-permute-start(bf16[1280,1280]{1,0:T(8,128)(2,1)} %collective-permute-done.19.refs_8_.refs_0_), channel_id=1, source_target_pairs={{0,1},{1,0},{2,3},{3,2},{4,5},{5,4},{6,7},{7,6},{8,9},{9,8},{10,11... | collective-permute-start | bytes 9830408 | tf_op jit(solution)/shard_map/ppermute | solution.py:299
  830.8 77.7 %collective-permute-start.22 = (bf16[1280,1280]{1,0:T(8,128)(2,1)}, bf16[1280,1280]{1,0:T(8,128)(2,1)}, u32[]{:S(2)}, u32[]{:S(2)}) collective-permute-start(bf16[1280,1280]{1,0:T(8,128)(2,1)} %collective-permute-done.21.refs_10_.refs_3_), channel_id=1, source_target_pairs={{0,1},{1,0},{2,3},{3,2},{4,5},{5,4},{6,7},{7,6},{8,9},{9,8},{10,11... | collective-permute-start | bytes 9830408 | tf_op jit(solution)/shard_map/ppermute | solution.py:299
  831.3 115.2 %collective-permute-start.45 = (bf16[1280,1280]{1,0:T(8,128)(2,1)}, bf16[1280,1280]{1,0:T(8,128)(2,1)}, u32[]{:S(2)}, u32[]{:S(2)}) collective-permute-start(bf16[1280,1280]{1,0:T(8,128)(2,1)} %collective-permute-done.44.refs_8_), channel_id=1, source_target_pairs={{0,1},{1,0},{2,3},{3,2},{4,5},{5,4},{6,7},{7,6},{8,9},{9,8},{10,11... | collective-permute-start | bytes 9830408 | tf_op jit(solution)/shard_map/ppermute | solution.py:299
  831.3 292.5 %collective-permute-start.71 = (bf16[2048,1280]{1,0:T(8,128)(2,1)}, bf16[2048,1280]{1,0:T(8,128)(2,1)}, u32[]{:S(2)}, u32[]{:S(2)}) collective-permute-start(bf16[2048,1280]{1,0:T(8,128)(2,1)} %get-tuple-element.149), channel_id=1, source_target_pairs={{0,1},{1,0},{2,3},{3,2},{4,5},{5,4},{6,7},{7,6},{8,9},{9,8},{10,11... | collective-permute-start | bytes 15728648 | tf_op jit(solution)/shard_map/ppermute | solution.py:299
  882.5 242.1 %collective-permute-start.64 = (bf16[1280,2048]{1,0:T(8,128)(2,1)}, bf16[1280,2048]{1,0:T(8,128)(2,1)}, u32[]{:S(2)}, u32[]{:S(2)}) collective-permute-start(bf16[1280,2048]{1,0:T(8,128)(2,1)} %bitcast.11), channel_id=1, source_target_pairs={{0,1},{1,0},{2,3},{3,2},{4,5},{5,4},{6,7},{7,6},{8,9},{9,8},{10,11... | collective-permute-start | bytes 15728648 | tf_op jit(solution)/shard_map/ppermute | solution.py:299
  1004.0 156.8 %collective-permute-start.62 = (f32[1280,512]{1,0:T(8,128)}, f32[1280,512]{1,0:T(8,128)}, u32[]{:S(2)}, u32[]{:S(2)}) collective-permute-start(f32[1280,512]{1,0:T(8,128)} %get-tuple-element.112), channel_id=1, source_target_pairs={{0,8},{4,12},{8,0},{12,4},{1,9},{5,13},{9,1},{13,5},{2,10},{6,14},... | collective-permute-start | bytes 7864328 | tf_op jit(solution)/shard_map/ppermute | solution.py:299
  1032.7 129.6 %collective-permute-start.60 = (f32[1280,512]{1,0:T(8,128)}, f32[1280,512]{1,0:T(8,128)}, u32[]{:S(2)}, u32[]{:S(2)}) collective-permute-start(f32[1280,512]{1,0:T(8,128)} %get-tuple-element.110), channel_id=1, source_target_pairs={{0,4},{4,0},{8,12},{12,8},{1,5},{5,1},{9,13},{13,9},{2,6},{6,2},{1... | collective-permute-start | bytes 7864328 | tf_op jit(solution)/shard_map/ppermute | solution.py:299
  1061.1 102.1 %collective-permute-start.58 = (f32[1280,512]{1,0:T(8,128)}, f32[1280,512]{1,0:T(8,128)}, u32[]{:S(2)}, u32[]{:S(2)}) collective-permute-start(f32[1280,512]{1,0:T(8,128)} %get-tuple-element.108), channel_id=1, source_target_pairs={{0,8},{4,12},{8,0},{12,4},{1,9},{5,13},{9,1},{13,5},{2,10},{6,14},... | collective-permute-start | bytes 7864328 | tf_op jit(solution)/shard_map/ppermute | solution.py:299
  1123.8 60.1 %collective-permute-start.56 = (f32[1280,512]{1,0:T(8,128)}, f32[1280,512]{1,0:T(8,128)}, u32[]{:S(2)}, u32[]{:S(2)}) collective-permute-start(f32[1280,512]{1,0:T(8,128)} %get-tuple-element.106), channel_id=1, source_target_pairs={{0,4},{4,0},{8,12},{12,8},{1,5},{5,1},{9,13},{13,9},{2,6},{6,2},{1... | collective-permute-start | bytes 7864328 | tf_op jit(solution)/shard_map/ppermute | solution.py:299
  1124.6 60.1 %collective-permute-start.34 = (f32[1280,512]{1,0:T(8,128)}, f32[1280,512]{1,0:T(8,128)}, u32[]{:S(2)}, u32[]{:S(2)}) collective-permute-start(f32[1280,512]{1,0:T(8,128)} %get-tuple-element.92), channel_id=1, source_target_pairs={{0,8},{4,12},{8,0},{12,4},{1,9},{5,13},{9,1},{13,5},{2,10},{6,14},... | collective-permute-start | bytes 7864328 | tf_op jit(solution)/shard_map/ppermute | solution.py:299
  1160.8 79.2 %collective-permute-start.32 = (f32[1280,512]{1,0:T(8,128)}, f32[1280,512]{1,0:T(8,128)S(1)}, u32[]{:S(2)}, u32[]{:S(2)}) collective-permute-start(f32[1280,512]{1,0:T(8,128)} %get-tuple-element.90), channel_id=1, source_target_pairs={{0,4},{4,0},{8,12},{12,8},{1,5},{5,1},{9,13},{13,9},{2,6},{6,2},{1... | collective-permute-start | bytes 7864328 | tf_op jit(solution)/shard_map/ppermute | solution.py:299
  1162.4 78.9 %collective-permute-start.30 = (f32[1280,512]{1,0:T(8,128)}, f32[1280,512]{1,0:T(8,128)S(1)}, u32[]{:S(2)}, u32[]{:S(2)}) collective-permute-start(f32[1280,512]{1,0:T(8,128)} %get-tuple-element.88), channel_id=1, source_target_pairs={{0,8},{4,12},{8,0},{12,4},{1,9},{5,13},{9,1},{13,5},{2,10},{6,14},... | collective-permute-start | bytes 7864328 | tf_op jit(solution)/shard_map/ppermute | solution.py:299
  1163.1 133.0 %collective-permute-start.27 = (f32[1280,512]{1,0:T(8,128)}, f32[1280,512]{1,0:T(8,128)S(1)}, u32[]{:S(2)}, u32[]{:S(2)}) collective-permute-start(f32[1280,512]{1,0:T(8,128)} %get-tuple-element.82), channel_id=1, source_target_pairs={{0,4},{4,0},{8,12},{12,8},{1,5},{5,1},{9,13},{13,9},{2,6},{6,2},{1... | collective-permute-start | bytes 7864328 | tf_op jit(solution)/shard_map/ppermute | solution.py:299
  1183.9 233.4 %collective-permute-start.74 = (bf16[1280,2048]{1,0:T(8,128)(2,1)}, bf16[1280,2048]{1,0:T(8,128)(2,1)}, u32[]{:S(2)}, u32[]{:S(2)}) collective-permute-start(bf16[1280,2048]{1,0:T(8,128)(2,1)} %get-tuple-element.71.refs_1_.refs_2_), channel_id=1, source_target_pairs={{0,1},{1,0},{2,3},{3,2},{4,5},{5,4},{6,7},{7,6},{8,9},{9,8},{10,11... | collective-permute-start | bytes 15728648 | tf_op jit(solution)/shard_map/ppermute | solution.py:299
  1184.7 139.6 %collective-permute-start.63 = (f32[1280,256]{1,0:T(8,128)S(1)}, f32[1280,256]{1,0:T(8,128)S(1)}, u32[]{:S(2)}, u32[]{:S(2)}) collective-permute-start(f32[1280,256]{1,0:T(8,128)S(1)} %slice_add_fusion), channel_id=1, source_target_pairs={{0,4},{4,0},{8,12},{12,8},{1,5},{5,1},{9,13},{13,9},{2,6},{6,2},{1... | collective-permute-start | bytes 3932168 | tf_op jit(solution)/shard_map/ppermute | solution.py:299
  1240.0 88.1 %collective-permute-start.61 = (f32[1280,256]{1,0:T(8,128)S(1)}, f32[1280,256]{1,0:T(8,128)S(1)}, u32[]{:S(2)}, u32[]{:S(2)}) collective-permute-start(f32[1280,256]{1,0:T(8,128)S(1)} %slice_add_fusion.1), channel_id=1, source_target_pairs={{0,8},{4,12},{8,0},{12,4},{1,9},{5,13},{9,1},{13,5},{2,10},{6,14},... | collective-permute-start | bytes 3932168 | tf_op jit(solution)/shard_map/ppermute | solution.py:299
  1241.3 111.1 %collective-permute-start.59 = (f32[1280,256]{1,0:T(8,128)S(1)}, f32[1280,256]{1,0:T(8,128)S(1)}, u32[]{:S(2)}, u32[]{:S(2)}) collective-permute-start(f32[1280,256]{1,0:T(8,128)S(1)} %slice_add_fusion.2), channel_id=1, source_target_pairs={{0,4},{4,0},{8,12},{12,8},{1,5},{5,1},{9,13},{13,9},{2,6},{6,2},{1... | collective-permute-start | bytes 3932168 | tf_op jit(solution)/shard_map/ppermute | solution.py:299
  1296.2 82.5 %collective-permute-start.35 = (f32[1280,256]{1,0:T(8,128)S(1)}, f32[1280,256]{1,0:T(8,128)S(1)}, u32[]{:S(2)}, u32[]{:S(2)}) collective-permute-start(f32[1280,256]{1,0:T(8,128)S(1)} %slice_add_fusion.4), channel_id=1, source_target_pairs={{0,4},{4,0},{8,12},{12,8},{1,5},{5,1},{9,13},{13,9},{2,6},{6,2},{1... | collective-permute-start | bytes 3932168 | tf_op jit(solution)/shard_map/ppermute | solution.py:299
  1324.3 56.5 %collective-permute-start.33 = (f32[1280,256]{1,0:T(8,128)S(1)}, f32[1280,256]{1,0:T(8,128)S(1)}, u32[]{:S(2)}, u32[]{:S(2)}) collective-permute-start(f32[1280,256]{1,0:T(8,128)S(1)} %slice_add_fusion.5), channel_id=1, source_target_pairs={{0,8},{4,12},{8,0},{12,4},{1,9},{5,13},{9,1},{13,5},{2,10},{6,14},... | collective-permute-start | bytes 3932168 | tf_op jit(solution)/shard_map/ppermute | solution.py:299
  1328.1 60.3 %collective-permute-start.57 = (f32[1280,256]{1,0:T(8,128)}, f32[1280,256]{1,0:T(8,128)}, u32[]{:S(2)}, u32[]{:S(2)}) collective-permute-start(f32[1280,256]{1,0:T(8,128)} %slice_add_fusion.3), channel_id=1, source_target_pairs={{0,8},{4,12},{8,0},{12,4},{1,9},{5,13},{9,1},{13,5},{2,10},{6,14},... | collective-permute-start | bytes 3932168 | tf_op jit(solution)/shard_map/ppermute | solution.py:299
  1352.4 109.7 %collective-permute-start.73 = (bf16[1280,2048]{1,0:T(8,128)(2,1)}, bf16[1280,2048]{1,0:T(8,128)(2,1)}, u32[]{:S(2)}, u32[]{:S(2)}) collective-permute-start(bf16[1280,2048]{1,0:T(8,128)(2,1)} %get-tuple-element.76.refs_2_), channel_id=1, source_target_pairs={{0,1},{1,0},{2,3},{3,2},{4,5},{5,4},{6,7},{7,6},{8,9},{9,8},{10,11... | collective-permute-start | bytes 15728648 | tf_op jit(solution)/shard_map/ppermute | solution.py:299
  1408.0 54.0 %collective-permute-start.72 = (bf16[896,2048]{1,0:T(8,128)(2,1)}, bf16[896,2048]{1,0:T(8,128)(2,1)}, u32[]{:S(2)}, u32[]{:S(2)}) collective-permute-start(bf16[896,2048]{1,0:T(8,128)(2,1)} %get-tuple-element.66.refs_1_.refs_2_), channel_id=1, source_target_pairs={{0,1},{1,0},{2,3},{3,2},{4,5},{5,4},{6,7},{7,6},{8,9},{9,8},{10,11... | collective-permute-start | bytes 11010056 | tf_op jit(solution)/shard_map/ppermute | solution.py:299
  1410.9 89.4 %collective-permute-start.69 = (bf16[2048,1280]{1,0:T(8,128)(2,1)}, bf16[2048,1280]{1,0:T(8,128)(2,1)}, u32[]{:S(2)}, u32[]{:S(2)}) collective-permute-start(bf16[2048,1280]{1,0:T(8,128)(2,1)} %get-tuple-element.117.refs_4_), channel_id=1, source_target_pairs={{0,1},{1,0},{2,3},{3,2},{4,5},{5,4},{6,7},{7,6},{8,9},{9,8},{10,11... | collective-permute-start | bytes 15728648 | tf_op jit(solution)/shard_map/ppermute | solution.py:299
  1417.3 83.0 %collective-permute-start.68 = (bf16[2048,1280]{1,0:T(8,128)(2,1)}, bf16[2048,1280]{1,0:T(8,128)(2,1)}, u32[]{:S(2)}, u32[]{:S(2)}) collective-permute-start(bf16[2048,1280]{1,0:T(8,128)(2,1)} %get-tuple-element.116.refs_2_), channel_id=1, source_target_pairs={{0,1},{1,0},{2,3},{3,2},{4,5},{5,4},{6,7},{7,6},{8,9},{9,8},{10,11... | collective-permute-start | bytes 15728648 | tf_op jit(solution)/shard_map/ppermute | solution.py:299
  1417.3 65.9 %collective-permute-start.70 = (bf16[2048,896]{1,0:T(8,128)(2,1)}, bf16[2048,896]{1,0:T(8,128)(2,1)}, u32[]{:S(2)}, u32[]{:S(2)}) collective-permute-start(bf16[2048,896]{1,0:T(8,128)(2,1)} %get-tuple-element.118.refs_6_), channel_id=1, source_target_pairs={{0,1},{1,0},{2,3},{3,2},{4,5},{5,4},{6,7},{7,6},{8,9},{9,8},{10,11... | collective-permute-start | bytes 11010056 | tf_op jit(solution)/shard_map/ppermute | solution.py:299
  1462.0 87.2 %collective-permute-start.66 = (bf16[2048,1280]{1,0:T(8,128)(2,1)}, bf16[2048,1280]{1,0:T(8,128)(2,1)}, u32[]{:S(2)}, u32[]{:S(2)}) collective-permute-start(bf16[2048,1280]{1,0:T(8,128)(2,1)} %get-tuple-element.114.refs_4_), channel_id=1, source_target_pairs={{0,1},{1,0},{2,3},{3,2},{4,5},{5,4},{6,7},{7,6},{8,9},{9,8},{10,11... | collective-permute-start | bytes 15728648 | tf_op jit(solution)/shard_map/ppermute | solution.py:299
  1462.0 87.1 %collective-permute-start.65 = (bf16[2048,1280]{1,0:T(8,128)(2,1)}, bf16[2048,1280]{1,0:T(8,128)(2,1)}, u32[]{:S(2)}, u32[]{:S(2)}) collective-permute-start(bf16[2048,1280]{1,0:T(8,128)(2,1)} %get-tuple-element.113.refs_2_), channel_id=1, source_target_pairs={{0,1},{1,0},{2,3},{3,2},{4,5},{5,4},{6,7},{7,6},{8,9},{9,8},{10,11... | collective-permute-start | bytes 15728648 | tf_op jit(solution)/shard_map/ppermute | solution.py:299
  1483.2 66.0 %collective-permute-start.67 = (bf16[2048,896]{1,0:T(8,128)(2,1)S(1)}, bf16[2048,896]{1,0:T(8,128)(2,1)}, u32[]{:S(2)}, u32[]{:S(2)}) collective-permute-start(bf16[2048,896]{1,0:T(8,128)(2,1)S(1)} %copy-done.45), channel_id=1, source_target_pairs={{0,1},{1,0},{2,3},{3,2},{4,5},{5,4},{6,7},{7,6},{8,9},{9,8},{10,11... | collective-permute-start | bytes 11010056 | tf_op jit(solution)/shard_map/ppermute | solution.py:299
  (59 other events, 2089.9 us)
